TPU v7x, 32 devices: a whole 2x2x4 slice. The times are simulated.
32 devices in a mesh: replica: 8 (over z, y), model: 4 (over x, core).
Axes of the slice: x: 2, y: 2, z: 4, core: 2. Of those that a mesh axis runs over, the one named last changes fastest.
Arguments:
- slope_up: float32 [8, 1024, 4096], P('replica', None, 'model'), may hold values from -4 to 4
- slope_down: float32 [8, 4096, 1024], P('replica', 'model'), may hold values from -4 to 4
- slope_query: float32 [8, 1024, 1024], P('replica', None, 'model'), may hold values from -4 to 4
- slope_key: float32 [8, 1024, 1024], P('replica', None, 'model'), may hold values from -4 to 4
- slope_value: float32 [8, 1024, 1024], P('replica', None, 'model'), may hold values from -4 to 4
- slope_mixed: float32 [8, 1024, 1024], P('replica', 'model'), may hold values from -4 to 4
- slope_norm: float32 [8, 1024], P('replica'), may hold values from -8 to 8
- slope_bias: float32 [8, 1024], P('replica'), may hold values from -8 to 8
- param_up: float32 [1024, 4096], P('replica', 'model'), may hold values from -0.25 to 0.25
- param_down: float32 [4096, 1024], P('model', 'replica'), may hold values from -0.125 to 0.125
- param_query: float32 [1024, 1024], P('replica', 'model'), may hold values from -0.25 to 0.25
- param_key: float32 [1024, 1024], P('replica', 'model'), may hold values from -0.25 to 0.25
- param_value: float32 [1024, 1024], P('replica', 'model'), may hold values from -0.25 to 0.25
- param_mixed: float32 [1024, 1024], P('model', 'replica'), may hold values from -0.25 to 0.25
- param_norm: float32 [1024], P('replica'), may hold values from 0.25 to 1.75
- param_bias: float32 [1024], P('replica'), may hold values from -3 to 3
- state_up: float32 [1024, 4096], P('replica', 'model'), may hold values from 0.0001953125 to 0.001953125
- state_down: float32 [4096, 1024], P('model', 'replica'), may hold values from 4.8828126e-05 to 0.00048828125
- state_query: float32 [1024, 1024], P('replica', 'model'), may hold values from 0.0001953125 to 0.001953125
- state_key: float32 [1024, 1024], P('replica', 'model'), may hold values from 0.0001953125 to 0.001953125
- state_value: float32 [1024, 1024], P('replica', 'model'), may hold values from 0.0001953125 to 0.001953125
- state_mixed: float32 [1024, 1024], P('model', 'replica'), may hold values from 0.0001953125 to 0.001953125
- state_norm: float32 [1024], P('replica'), may hold values from 0.05 to 0.8
- state_bias: float32 [1024], P('replica'), may hold values from 0.05 to 0.8
Outputs:
- half_up: bfloat16 [1024, 4096], P(None, 'model')
- half_down: bfloat16 [4096, 1024], P('model')
- half_query: bfloat16 [1024, 1024], P(None, 'model')
- half_key: bfloat16 [1024, 1024], P(None, 'model')
- half_value: bfloat16 [1024, 1024], P(None, 'model')
- half_mixed: bfloat16 [1024, 1024], P('model')
- half_norm: bfloat16 [1024], replicated
- half_bias: bfloat16 [1024], replicated
- next_up: float32 [1024, 4096], P('replica', 'model')
- next_down: float32 [4096, 1024], P('model', 'replica')
- next_query: float32 [1024, 1024], P('replica', 'model')
- next_key: float32 [1024, 1024], P('replica', 'model')
- next_value: float32 [1024, 1024], P('replica', 'model')
- next_mixed: float32 [1024, 1024], P('model', 'replica')
- next_norm: float32 [1024], P('replica')
- next_bias: float32 [1024], P('replica')
- state_new_up: float32 [1024, 4096], P('replica', 'model')
- state_new_down: float32 [4096, 1024], P('model', 'replica')
- state_new_query: float32 [1024, 1024], P('replica', 'model')
- state_new_key: float32 [1024, 1024], P('replica', 'model')
- state_new_value: float32 [1024, 1024], P('replica', 'model')
- state_new_mixed: float32 [1024, 1024], P('model', 'replica')
- state_new_norm: float32 [1024], P('replica')
- state_new_bias: float32 [1024], P('replica')
All inputs are finite; a program needn't handle non-finite values.
Results may differ from a plain program's by a relative error of at most 0.001.
Values may be sent and summed in bfloat16 or wider, within the bound.
A program may use at most 64 MiB of HBM per device.

v0:
```python
import functools

import jax
import jax.numpy as jnp
from jax import lax
from jax.experimental import pallas as pl
from jax.experimental.pallas import tpu as pltpu
from jax.sharding import PartitionSpec as P

learn_rate = 0.025
hold_rate = 0.7
root = 9
MESH = pl.DeviceIdType.MESH


class Group:
    def __init__(self, members, rows, near_first):
        self.members = members
        self.rows = rows
        self.near_first = near_first


UP, DOWN, MIXED, QKV = range(4)
GROUPS = (
    Group((0,), True, False),
    Group((1,), False, False),
    Group((5,), False, False),
    Group((2, 3, 4), True, True),
)
ORDER = ((1, 1), (0, 1), (1, 0), (0, 0))


def place_of(r, k2, k1, ky):
    bit = lambda v, k: v if k == 0 else 1 - v
    return (bit(r // 4, k2) * 2 + bit((r // 2) % 2, k1)) * 2 + bit(r % 2, ky)


def slab_of(shapes, r, g, b, ref):
    at = place_of(r, b // 4, (b // 2) % 2, b % 2)
    h, w = shapes[g]
    if GROUPS[g].rows:
        return ref.at[pl.ds(pl.multiple_of(at * h, h), h), :]
    return ref.at[:, pl.ds(pl.multiple_of(at * w, w), w)]


def lanes_of(shapes, g, ref, i):
    n = len(GROUPS[g].members)
    w = shapes[g][1] // n
    return ref if n == 1 else ref.at[:, i * w : (i + 1) * w]


def finish(shapes, *refs):
    n = len(GROUPS)
    full, own, st = refs[0:n], refs[n : 2 * n], refs[2 * n : 3 * n]
    vectors = refs[3 * n : 3 * n + 6]
    halves, nexts, news = (refs[3 * n + 6 + 8 * k : 3 * n + 14 + 8 * k] for k in range(3))
    sem, vec_sem = refs[3 * n + 30 :]
    r = lax.axis_index("replica")
    for g, group in enumerate(GROUPS):
        for i, a in enumerate(group.members):
            for b in range(8):
                src = lanes_of(shapes, g, full[g].at[b], i)
                pltpu.make_async_copy(src, slab_of(shapes, r, g, b, halves[a]), sem.at[0, g]).start()
            pltpu.make_async_copy(lanes_of(shapes, g, own[g], i), nexts[a], sem.at[1, g]).start()
            pltpu.make_async_copy(lanes_of(shapes, g, st[g], i), news[a], sem.at[2, g]).start()
    copies = []
    for i, dst in enumerate((*halves[6:], *nexts[6:], *news[6:])):
        copies.append(pltpu.make_async_copy(vectors[i], dst, vec_sem.at[i]))
        copies[-1].start()
    for g in range(n):
        for k, ref in enumerate((full[g], own[g], st[g])):
            pltpu.make_async_copy(ref, ref, sem.at[k, g]).wait()
    for c in copies:
        c.wait()


def kernel(replicas, models, limit, shapes, *refs):
    slopes, slope_norm, slope_bias = refs[0:6], refs[6], refs[7]
    params, param_norm, param_bias = refs[8:14], refs[14], refs[15]
    states, state_norm, state_bias = refs[16:22], refs[22], refs[23]
    groups = range(len(GROUPS))
    n = len(GROUPS)
    full, own, st = refs[24 : 24 + n], refs[24 + n : 24 + 2 * n], refs[24 + 2 * n : 24 + 3 * n]
    half_norm, half_bias, next_norm, next_bias, new_norm, new_bias = refs[24 + 3 * n : 30 + 3 * n]
    scratch = list(refs[30 + 3 * n :])
    take = lambda: [scratch.pop(0) for _ in groups]
    xin, enc1, rec1, enc2, rec2, enc3, rec3, sq, sqr = (take() for _ in range(9))
    vs, vown, vrec, vnext, vag, vh_norm, vh_bias = (scratch.pop(0) for _ in range(7))
    rs_s, rs_r, ag_s, ag_r, n_s, n_r, v_s, v_r, w_s, w_r = (scratch.pop(0) for _ in range(10))
    load_sem, own_sem, st_sem, vown_sem = scratch

    r = lax.axis_index("replica")
    m = lax.axis_index("model")
    place = functools.partial(place_of, r)
    y_peer, near_peer, far_peer = place(0, 0, 1), place(0, 1, 0), place(1, 0, 0)

    scale = 2.0**13 / (limit * replicas)
    rate = replicas ** (-0.5)

    def encode(x):
        t = x * scale
        t2 = t * t
        t4 = t2 * t2
        return (t4 * t4 * t).astype(jnp.bfloat16)

    def decode(c):
        f = c.astype(jnp.float32)
        a = jnp.exp(jnp.log(jnp.abs(f)) * (1.0 / root)) * (1.0 / scale)
        return jnp.where(f < 0, -a, a)

    def block(g, kf, ks, kt):
        return kt * 4 + (kf * 2 + ks if GROUPS[g].near_first else ks * 2 + kf)

    lanes = functools.partial(lanes_of, shapes)
    slab = lambda g, b, ref, i: slab_of(shapes, r, g, b, ref)

    def loop(g, body):
        h, w = shapes[g]
        step = min(h, max(16, 16 * 1024 // w // 16 * 16))
        while h % step:
            step -= 16
        lax.fori_loop(0, h // step, lambda i, c: (body(pl.ds(pl.multiple_of(i * step, step), step)), c)[1], 0)

    def remote(src, dst, s, d, peer, axis="replica"):
        return pltpu.make_async_remote_copy(
            src_ref=src, dst_ref=dst, send_sem=s, recv_sem=d, device_id={axis: peer}, device_id_type=MESH
        )

    barrier = pltpu.get_barrier_semaphore()
    for j in range(1, replicas):
        pl.semaphore_signal(barrier, inc=1, device_id={"replica": lax.rem(r + j, replicas)}, device_id_type=MESH)
    for j in range(1, models):
        pl.semaphore_signal(barrier, inc=1, device_id={"model": lax.rem(m + j, models)}, device_id_type=MESH)

    def load(g, b):
        for i, a in enumerate(GROUPS[g].members):
            pltpu.make_async_copy(
                slab(g, b, slopes[a].at[0], i), lanes(g, xin[g].at[b], i), load_sem.at[g, b]
            ).start()

    def loaded(g, b):
        pltpu.make_async_copy(xin[g].at[b], xin[g].at[b], load_sem.at[g, b]).wait()

    for kt, ks in ORDER:
        load(UP, block(UP, 1, ks, kt))
        load(QKV, block(QKV, 1, ks, kt))
    for kt, ks in ORDER:
        load(QKV, block(QKV, 0, ks, kt))
    for g in (DOWN, MIXED):
        for kt, ks in ORDER:
            load(g, block(g, 1, ks, kt))
    for g in groups:
        for i, a in enumerate(GROUPS[g].members):
            pltpu.make_async_copy(params[a], lanes(g, own[g], i), own_sem.at[g]).start()
            pltpu.make_async_copy(states[a], lanes(g, st[g], i), st_sem.at[g]).start()
    for g in (UP, DOWN, MIXED):
        for kt, ks in ORDER:
            load(g, block(g, 0, ks, kt))

    def peer_of(g, stage):
        if stage == 3:
            return far_peer
        return near_peer if (stage == 1) == GROUPS[g].near_first else y_peer

    def copy1(g, i):
        return remote(enc1[g].at[i], rec1[g].at[i], rs_s.at[g, i], rs_r.at[g, i], peer_of(g, 1))

    def copy2(g, kt):
        return remote(enc2[g].at[kt], rec2[g].at[kt], rs_s.at[g, 4 + kt], rs_r.at[g, 4 + kt], peer_of(g, 2))

    def copy3(g):
        return remote(enc3[g], rec3[g], rs_s.at[g, 6], rs_r.at[g, 6], peer_of(g, 3))

    def encode1(g, i):
        kt, ks = ORDER[i]
        b = block(g, 1, ks, kt)
        loaded(g, b)
        src, dst = xin[g].at[b], enc1[g].at[i]

        def body(d):
            dst[d, :] = encode(src[d, :])

        loop(g, body)

    def add(g, b, rec):
        acc = xin[g].at[b]

        def body(d):
            acc[d, :] = acc[d, :] + decode(rec[d, :])

        loop(g, body)

    def add_encode(g, b, rec, dst):
        acc = xin[g].at[b]

        def body(d):
            dst[d, :] = encode(acc[d, :] + decode(rec[d, :]))

        loop(g, body)

    def take1(g, i):
        kt, ks = ORDER[i]
        b = block(g, 0, ks, kt)
        loaded(g, b)
        copy1(g, i).wait_recv()
        if ks:
            add_encode(g, b, rec1[g].at[i], enc2[g].at[kt])
            copy2(g, kt).start()
        else:
            add(g, b, rec1[g].at[i])

    def take2(g, kt):
        b = block(g, 0, 0, kt)
        copy2(g, kt).wait_recv()
        if kt:
            add_encode(g, b, rec2[g].at[kt], enc3[g])
            copy3(g).start()
        else:
            add(g, b, rec2[g].at[kt])

    def fold(x):
        w = x.shape[1]
        total = x[:, 0:128]
        for k in range(128, w, 128):
            total = total + x[:, k : k + 128]
        return total

    def squares(g, which, read):
        h, w = shapes[g]
        if GROUPS[g].rows:
            n = len(GROUPS[g].members)

            def body(d):
                v = read(d)
                v = v * v
                for i in range(n):
                    sq[g][which, i, d, :] = fold(v[:, i * (w // n) : (i + 1) * (w // n)])

            loop(g, body)
        else:
            sq[g][which] = jnp.zeros((8, w), jnp.float32)

            def body(d):
                v = read(d)
                sq[g][which] += jnp.sum((v * v).reshape(-1, 8, w), axis=0)

            loop(g, body)

    def copyn(g, j):
        return remote(
            sq[g], sqr[g].at[j - 1], n_s.at[g, j - 1], n_r.at[g, j - 1], lax.rem(m + j, models), "model"
        )

    def own_squares(g):
        pltpu.make_async_copy(own[g], own[g], own_sem.at[g]).wait()
        squares(g, 0, lambda d: own[g][d, :])

    def take3(g):
        copy3(g).wait_recv()
        acc, rec = xin[g].at[0], rec3[g]

        def read(d):
            v = (acc[d, :] + decode(rec[d, :])) * rate
            acc[d, :] = v
            return v

        squares(g, 1, read)
        for j in range(1, models):
            copyn(g, j).start()

    def rule(p, s, v):
        s = hold_rate * s + (1.0 - hold_rate) * v * v
        return p - learn_rate * v * lax.rsqrt(s + 1e-06), s

    def update(g):
        h, w = shapes[g]
        for j in range(1, models):
            copyn(g, j).wait_recv()
        pltpu.make_async_copy(st[g], st[g], st_sem.at[g]).wait()
        acc, half = xin[g].at[0], full[g].at[0]

        def ratio(index, axis):
            p, s = sq[g][(0, *index)], sq[g][(1, *index)]
            for j in range(models - 1):
                p = p + sqr[g][(j, 0, *index)]
                s = s + sqr[g][(j, 1, *index)]
            p = jnp.sum(p, axis=axis, keepdims=True)
            s = jnp.sum(s, axis=axis, keepdims=True)
            return jnp.sqrt(p) * lax.rsqrt(s + 1e-06)

        if GROUPS[g].rows:
            n = len(GROUPS[g].members)

            def body(d):
                for i in range(n):
                    cols = slice(i * (w // n), (i + 1) * (w // n))
                    v = acc[d, cols] * ratio((i, d), 1)
                    p, s = rule(own[g][d, cols], st[g][d, cols], v)
                    own[g][d, cols] = p
                    st[g][d, cols] = s
                    half[d, cols] = p.astype(jnp.bfloat16)

            loop(g, body)
        else:
            t = ratio((), 0)

            def body(d):
                p, s = rule(own[g][d, :], st[g][d, :], acc[d, :] * t)
                own[g][d, :] = p
                st[g][d, :] = s
                half[d, :] = p.astype(jnp.bfloat16)

            loop(g, body)
        gather3(g).start()

    def gather3(g):
        return remote(
            full[g].at[0], full[g].at[block(g, 0, 0, 1)], ag_s.at[g, 6], ag_r.at[g, 6], peer_of(g, 3)
        )

    def gather2(g, kt):
        return remote(
            full[g].at[block(g, 0, 0, kt)],
            full[g].at[block(g, 0, 1, kt)],
            ag_s.at[g, 4 + kt],
            ag_r.at[g, 4 + kt],
            peer_of(g, 2),
        )

    def gather1(g, kt, ks):
        i = kt * 2 + ks
        return remote(
            full[g].at[block(g, 0, ks, kt)],
            full[g].at[block(g, 1, ks, kt)],
            ag_s.at[g, i],
            ag_r.at[g, i],
            peer_of(g, 1),
        )

    def got3(g):
        gather3(g).wait_recv()
        gather2(g, 1).start()
        gather1(g, 1, 0).start()

    def got2(g, kt):
        gather2(g, kt).wait_recv()
        gather1(g, kt, 1).start()

    def got1(g):
        for kt, ks in ((0, 0), (1, 0), (0, 1), (1, 1)):
            gather1(g, kt, ks).wait_recv()

    width = vs.shape[1] // replicas

    def vec_out(j):
        to = lax.rem(r + j, replicas)
        return remote(
            vs.at[:, pl.ds(pl.multiple_of(to * width, width), width)],
            vrec.at[j - 1], v_s.at[j - 1], v_r.at[j - 1], to,
        )

    def vec_back(j):
        return remote(vnext, vag.at[j - 1], w_s.at[j - 1], w_r.at[j - 1], lax.rem(r + j, replicas))

    def vec_update():
        pltpu.make_async_copy(vown, vown, vown_sem).wait()
        total = vown[...]
        for j in range(1, replicas):
            vec_out(j).wait_recv()
            total = total + vrec[j - 1]
        v = total * rate
        p, s = rule(param_norm[...], state_norm[...], v[0:1, :])
        next_norm[...] = p
        new_norm[...] = s
        vnext[0:1, :] = p
        p, s = rule(param_bias[...], state_bias[...], v[1:2, :])
        next_bias[...] = p
        new_bias[...] = s
        vnext[1:2, :] = p
        for j in range(1, replicas):
            vec_back(j).start()

    def vec_finish():
        vh_norm[pl.ds(r, 1), :] = vnext[0:1, :]
        vh_bias[pl.ds(r, 1), :] = vnext[1:2, :]
        for j in range(1, replicas):
            vec_back(j).wait_recv()
            at = lax.rem(r + replicas - j, replicas)
            vh_norm[pl.ds(at, 1), :] = vag[j - 1, 0:1, :]
            vh_bias[pl.ds(at, 1), :] = vag[j - 1, 1:2, :]
        half_norm[...] = vh_norm[...].astype(jnp.bfloat16)
        half_bias[...] = vh_bias[...].astype(jnp.bfloat16)

    vs[0:1, :] = slope_norm[...]
    vs[1:2, :] = slope_bias[...]
    encode1(MIXED, 1)
    encode1(MIXED, 0)
    encode1(QKV, 0)
    pl.semaphore_wait(barrier, replicas + models - 2)
    copy1(QKV, 0).start()
    copy1(MIXED, 0).start()
    encode1(QKV, 3)
    encode1(QKV, 1)
    encode1(UP, 3)
    own_squares(UP)
    encode1(UP, 2)
    own_squares(DOWN)
    copy1(MIXED, 1).start()
    encode1(QKV, 2)
    copy1(UP, 2).start()
    pltpu.make_async_copy(vs.at[:, pl.ds(pl.multiple_of(r * width, width), width)], vown, vown_sem).start()
    for j in range(1, replicas):
        vec_out(j).start()
    copy1(QKV, 3).start()
    copy1(QKV, 1).start()
    take1(MIXED, 0)
    encode1(UP, 1)
    encode1(MIXED, 2)
    encode1(UP, 0)
    copy1(QKV, 2).start()
    copy1(UP, 0).start()
    encode1(DOWN, 0)
    take1(QKV, 0)
    own_squares(MIXED)
    take1(QKV, 3)
    take1(UP, 2)
    own_squares(QKV)
    take1(UP, 0)
    copy1(UP, 1).start()
    take1(QKV, 1)
    take1(QKV, 2)
    encode1(DOWN, 1)
    copy1(DOWN, 0).start()
    take2(QKV, 1)
    copy1(UP, 3).start()
    take1(MIXED, 1)
    encode1(MIXED, 3)
    copy1(DOWN, 1).start()
    take1(UP, 1)
    copy1(MIXED, 3).start()
    encode1(DOWN, 3)
    take2(UP, 1)
    take2(QKV, 0)
    vec_update()
    take3(QKV)
    take1(DOWN, 0)
    take1(UP, 3)
    copy1(DOWN, 3).start()
    update(QKV)
    copy1(MIXED, 2).start()
    take2(UP, 0)
    take3(UP)
    encode1(DOWN, 2)
    copy1(DOWN, 2).start()
    take1(DOWN, 1)
    take1(DOWN, 3)
    update(UP)
    gather2(QKV, 0).start()
    take1(DOWN, 2)
    gather2(UP, 0).start()
    take1(MIXED, 2)
    take2(DOWN, 0)
    take2(DOWN, 1)
    gather1(UP, 0, 0).start()
    got3(UP)
    got2(QKV, 0)
    got2(UP, 0)
    got3(QKV)
    take3(DOWN)
    update(DOWN)
    take1(MIXED, 3)
    got2(UP, 1)
    take2(MIXED, 0)
    take2(MIXED, 1)
    got1(UP)
    gather2(DOWN, 0).start()
    vec_finish()
    gather1(DOWN, 0, 0).start()
    got3(DOWN)
    take3(MIXED)
    update(MIXED)
    gather1(QKV, 0, 0).start()
    gather1(MIXED, 0, 0).start()
    got2(DOWN, 0)
    got2(DOWN, 1)
    gather2(MIXED, 0).start()
    got3(MIXED)
    got2(QKV, 1)
    got2(MIXED, 0)
    got2(MIXED, 1)
    got1(DOWN)
    got1(QKV)
    got1(MIXED)

    for g in groups:
        for i in range(4):
            copy1(g, i).wait_send()
        for kt in (0, 1):
            copy2(g, kt).wait_send()
            gather2(g, kt).wait_send()
            for ks in (0, 1):
                gather1(g, kt, ks).wait_send()
        copy3(g).wait_send()
        gather3(g).wait_send()
        for j in range(1, models):
            copyn(g, j).wait_send()
    for j in range(1, replicas):
        vec_out(j).wait_send()
        vec_back(j).wait_send()


def fused(replicas, models, *args):
    slopes, params = args[0:6], args[8:14]
    f32, bf16 = jnp.float32, jnp.bfloat16
    vec = args[6].shape[1]
    width = vec // replicas
    row = lambda a: a.reshape(1, -1)
    args = (*args[0:14], row(args[14]), row(args[15]), *args[16:22], row(args[22]), row(args[23]))
    shapes = []
    for g in GROUPS:
        h, w = params[g.members[0]].shape
        shapes.append((h, w * len(g.members)))
    S = jax.ShapeDtypeStruct
    n = len(GROUPS)
    held = [((replicas, *s), bf16) for s in shapes] + [(s, f32) for s in shapes] * 2
    held += [((replicas, width), bf16)] * 2 + [((1, width), f32)] * 4
    ANY, VM = pl.BlockSpec(memory_space=pl.ANY), pl.BlockSpec(memory_space=pltpu.VMEM)
    part = [ANY] * 6 + [VM] * 2
    scratch = []
    for count, dtype in ((8, f32), (4, bf16), (4, bf16), (2, bf16), (2, bf16), (0, bf16), (0, bf16)):
        scratch += [pltpu.VMEM((count, *s) if count else s, dtype) for s in shapes]
    sq = [(2, len(g.members), s[0], 128) if g.rows else (2, 8, s[1]) for g, s in zip(GROUPS, shapes)]
    scratch += [pltpu.VMEM(s, f32) for s in sq]
    scratch += [pltpu.VMEM((models - 1, *s), f32) for s in sq]
    scratch += [
        pltpu.VMEM((2, vec), f32),
        pltpu.VMEM((2, width), f32),
        pltpu.VMEM((replicas - 1, 2, width), f32),
        pltpu.VMEM((2, width), f32),
        pltpu.VMEM((replicas - 1, 2, width), f32),
        pltpu.VMEM((replicas, width), f32),
        pltpu.VMEM((replicas, width), f32),
    ]
    dma = pltpu.SemaphoreType.DMA
    scratch += [dma((n, 7))] * 4 + [dma((n, models - 1))] * 2 + [dma((replicas - 1,))] * 4
    scratch += [dma((n, 8))] + [dma((n,))] * 2 + [dma(())]
    out = pl.pallas_call(
        functools.partial(kernel, replicas, models, 4.0, shapes),
        out_shape=[pltpu.VMEM(*h) for h in held],
        in_specs=part * 3,
        out_specs=[VM] * len(held),
        scratch_shapes=scratch,
        compiler_params=pltpu.CompilerParams(
            collective_id=0, has_side_effects=True, vmem_limit_bytes=54 * 1024 * 1024
        ),
    )(*args)
    outs = [S(a.shape[1:], bf16) for a in slopes] + [S((replicas, width), bf16)] * 2
    for _ in range(2):
        outs += [S(a.shape, f32) for a in params] + [S((1, width), f32)] * 2
    out = pl.pallas_call(
        functools.partial(finish, shapes),
        out_shape=outs,
        in_specs=[VM] * len(held),
        out_specs=[ANY] * len(outs),
        scratch_shapes=[dma((3, n)), dma((6,))],
        compiler_params=pltpu.CompilerParams(vmem_limit_bytes=1024 * 1024),
    )(*out)
    flat = lambda a: a.reshape(-1)
    return (
        *out[0:6], flat(out[6]), flat(out[7]),
        *out[8:14], flat(out[14]), flat(out[15]),
        *out[16:22], flat(out[22]), flat(out[23]),
    )


def plain(
    slope_up,
    slope_down,
    slope_query,
    slope_key,
    slope_value,
    slope_mixed,
    slope_norm,
    slope_bias,
    param_up,
    param_down,
    param_query,
    param_key,
    param_value,
    param_mixed,
    param_norm,
    param_bias,
    state_up,
    state_down,
    state_query,
    state_key,
    state_value,
    state_mixed,
    state_norm,
    state_bias,
):
    mean_up, mean_down, mean_query, mean_key, mean_value, mean_mixed = (
        lax.psum_scatter(slope_up[0], "replica", scatter_dimension=0, tiled=True),
        lax.psum_scatter(slope_down[0], "replica", scatter_dimension=1, tiled=True),
        lax.psum_scatter(slope_query[0], "replica", scatter_dimension=0, tiled=True),
        lax.psum_scatter(slope_key[0], "replica", scatter_dimension=0, tiled=True),
        lax.psum_scatter(slope_value[0], "replica", scatter_dimension=0, tiled=True),
        lax.psum_scatter(slope_mixed[0], "replica", scatter_dimension=1, tiled=True),
    )
    whole_norm, whole_bias = lax.psum((slope_norm[0], slope_bias[0]), "replica")
    place = lax.axis_index("replica")
    mean_norm = lax.dynamic_slice_in_dim(
        whole_norm, place * param_norm.shape[0], param_norm.shape[0]
    )
    mean_bias = lax.dynamic_slice_in_dim(
        whole_bias, place * param_bias.shape[0], param_bias.shape[0]
    )
    mean_rate = lax.axis_size("replica") ** (-0.5)
    mean_up = mean_up * mean_rate
    mean_down = mean_down * mean_rate
    mean_query = mean_query * mean_rate
    mean_key = mean_key * mean_rate
    mean_value = mean_value * mean_rate
    mean_mixed = mean_mixed * mean_rate
    mean_norm = mean_norm * mean_rate
    mean_bias = mean_bias * mean_rate
    (
        own_up,
        own_down,
        own_query,
        own_key,
        own_value,
        own_mixed,
        slope_up_norm,
        slope_down_norm,
        slope_query_norm,
        slope_key_norm,
        slope_value_norm,
        slope_mixed_norm,
    ) = lax.psum(
        (
            jnp.sum(param_up * param_up, axis=1, keepdims=True),
            jnp.sum(param_down * param_down, axis=0, keepdims=True),
            jnp.sum(param_query * param_query, axis=1, keepdims=True),
            jnp.sum(param_key * param_key, axis=1, keepdims=True),
            jnp.sum(param_value * param_value, axis=1, keepdims=True),
            jnp.sum(param_mixed * param_mixed, axis=0, keepdims=True),
            jnp.sum(mean_up * mean_up, axis=1, keepdims=True),
            jnp.sum(mean_down * mean_down, axis=0, keepdims=True),
            jnp.sum(mean_query * mean_query, axis=1, keepdims=True),
            jnp.sum(mean_key * mean_key, axis=1, keepdims=True),
            jnp.sum(mean_value * mean_value, axis=1, keepdims=True),
            jnp.sum(mean_mixed * mean_mixed, axis=0, keepdims=True),
        ),
        "model",
    )
    mean_up = mean_up * (jnp.sqrt(own_up) * lax.rsqrt(slope_up_norm + 1e-06))
    mean_down = mean_down * (jnp.sqrt(own_down) * lax.rsqrt(slope_down_norm + 1e-06))
    mean_query = mean_query * (jnp.sqrt(own_query) * lax.rsqrt(slope_query_norm + 1e-06))
    mean_key = mean_key * (jnp.sqrt(own_key) * lax.rsqrt(slope_key_norm + 1e-06))
    mean_value = mean_value * (jnp.sqrt(own_value) * lax.rsqrt(slope_value_norm + 1e-06))
    mean_mixed = mean_mixed * (jnp.sqrt(own_mixed) * lax.rsqrt(slope_mixed_norm + 1e-06))
    state_new_up = hold_rate * state_up + (1.0 - hold_rate) * mean_up * mean_up
    next_up = param_up - learn_rate * mean_up * lax.rsqrt(state_new_up + 1e-06)
    state_new_down = hold_rate * state_down + (1.0 - hold_rate) * mean_down * mean_down
    next_down = param_down - learn_rate * mean_down * lax.rsqrt(state_new_down + 1e-06)
    state_new_query = hold_rate * state_query + (1.0 - hold_rate) * mean_query * mean_query
    next_query = param_query - learn_rate * mean_query * lax.rsqrt(state_new_query + 1e-06)
    state_new_key = hold_rate * state_key + (1.0 - hold_rate) * mean_key * mean_key
    next_key = param_key - learn_rate * mean_key * lax.rsqrt(state_new_key + 1e-06)
    state_new_value = hold_rate * state_value + (1.0 - hold_rate) * mean_value * mean_value
    next_value = param_value - learn_rate * mean_value * lax.rsqrt(state_new_value + 1e-06)
    state_new_mixed = hold_rate * state_mixed + (1.0 - hold_rate) * mean_mixed * mean_mixed
    next_mixed = param_mixed - learn_rate * mean_mixed * lax.rsqrt(state_new_mixed + 1e-06)
    state_new_norm = hold_rate * state_norm + (1.0 - hold_rate) * mean_norm * mean_norm
    next_norm = param_norm - learn_rate * mean_norm * lax.rsqrt(state_new_norm + 1e-06)
    state_new_bias = hold_rate * state_bias + (1.0 - hold_rate) * mean_bias * mean_bias
    next_bias = param_bias - learn_rate * mean_bias * lax.rsqrt(state_new_bias + 1e-06)
    half_up, half_down, half_query, half_key, half_value, half_mixed, half_norm, half_bias = (
        lax.all_gather(next_up.astype(jnp.bfloat16), "replica", axis=0, tiled=True),
        lax.all_gather(next_down.astype(jnp.bfloat16), "replica", axis=1, tiled=True),
        lax.all_gather(next_query.astype(jnp.bfloat16), "replica", axis=0, tiled=True),
        lax.all_gather(next_key.astype(jnp.bfloat16), "replica", axis=0, tiled=True),
        lax.all_gather(next_value.astype(jnp.bfloat16), "replica", axis=0, tiled=True),
        lax.all_gather(next_mixed.astype(jnp.bfloat16), "replica", axis=1, tiled=True),
        lax.all_gather(next_norm.astype(jnp.bfloat16), "replica", axis=0, tiled=True),
        lax.all_gather(next_bias.astype(jnp.bfloat16), "replica", axis=0, tiled=True),
    )
    return (
        half_up,
        half_down,
        half_query,
        half_key,
        half_value,
        half_mixed,
        half_norm,
        half_bias,
        next_up,
        next_down,
        next_query,
        next_key,
        next_value,
        next_mixed,
        next_norm,
        next_bias,
        state_new_up,
        state_new_down,
        state_new_query,
        state_new_key,
        state_new_value,
        state_new_mixed,
        state_new_norm,
        state_new_bias,
    )


def solution(mesh):
    replicas, models = mesh.shape["replica"], mesh.shape["model"]

    def local(*args):
        ok = replicas == 2**3 and all(a.shape[k] % 128 == 0 for a in args[8:14] for k in (0, 1))
        if ok and args[14].shape[0] % 128 == 0:
            return fused(replicas, models, *args)
        return plain(*args)

    placed = (
        P("replica", None, "model"),
        P("replica", "model", None),
        P("replica", None, "model"),
        P("replica", None, "model"),
        P("replica", None, "model"),
        P("replica", "model", None),
        P("replica", None),
        P("replica", None),
        P("replica", "model"),
        P("model", "replica"),
        P("replica", "model"),
        P("replica", "model"),
        P("replica", "model"),
        P("model", "replica"),
        P("replica"),
        P("replica"),
        P("replica", "model"),
        P("model", "replica"),
        P("replica", "model"),
        P("replica", "model"),
        P("replica", "model"),
        P("model", "replica"),
        P("replica"),
        P("replica"),
    )
    return jax.shard_map(
        local,
        mesh=mesh,
        in_specs=placed,
        out_specs=(
            P(None, "model"),
            P("model", None),
            P(None, "model"),
            P(None, "model"),
            P(None, "model"),
            P("model", None),
            P(),
            P(),
            P("replica", "model"),
            P("model", "replica"),
            P("replica", "model"),
            P("replica", "model"),
            P("replica", "model"),
            P("model", "replica"),
            P("replica"),
            P("replica"),
            P("replica", "model"),
            P("model", "replica"),
            P("replica", "model"),
            P("replica", "model"),
            P("replica", "model"),
            P("model", "replica"),
            P("replica"),
            P("replica"),
        ),
        check_vma=False,
    )
```

profile of v0, /device:TPU:0, one launch (start us, length us, event | category | flops | bytes accessed | tf_op | source)
XLA Modules:
  0.0 138.3 jit_solution(15102658268231249617)
XLA Ops:
  0.7 133.8 %shard_map.415 = (bf16[8,128,1024]{2,1,0:T(8,128)(2,1)S(1)}, bf16[8,1024,128]{2,1,0:T(8,128)(2,1)S(1)}, bf16[8,256,128]{2,1,0:T(8,128)(2,1)S(1)}, bf16[8,128,768...) custom-call(f32[1,1024,1024]{2,1,0:T(8,128)} %refs_0_.1, ...), custom_call_target="tpu_custom_call" | custom-call | tf_op jit(solution)/shard_map/pallas_call | solution.py:547
  134.5 3.8 %shard_map.416 = (bf16[1024,1024]{1,0:T(8,128)(2,1)}, bf16[1024,1024]{1,0:T(8,128)(2,1)}, bf16[1024,256]{1,0:T(8,128)(2,1)}, bf16[1024,256]{1,0:T(8,128)(2,1)}, ...) custom-call(bf16[8,128,1024]{2,1,0:T(8,128)(2,1)S(1)} %get-tuple-ele, ...), custom_call_target="tpu_custom_call" | custom-call | tf_op jit(solution)/shard_map/pallas_call | solution.py:560
where the time goes:
time: 138 us
  Pallas kernels  138 us (100%)
    pallas_call x1, Pallas kernels, fused(): pl.pallas_call(functools.partial(kernel, replicas, models, 4.0, shapes),...  134 us
    pallas_call x1, Pallas kernels, fused(): pl.pallas_call(functools.partial(finish, shapes), out_shape=outs, in_spec...  3.8 us

commit v1 on v0

v1 whole, which is shorter than its diff:
```python
import functools

import jax
import jax.numpy as jnp
from jax import lax
from jax.experimental import pallas as pl
from jax.experimental.pallas import tpu as pltpu
from jax.sharding import PartitionSpec as P

learn_rate = 0.025
hold_rate = 0.7
root = 9
MESH = pl.DeviceIdType.MESH


class Group:
    def __init__(self, members, rows):
        self.members = members
        self.rows = rows


GROUPS = (Group((0,), True), Group((1,), False), Group((5,), False), Group((2, 3, 4), True))
KINDS = (("A", "A", "B", "B"), ("A", "A", "A", "A"), ("A",), ("A", "B", "A", "B"))
CHUNKS = ((0, 0), (0, 2), (0, 3), (3, 1), (1, 2), (3, 0), (1, 0), (1, 3), (1, 1), (3, 2), (0, 1), (3, 3), (2, 0))
OWN = (0, 3, 1, 2)
SENT = ({"A": (4, 1, 0), "B": (1, 2, 0)}, {"A": (4, 2, 3), "B": (1, 4, 6)})
STEP = 16384
END = (
    ("E", 0, 0, 7), ("sY", 0, 0, 6), ("E", 0, 0, 5), ("sY", 0, 0, 4), ("E", 0, 0, 3), ("E", 0, 2, 6),
    ("sI", 0, 2, 6), ("E", 0, 2, 7), ("sI", 0, 2, 7), ("E", 0, 2, 4), ("E", 0, 2, 5), ("E", 0, 2, 2),
    ("E", 0, 2, 3), ("E", 0, 0, 1), ("E", 0, 3, 6), ("E", 0, 3, 7), ("E", 0, 3, 4), ("sY", 0, 0, 2),
    ("E", 0, 3, 5), ("E", 0, 3, 2), ("E", 0, 3, 3), ("sI", 0, 2, 4), ("E", 3, 1, 6), ("E", 3, 1, 7),
    ("E", 3, 1, 4), ("E", 3, 1, 5), ("E", 3, 1, 2), ("E", 3, 1, 3), ("E", 1, 2, 7), ("E", 1, 2, 5),
    ("E", 1, 2, 3), ("sY", 0, 0, 0), ("E", 1, 2, 1), ("V", 0, 0, 0), ("E", 3, 0, 7), ("E", 3, 0, 5),
    ("sI", 0, 2, 5), ("E", 3, 0, 3), ("E", 3, 0, 1), ("G", 0, 0, 6), ("E", 1, 0, 7), ("E", 1, 0, 5),
    ("E", 1, 0, 3), ("E", 1, 0, 1), ("E", 1, 3, 7), ("sY", 1, 2, 6), ("E", 1, 3, 5), ("E", 1, 3, 3),
    ("E", 1, 3, 1), ("sI", 0, 0, 6), ("E", 1, 1, 7), ("E", 1, 1, 5), ("G", 0, 0, 4), ("E", 1, 1, 3),
    ("E", 1, 1, 1), ("E", 3, 2, 7), ("E", 3, 2, 5), ("E", 3, 2, 3), ("sY", 1, 2, 4), ("E", 3, 2, 1),
    ("E", 0, 1, 7), ("E", 0, 1, 5), ("E", 0, 1, 3), ("sI", 0, 0, 4), ("E", 0, 1, 1), ("G", 0, 0, 2),
    ("E", 3, 3, 6), ("E", 3, 3, 7), ("E", 3, 3, 4), ("E", 3, 3, 5), ("E", 3, 3, 2), ("E", 3, 3, 3),
    ("sY", 1, 2, 2), ("E", 2, 0, 7), ("E", 2, 0, 5), ("E", 2, 0, 3), ("sI", 0, 0, 2), ("E", 2, 0, 1),
    ("sY", 1, 2, 0), ("sI", 0, 2, 2), ("G", 1, 2, 6), ("sY", 3, 0, 6), ("sI", 0, 2, 3), ("G", 1, 2, 4),
    ("sY", 3, 0, 4), ("sI", 0, 3, 6), ("G", 1, 2, 2), ("sY", 3, 0, 2), ("G", 0, 2, 1), ("sI", 0, 3, 7),
    ("sY", 0, 2, 0), ("G", 3, 0, 6), ("sY", 3, 0, 0), ("sI", 0, 3, 4), ("G", 3, 0, 4), ("sY", 1, 0, 6),
    ("sI", 0, 3, 5), ("G", 3, 0, 2), ("N", 0, 0, 0), ("n", 0, 0, 0), ("sY", 1, 0, 4), ("sI", 0, 3, 2),
    ("N", 0, 2, 0), ("n", 0, 2, 0), ("sY", 1, 0, 2), ("sI", 0, 3, 3), ("sY", 1, 0, 0), ("sI", 3, 1, 6),
    ("G", 1, 0, 6), ("U", 0, 0, 0), ("aY", 0, 0, 0), ("U", 0, 2, 0), ("sI", 3, 1, 7), ("G", 1, 0, 4),
    ("aY", 0, 0, 2), ("sI", 3, 1, 4), ("G", 1, 0, 2), ("sI", 3, 1, 5), ("aY", 0, 2, 0), ("sI", 3, 1, 2),
    ("G", 0, 3, 1), ("sY", 0, 3, 0), ("sI", 3, 1, 3), ("aY", 0, 0, 4), ("aI", 0, 0, 0), ("V", 0, 0, 1),
    ("aI", 0, 2, 0), ("sY", 1, 3, 6), ("aI", 0, 2, 1), ("sY", 1, 3, 4), ("N", 0, 3, 0), ("n", 0, 3, 0),
    ("sI", 1, 2, 6), ("sY", 1, 3, 2), ("sI", 1, 2, 4), ("sY", 1, 3, 0), ("G", 1, 3, 6), ("G", 3, 1, 1),
    ("sI", 1, 2, 2), ("U", 0, 3, 0), ("sY", 3, 1, 0), ("G", 1, 3, 4), ("aI", 0, 3, 0), ("aY", 0, 3, 0),
    ("G", 1, 3, 2), ("sY", 1, 1, 6), ("sI", 3, 0, 6), ("sY", 1, 1, 4), ("sI", 3, 0, 4), ("N", 3, 1, 0),
    ("n", 3, 1, 0), ("sI", 3, 0, 2), ("aY", 0, 0, 6), ("aI", 0, 3, 1), ("sY", 1, 1, 2), ("sI", 1, 0, 6),
    ("G", 1, 1, 6), ("U", 3, 1, 0), ("sY", 1, 1, 0), ("sI", 1, 0, 4), ("G", 1, 1, 4), ("sY", 3, 2, 6),
    ("sI", 1, 0, 2), ("sY", 3, 2, 4), ("sI", 1, 3, 6), ("G", 1, 1, 2), ("N", 1, 2, 0), ("sY", 3, 2, 2),
    ("sI", 1, 3, 4), ("sY", 3, 2, 0), ("G", 3, 2, 6), ("sY", 0, 1, 6), ("sI", 1, 3, 2), ("G", 3, 2, 4),
    ("sY", 0, 1, 4), ("sI", 1, 1, 6), ("G", 3, 2, 2), ("sY", 0, 1, 2), ("N", 3, 0, 0), ("n", 3, 0, 0),
    ("sI", 1, 1, 4), ("sY", 0, 1, 0), ("sI", 1, 1, 2), ("G", 0, 1, 6), ("aY", 3, 1, 0), ("aI", 3, 1, 0),
    ("G", 0, 1, 4), ("U", 3, 0, 0), ("aY", 3, 0, 0), ("sI", 3, 2, 6), ("G", 0, 1, 2), ("sY", 2, 0, 6),
    ("N", 1, 0, 0), ("sI", 3, 2, 4), ("sY", 2, 0, 4), ("sI", 3, 2, 2), ("aY", 3, 0, 2), ("aI", 3, 1, 1),
    ("N", 1, 3, 0), ("sI", 0, 1, 6), ("aY", 3, 0, 4), ("G", 2, 0, 6), ("sI", 0, 1, 4), ("sY", 2, 0, 2),
    ("G", 2, 0, 4), ("sY", 2, 0, 0), ("sI", 0, 1, 2), ("N", 1, 1, 0), ("V", 0, 0, 2), ("n", 1, 0, 0),
    ("aI", 3, 0, 0), ("sI", 3, 3, 6), ("U", 1, 2, 0), ("aY", 1, 2, 0), ("U", 1, 0, 0), ("aY", 1, 0, 0),
    ("U", 1, 3, 0), ("U", 1, 1, 0), ("aI", 1, 2, 0), ("G", 2, 0, 2), ("aY", 1, 2, 2), ("sI", 3, 3, 7),
    ("aY", 1, 0, 2), ("sI", 3, 3, 4), ("N", 3, 2, 0), ("n", 3, 2, 0), ("sI", 3, 3, 5), ("aY", 1, 3, 0),
    ("sI", 3, 3, 2), ("aY", 1, 1, 0), ("sI", 3, 3, 3), ("aY", 1, 3, 2), ("U", 3, 2, 0), ("aI", 1, 0, 0),
    ("sI", 2, 0, 6), ("aY", 1, 2, 4), ("sI", 2, 0, 4), ("aY", 1, 0, 4), ("N", 0, 1, 0), ("n", 0, 1, 0),
    ("sI", 2, 0, 2), ("aY", 3, 2, 0), ("aI", 1, 3, 0), ("aY", 1, 1, 2), ("U", 0, 1, 0), ("aY", 0, 1, 0),
    ("aI", 1, 1, 0), ("aY", 1, 2, 6), ("aI", 3, 2, 0), ("G", 3, 3, 1), ("sY", 3, 3, 0), ("aI", 0, 1, 0),
    ("aY", 3, 0, 6), ("aY", 1, 3, 4), ("aY", 3, 2, 2), ("N", 3, 3, 0), ("n", 3, 3, 0), ("aY", 1, 1, 4),
    ("aY", 0, 1, 2), ("aY", 1, 0, 6), ("N", 2, 0, 0), ("n", 2, 0, 0), ("U", 3, 3, 0), ("aI", 3, 3, 0),
    ("aY", 3, 3, 0), ("aY", 3, 2, 4), ("U", 2, 0, 0), ("aI", 2, 0, 0), ("aY", 1, 3, 6), ("aY", 2, 0, 0),
    ("aI", 3, 3, 1), ("aY", 1, 1, 6), ("aY", 3, 2, 6), ("aY", 0, 1, 4), ("aY", 0, 1, 6), ("aY", 2, 0, 4),
    ("aY", 2, 0, 2), ("aY", 2, 0, 6),
)
MID = (
    ("E", 0, 0, 7), ("sY", 0, 0, 6), ("E", 0, 0, 5), ("sY", 0, 0, 4), ("E", 0, 0, 3), ("E", 0, 0, 1),
    ("E", 1, 2, 7), ("E", 1, 2, 5), ("E", 1, 2, 3), ("sY", 0, 0, 2), ("E", 1, 2, 1), ("E", 3, 0, 7),
    ("E", 3, 0, 5), ("E", 3, 0, 3), ("E", 3, 0, 1), ("E", 1, 0, 7), ("E", 1, 0, 5), ("E", 1, 0, 3),
    ("E", 1, 0, 1), ("E", 1, 3, 7), ("E", 1, 3, 5), ("E", 1, 3, 3), ("sY", 0, 0, 0), ("E", 1, 3, 1),
    ("E", 1, 1, 7), ("E", 1, 1, 5), ("E", 1, 1, 3), ("E", 1, 1, 1), ("E", 3, 2, 7), ("E", 3, 2, 5),
    ("E", 3, 2, 3), ("E", 3, 2, 1), ("G", 0, 2, 6), ("sI", 0, 2, 6), ("E", 0, 1, 7), ("E", 0, 1, 5),
    ("sY", 1, 2, 6), ("E", 0, 1, 3), ("E", 0, 1, 1), ("E", 2, 0, 7), ("E", 2, 0, 5), ("V", 0, 0, 0),
    ("E", 2, 0, 3), ("E", 2, 0, 1), ("G", 0, 2, 7), ("sI", 0, 2, 7), ("sY", 1, 2, 4), ("G", 0, 2, 4),
    ("sI", 0, 2, 4), ("sY", 1, 2, 2), ("G", 0, 2, 0), ("sO", 0, 2, 0), ("G", 0, 2, 5), ("sI", 0, 2, 5),
    ("sY", 1, 2, 0), ("G", 0, 2, 1), ("sO", 0, 2, 1), ("G", 0, 0, 6), ("sI", 0, 0, 6), ("sY", 3, 0, 6),
    ("G", 0, 0, 4), ("sI", 0, 0, 4), ("sY", 3, 0, 4), ("sY", 3, 0, 2), ("G", 0, 0, 0), ("sO", 0, 0, 0),
    ("sY", 3, 0, 0), ("sY", 1, 0, 6), ("N", 0, 0, 0), ("n", 0, 0, 0), ("G", 0, 2, 3), ("sY", 0, 2, 2),
    ("G", 0, 3, 6), ("sI", 0, 3, 6), ("sY", 1, 0, 4), ("G", 0, 3, 7), ("sI", 0, 3, 7), ("U", 0, 0, 0),
    ("aY", 0, 0, 2), ("aO", 0, 0, 2), ("aI", 0, 0, 2), ("G", 0, 3, 4), ("sI", 0, 3, 4), ("sY", 1, 0, 2),
    ("G", 0, 3, 0), ("sO", 0, 3, 0), ("N", 0, 2, 0), ("n", 0, 2, 0), ("G", 0, 3, 5), ("sI", 0, 3, 5),
    ("sY", 1, 0, 0), ("G", 0, 3, 1), ("sO", 0, 3, 1), ("sY", 1, 3, 6), ("aO", 0, 0, 4), ("aY", 0, 0, 4),
    ("U", 0, 2, 0), ("aO", 0, 2, 2), ("aI", 0, 2, 2), ("G", 3, 1, 6), ("sI", 3, 1, 6), ("aY", 0, 2, 2),
    ("G", 3, 1, 7), ("sI", 3, 1, 7), ("G", 0, 3, 3), ("G", 3, 1, 4), ("sY", 0, 3, 2), ("sI", 3, 1, 4),
    ("aO", 0, 2, 4), ("G", 3, 1, 5), ("sI", 3, 1, 5), ("sY", 1, 3, 4), ("G", 3, 1, 0), ("sO", 3, 1, 0),
    ("sY", 1, 3, 2), ("G", 3, 1, 1), ("sO", 3, 1, 1), ("aO", 0, 2, 3), ("aI", 0, 2, 3), ("sY", 1, 3, 0),
    ("aI", 0, 0, 0), ("N", 0, 3, 0), ("n", 0, 3, 0), ("G", 3, 1, 3), ("sY", 3, 1, 2), ("aI", 0, 2, 0),
    ("aO", 0, 2, 5), ("aY", 0, 0, 0), ("aI", 0, 2, 1), ("sY", 1, 1, 6), ("aO", 0, 0, 6), ("U", 0, 3, 0),
    ("aO", 0, 3, 2), ("aI", 0, 3, 2), ("G", 1, 2, 6), ("sI", 1, 2, 6), ("aY", 0, 0, 6), ("aO", 0, 2, 6),
    ("N", 3, 1, 0), ("n", 3, 1, 0), ("G", 1, 2, 4), ("sI", 1, 2, 4), ("aY", 0, 3, 2), ("aO", 0, 2, 7),
    ("sY", 1, 1, 4), ("aO", 0, 3, 4), ("aI", 0, 3, 0), ("U", 3, 1, 0), ("sY", 1, 1, 2), ("aI", 3, 1, 2),
    ("G", 1, 2, 0), ("sO", 1, 2, 0), ("G", 3, 0, 6), ("sI", 3, 0, 6), ("G", 3, 0, 4), ("V", 0, 0, 1),
    ("sY", 1, 1, 0), ("N", 1, 2, 0), ("aO", 3, 1, 2), ("aI", 0, 3, 3), ("sY", 3, 2, 6), ("aO", 0, 3, 6),
    ("sI", 3, 0, 4), ("aO", 0, 3, 3), ("sY", 3, 2, 4), ("aI", 0, 3, 1), ("G", 3, 0, 0), ("sY", 3, 2, 2),
    ("G", 1, 0, 6), ("sO", 3, 0, 0), ("sI", 1, 0, 6), ("sY", 3, 2, 0), ("G", 1, 0, 4), ("aO", 0, 3, 5),
    ("sI", 1, 0, 4), ("sY", 0, 1, 6), ("N", 3, 0, 0), ("n", 3, 0, 0), ("aO", 3, 1, 4), ("sY", 0, 1, 4),
    ("aO", 0, 3, 7), ("G", 1, 3, 6), ("sI", 1, 3, 6), ("sY", 0, 1, 2), ("G", 1, 0, 0), ("sO", 1, 0, 0),
    ("G", 1, 3, 4), ("sI", 1, 3, 4), ("U", 3, 0, 0), ("aY", 3, 1, 2), ("aI", 3, 0, 2), ("N", 1, 0, 0),
    ("aO", 3, 0, 2), ("sY", 0, 1, 0), ("G", 1, 3, 0), ("sO", 1, 3, 0), ("G", 1, 1, 6), ("aY", 3, 0, 2),
    ("sI", 1, 1, 6), ("N", 1, 3, 0), ("G", 1, 1, 4), ("sY", 2, 0, 6), ("sI", 1, 1, 4), ("aO", 3, 0, 4),
    ("aO", 3, 1, 3), ("aI", 3, 1, 3), ("aY", 3, 0, 4), ("G", 1, 1, 0), ("sO", 1, 1, 0), ("sY", 2, 0, 4),
    ("aI", 3, 1, 0), ("G", 3, 2, 6), ("sY", 2, 0, 2), ("sI", 3, 2, 6), ("N", 1, 1, 0), ("n", 1, 0, 0),
    ("G", 3, 2, 4), ("aO", 3, 1, 5), ("sI", 3, 2, 4), ("sY", 2, 0, 0), ("aO", 3, 1, 6), ("aI", 3, 1, 1),
    ("U", 1, 2, 0), ("aY", 1, 2, 2), ("aO", 1, 2, 2), ("aI", 1, 2, 2), ("U", 1, 0, 0), ("aO", 1, 0, 2),
    ("U", 1, 3, 0), ("U", 1, 1, 0), ("G", 3, 2, 0), ("aY", 1, 0, 2), ("aI", 1, 0, 2), ("N", 3, 2, 0),
    ("n", 3, 2, 0), ("G", 0, 1, 6), ("sO", 3, 2, 0), ("sI", 0, 1, 6), ("aY", 1, 3, 2), ("G", 0, 1, 4),
    ("aO", 3, 1, 7), ("sI", 0, 1, 4), ("aY", 1, 1, 2), ("aO", 1, 3, 2), ("U", 3, 2, 0), ("aO", 1, 2, 4),
    ("aY", 1, 2, 4), ("aI", 3, 0, 0), ("G", 3, 3, 6), ("aO", 1, 0, 4), ("aY", 3, 0, 0), ("sI", 3, 3, 6),
    ("G", 0, 1, 0), ("aI", 1, 2, 0), ("sO", 0, 1, 0), ("aY", 1, 2, 0), ("N", 0, 1, 0), ("n", 0, 1, 0),
    ("aI", 1, 3, 2), ("V", 0, 0, 2), ("G", 3, 3, 7), ("aY", 1, 0, 4), ("aO", 1, 1, 2), ("G", 3, 3, 4),
    ("sI", 3, 3, 7), ("aY", 3, 0, 6), ("G", 3, 3, 0), ("sO", 3, 3, 0), ("G", 3, 3, 5), ("sI", 3, 3, 4),
    ("aY", 3, 2, 2), ("aO", 1, 2, 6), ("U", 0, 1, 0), ("sI", 3, 3, 5), ("aY", 1, 2, 6), ("aO", 3, 0, 6),
    ("aI", 1, 1, 2), ("aY", 1, 3, 4), ("G", 3, 3, 1), ("sO", 3, 3, 1), ("aI", 1, 0, 0), ("aY", 1, 0, 0),
    ("G", 2, 0, 6), ("aO", 1, 3, 4), ("sI", 2, 0, 6), ("G", 3, 3, 3), ("sY", 3, 3, 2), ("aO", 3, 2, 2),
    ("G", 2, 0, 4), ("sI", 2, 0, 4), ("aO", 1, 1, 4), ("aY", 1, 1, 4), ("aI", 3, 2, 2), ("aO", 0, 1, 2),
    ("aY", 0, 1, 2), ("aI", 1, 3, 0), ("aO", 1, 0, 6), ("aY", 1, 0, 6), ("G", 2, 0, 0), ("N", 3, 3, 0),
    ("n", 3, 3, 0), ("aI", 1, 1, 0), ("sO", 2, 0, 0), ("aY", 1, 3, 0), ("N", 2, 0, 0), ("n", 2, 0, 0),
    ("aI", 3, 2, 0), ("aO", 3, 2, 4), ("aY", 1, 1, 0), ("aI", 0, 1, 2), ("U", 3, 3, 0), ("aY", 1, 3, 6),
    ("aO", 1, 3, 6), ("aI", 0, 1, 0), ("U", 2, 0, 0), ("aO", 3, 3, 2), ("aY", 1, 1, 6), ("aI", 3, 3, 2),
    ("aO", 1, 1, 6), ("aY", 3, 2, 6), ("aI", 2, 0, 2), ("aO", 3, 2, 6), ("aY", 3, 2, 4), ("aO", 0, 1, 4),
    ("aY", 3, 2, 0), ("aI", 3, 3, 0), ("aO", 0, 1, 6), ("aY", 0, 1, 6), ("aO", 3, 3, 4), ("aY", 0, 1, 4),
    ("aI", 2, 0, 0), ("aO", 3, 3, 6), ("aY", 0, 1, 0), ("aO", 2, 0, 4), ("aY", 3, 3, 2), ("aI", 3, 3, 1),
    ("aO", 2, 0, 2), ("aY", 2, 0, 4), ("aO", 2, 0, 6), ("aY", 2, 0, 6), ("aO", 3, 3, 7), ("aY", 2, 0, 2),
    ("aI", 3, 3, 3), ("aO", 3, 3, 3), ("aY", 2, 0, 0), ("aO", 3, 3, 5),
)


def lanes_of(shapes, g, ref, i):
    n = len(GROUPS[g].members)
    w = shapes[g][1] // n
    return ref if n == 1 else ref.at[..., i * w : (i + 1) * w]


def finish(shapes, *refs):
    n = len(GROUPS)
    full, own, st = refs[0:n], refs[n : 2 * n], refs[2 * n : 3 * n]
    vectors = refs[3 * n : 3 * n + 6]
    halves, nexts, news = (refs[3 * n + 6 + 8 * k : 3 * n + 14 + 8 * k] for k in range(3))
    sem, vec_sem = refs[3 * n + 30 :]
    for g, group in enumerate(GROUPS):
        w = shapes[g][1]
        for i, a in enumerate(group.members):
            if group.rows:
                pltpu.make_async_copy(lanes_of(shapes, g, full[g], i), halves[a], sem.at[0, g]).start()
            else:
                for b in range(8):
                    dst = halves[a].at[:, b * w : (b + 1) * w]
                    pltpu.make_async_copy(full[g].at[b], dst, sem.at[0, g]).start()
            pltpu.make_async_copy(lanes_of(shapes, g, own[g], i), nexts[a], sem.at[1, g]).start()
            pltpu.make_async_copy(lanes_of(shapes, g, st[g], i), news[a], sem.at[2, g]).start()
    copies = []
    for i, dst in enumerate((*halves[6:], *nexts[6:], *news[6:])):
        copies.append(pltpu.make_async_copy(vectors[i], dst, vec_sem.at[i]))
        copies[-1].start()
    for g in range(n):
        for k, ref in enumerate((full[g], own[g], st[g])):
            pltpu.make_async_copy(ref, ref, sem.at[k, g]).wait()
    for c in copies:
        c.wait()


def kernel(replicas, models, limit, shapes, *refs):
    slopes, slope_norm, slope_bias = refs[0:6], refs[6], refs[7]
    params, param_norm, param_bias = refs[8:14], refs[14], refs[15]
    states, state_norm, state_bias = refs[16:22], refs[22], refs[23]
    groups = range(len(GROUPS))
    n = len(GROUPS)
    full, own, st = refs[24 : 24 + n], refs[24 + n : 24 + 2 * n], refs[24 + 2 * n : 24 + 3 * n]
    half_norm, half_bias, next_norm, next_bias, new_norm, new_bias = refs[24 + 3 * n : 30 + 3 * n]
    scratch = list(refs[30 + 3 * n :])
    take = lambda: [scratch.pop(0) for _ in groups]
    xin, enc, rec, sq, sqr = (take() for _ in range(5))
    vs, vown, vrec, vnext, vag, vh_norm, vh_bias = (scratch.pop(0) for _ in range(7))
    rs_s, rs_r, ag_s, ag_r, n_s, n_r, v_s, v_r, w_s, w_r = (scratch.pop(0) for _ in range(10))
    load_sem, own_sem, st_sem, vown_sem = scratch

    r = lax.axis_index("replica")
    m = lax.axis_index("model")
    y, z = lax.rem(r, 2), r // 2
    side = z // 2
    slab = [(p + side * (3 - 2 * p)) * 2 + (y if d == 0 else 1 - y) for p in range(4) for d in (0, 1)]

    scale = 2.0**13 / (limit * replicas)
    rate = replicas ** (-0.5)

    def encode(x):
        t = x * scale
        t2 = t * t
        t4 = t2 * t2
        return (t4 * t4 * t).astype(jnp.bfloat16)

    def decode(c):
        f = c.astype(jnp.float32)
        a = jnp.exp(jnp.log(jnp.abs(f)) * (1.0 / root)) * (1.0 / scale)
        return jnp.where(f < 0, -a, a)

    lanes = functools.partial(lanes_of, shapes)
    at = {k: i for i, k in enumerate(CHUNKS)}
    height = lambda g: shapes[g][0] // len(KINDS[g])
    rows = lambda g, c: pl.ds(c * height(g), height(g))

    def source(g, c, s):
        w = shapes[g][1]
        if GROUPS[g].rows:
            return xin[g].at[slab[s], rows(g, c)]
        return xin[g].at[rows(g, c), pl.ds(pl.multiple_of(slab[s] * w, w), w)]

    def loop(g, body):
        h, w = height(g), shapes[g][1]
        step = min(h, max(16, STEP // w // 16 * 16))
        while h % step:
            step -= 16
        lax.fori_loop(0, h // step, lambda i, c: (body(pl.ds(pl.multiple_of(i * step, step), step)), c)[1], 0)

    def remote(src, dst, s, d, peer, axis="replica"):
        return pltpu.make_async_remote_copy(
            src_ref=src, dst_ref=dst, send_sem=s, recv_sem=d, device_id={axis: peer}, device_id_type=MESH
        )

    def whole(ref, sem):
        pltpu.make_async_copy(ref, ref, sem).wait()

    barrier = pltpu.get_barrier_semaphore()
    for j in range(1, replicas):
        pl.semaphore_signal(barrier, inc=1, device_id={"replica": lax.rem(r + j, replicas)}, device_id_type=MESH)
    for j in range(1, models):
        pl.semaphore_signal(barrier, inc=1, device_id={"model": lax.rem(m + j, models)}, device_id_type=MESH)

    def chunk_of(g, c):
        return xin[g].at[:, rows(g, c)] if GROUPS[g].rows else xin[g].at[rows(g, c)]

    for g, c in CHUNKS:
        for i, a in enumerate(GROUPS[g].members):
            src = slopes[a].at[:, rows(g, c)] if GROUPS[g].rows else slopes[a].at[rows(g, c)]
            pltpu.make_async_copy(src, lanes(g, chunk_of(g, c), i), load_sem.at[at[g, c]]).start()
    for g in OWN:
        for i, a in enumerate(GROUPS[g].members):
            pltpu.make_async_copy(params[a], lanes(g, own[g], i), own_sem.at[g]).start()
            pltpu.make_async_copy(states[a], lanes(g, st[g], i), st_sem.at[g]).start()

    vs[0:1, :] = slope_norm[...]
    vs[1:2, :] = slope_bias[...]
    for g in groups:
        if not GROUPS[g].rows:
            sq[g][...] = jnp.zeros_like(sq[g])

    def rule(p, s, v):
        s = hold_rate * s + (1.0 - hold_rate) * v * v
        return p - learn_rate * v * lax.rsqrt(s + 1e-06), s

    def fold(x):
        total = x[:, 0:128]
        for k in range(128, x.shape[1], 128):
            total = total + x[:, k : k + 128]
        return jnp.sum(total, axis=1, keepdims=True)

    width = vs.shape[1] // replicas

    def vec_out(j):
        to = lax.rem(r + j, replicas)
        return remote(
            vs.at[:, pl.ds(pl.multiple_of(to * width, width), width)],
            vrec.at[j - 1], v_s.at[j - 1], v_r.at[j - 1], to,
        )

    def vec_back(j):
        return remote(vnext, vag.at[j - 1], w_s.at[j - 1], w_r.at[j - 1], lax.rem(r + j, replicas))

    def vec_start():
        pltpu.make_async_copy(vs.at[:, pl.ds(pl.multiple_of(r * width, width), width)], vown, vown_sem).start()
        for j in range(1, replicas):
            vec_out(j).start()

    def vec_update():
        pltpu.make_async_copy(vown, vown, vown_sem).wait()
        total = vown[...]
        for j in range(1, replicas):
            vec_out(j).wait_recv()
            total = total + vrec[j - 1]
        v = total * rate
        p, s = rule(param_norm[...], state_norm[...], v[0:1, :])
        next_norm[...] = p
        new_norm[...] = s
        vnext[0:1, :] = p
        p, s = rule(param_bias[...], state_bias[...], v[1:2, :])
        next_bias[...] = p
        new_bias[...] = s
        vnext[1:2, :] = p
        for j in range(1, replicas):
            vec_back(j).start()

    def vec_finish():
        vh_norm[pl.ds(r, 1), :] = vnext[0:1, :]
        vh_bias[pl.ds(r, 1), :] = vnext[1:2, :]
        for j in range(1, replicas):
            vec_back(j).wait_recv()
            at = lax.rem(r + replicas - j, replicas)
            vh_norm[pl.ds(at, 1), :] = vag[j - 1, 0:1, :]
            vh_bias[pl.ds(at, 1), :] = vag[j - 1, 1:2, :]
        half_norm[...] = vh_norm[...].astype(jnp.bfloat16)
        half_bias[...] = vh_bias[...].astype(jnp.bfloat16)

    def run(mid, order):
        mine = 1 if mid else 0
        peers = {"Y": z * 2 + (1 - y), "n": None}
        if mid:
            peers["sO"] = peers["aO"] = side * 6 + y
            peers["sI"] = peers["aI"] = (3 - z) * 2 + y
        else:
            peers["sI"] = peers["aI"] = (1 + side) * 2 + y
        peers["sY"] = peers["aY"] = z * 2 + (1 - y)
        done = set()

        def kind(g, c):
            return KINDS[g][c]

        def landing(g, c, by, s):
            if kind(g, c) == "A":
                return {"Y": 0, "O": 3, "I": 7}[by] + s // 2
            return {"Y": 10, "O": s - 2, "I": 6 + s}[by]

        def outgoing(g, c, op, s):
            p = s // 2
            if kind(g, c) == "A":
                if op == "sY":
                    return p
                return 3 + p if p else 4
            if op == "sY":
                return 6
            if not mid:
                return s - 2
            return s - 4 if p >= 2 else 4 + s

        def across(op, s):
            return (3 - s // 2) * 2 + s % 2 if mid and op[1] == "I" else s

        def send(op, g, c, s):
            by = {"sY": "Y", "sO": "I", "sI": "I" if mid else "O"}[op]
            slot = landing(g, c, by, across(op, s))
            return remote(
                enc[g].at[outgoing(g, c, op, s), rows(g, c)],
                rec[g].at[slot, rows(g, c)],
                rs_s.at[g],
                rs_r.at[at[g, c], slot],
                peers[op],
            )

        def gather(op, g, c, s):
            to = s + 1 if op == "aY" else across(op, s)
            ref = full[g].at[slab[s], rows(g, c)]
            link = {"aY": 0, "aI": 1, "aO": 2}[op]
            return remote(ref, ref, ag_s.at[at[g, c], link], ag_r.at[at[g, c], to], peers[op])

        def got(g, c, s):
            if s != mine * 2 and (g, c, s) not in done:
                done.add((g, c, s))
                ref = full[g].at[slab[s], rows(g, c)]
                whole(ref, ag_r.at[at[g, c], s])

        def arrived(g, c, by, s):
            slot = landing(g, c, by, s)
            ref = rec[g].at[slot, rows(g, c)]
            whole(ref, rs_r.at[at[g, c], slot])
            return ref

        def once(key, ref, sem):
            if key not in done:
                done.add(key)
                whole(ref, sem)

        def loaded(g, c):
            once(("load", g, c), chunk_of(g, c), load_sem.at[at[g, c]])

        def parts(g, c, s):
            loaded(g, c)
            by = []
            a, p = kind(g, c) == "A", s // 2
            if a or s == mine * 2:
                by.append("Y")
            if mid and p >= 1:
                by.append("O")
            if p == mine or (mid and p == 0):
                by.append("I")
            return [arrived(g, c, b, s) for b in by]

        def encode_op(g, c, s, op):
            loaded(g, c)
            src, dst = source(g, c, s), enc[g].at[outgoing(g, c, op, s), rows(g, c)]

            def body(d):
                dst[d, :] = encode(src[d, :])

            loop(g, body)

        def add_op(g, c, s):
            src = source(g, c, s)
            op = "sY" if s // 2 == mine else "sO" if mid and s < 2 else "sI"
            dst = enc[g].at[outgoing(g, c, op, s), rows(g, c)]
            got = parts(g, c, s)

            def body(d):
                total = src[d, :]
                for ref in got:
                    total = total + decode(ref[d, :])
                dst[d, :] = encode(total)

            loop(g, body)

        def mean_op(g, c):
            acc = source(g, c, mine * 2)
            got = parts(g, c, mine * 2)
            once(("own", g), own[g], own_sem.at[g])
            held = own[g].at[rows(g, c)]
            k = len(GROUPS[g].members)
            w = shapes[g][1] // k

            def mean(d):
                total = acc[d, :]
                for ref in got:
                    total = total + decode(ref[d, :])
                v = total * rate
                acc[d, :] = v
                return v

            if GROUPS[g].rows:
                sums = sq[g].at[rows(g, c)]

                def body(d):
                    v, p = mean(d), held[d, :]
                    v, p = v * v, p * p
                    lane = lax.broadcasted_iota(jnp.int32, (v.shape[0], 128), 1)
                    out = jnp.zeros((v.shape[0], 128), jnp.float32)
                    for i in range(k):
                        cols = slice(i * w, (i + 1) * w)
                        out = jnp.where(lane == 2 * i, fold(p[:, cols]), out)
                        out = jnp.where(lane == 2 * i + 1, fold(v[:, cols]), out)
                    sums[d, :] = out

            else:

                def body(d):
                    v, p = mean(d), held[d, :]
                    sq[g][0] += jnp.sum((p * p).reshape(-1, 8, w), axis=0)
                    sq[g][1] += jnp.sum((v * v).reshape(-1, 8, w), axis=0)

            loop(g, body)

        def norms(g, c, j):
            if GROUPS[g].rows:
                src, dst = sq[g].at[rows(g, c)], sqr[g].at[j - 1, rows(g, c)]
            else:
                src, dst = sq[g], sqr[g].at[j - 1]
            return remote(src, dst, n_s.at[at[g, c], j - 1], n_r.at[at[g, c], j - 1], lax.rem(m + j, models), "model")

        def update_op(g, c):
            first = c if GROUPS[g].rows else 0
            for j in range(1, models):
                if ("norm", g, first, j) not in done:
                    done.add(("norm", g, first, j))
                    norms(g, first, j).wait_recv()
            once(("st", g), st[g], st_sem.at[g])
            acc, half = source(g, c, mine * 2), full[g].at[slab[mine * 2], rows(g, c)]
            held, hold = own[g].at[rows(g, c)], st[g].at[rows(g, c)]
            k = len(GROUPS[g].members)
            w = shapes[g][1] // k

            def put(d, cols, t):
                p, s = rule(held[d, cols], hold[d, cols], acc[d, cols] * t)
                held[d, cols] = p
                hold[d, cols] = s
                half[d, cols] = p.astype(jnp.bfloat16)

            if GROUPS[g].rows:
                sums = [sq[g].at[rows(g, c)]] + [sqr[g].at[j, rows(g, c)] for j in range(models - 1)]

                def body(d):
                    total = sums[0][d, :]
                    for ref in sums[1:]:
                        total = total + ref[d, :]
                    lane = lax.broadcasted_iota(jnp.int32, total.shape, 1)
                    pick = lambda i: jnp.sum(jnp.where(lane == i, total, 0.0), axis=1, keepdims=True)
                    for i in range(k):
                        t = jnp.sqrt(pick(2 * i)) * lax.rsqrt(pick(2 * i + 1) + 1e-06)
                        put(d, slice(i * w, (i + 1) * w), t)

            else:
                total = sq[g][...]
                for j in range(models - 1):
                    total = total + sqr[g][j]
                total = jnp.sum(total, axis=1, keepdims=True)
                t = jnp.sqrt(total[0]) * lax.rsqrt(total[1] + 1e-06)

                def body(d):
                    put(d, slice(None), t)

            loop(g, body)

        met = False
        for op, g, c, s in order:
            if op not in ("E", "G") and not met:
                met = True
                pl.semaphore_wait(barrier, replicas + models - 2)
            if op == "E":
                encode_op(g, c, s, "sY" if kind(g, c) == "A" else "sI")
            elif op == "G":
                add_op(g, c, s)
            elif op in ("sY", "sI", "sO"):
                send(op, g, c, s).start()
            elif op == "N":
                mean_op(g, c)
            elif op == "n":
                for j in range(1, models):
                    norms(g, c, j).start()
            elif op == "U":
                update_op(g, c)
            elif op == "V":
                (vec_start, vec_update, vec_finish)[s]()
            else:
                got(g, c, s)
                gather(op, g, c, s).start()

        for g, c in CHUNKS:
            for s in range(8):
                got(g, c, s)
        for g in groups:
            whole(enc[g], rs_s.at[g])
        for g, c in CHUNKS:
            for link, count in enumerate(SENT[mid][kind(g, c)]):
                if count:
                    whole(full[g].at[pl.ds(0, count), rows(g, c)], ag_s.at[at[g, c], link])
            if GROUPS[g].rows or c == 0:
                for j in range(1, models):
                    norms(g, c, j).wait_send()
        for j in range(1, replicas):
            vec_out(j).wait_send()
            vec_back(j).wait_send()

    end = jnp.logical_or(z == 0, z == 3)

    @pl.when(end)
    def _():
        run(False, END)

    @pl.when(jnp.logical_not(end))
    def _():
        run(True, MID)


def fused(replicas, models, shapes, *args):
    slopes, params = args[0:6], args[8:14]
    f32, bf16 = jnp.float32, jnp.bfloat16
    vec = args[6].shape[1]
    width = vec // replicas
    row = lambda a: a.reshape(1, -1)
    by_rows = [a in g.members and g.rows for a in range(6) for g in GROUPS if a in g.members]
    cut = lambda a, rows: a.reshape(replicas, -1, a.shape[-1]) if rows else a[0]
    args = (
        *(cut(a, rows) for a, rows in zip(slopes, by_rows)), *args[6:14],
        row(args[14]), row(args[15]), *args[16:22], row(args[22]), row(args[23]),
    )
    S = jax.ShapeDtypeStruct
    n, chunks = len(GROUPS), len(CHUNKS)
    held = [((replicas, *s), bf16) for s in shapes] + [(s, f32) for s in shapes] * 2
    held += [((replicas, width), bf16)] * 2 + [((1, width), f32)] * 4
    ANY, VM = pl.BlockSpec(memory_space=pl.ANY), pl.BlockSpec(memory_space=pltpu.VMEM)
    part = [ANY] * 6 + [VM] * 2
    scratch = [
        pltpu.VMEM((replicas, *s) if g.rows else (s[0], s[1] * replicas), f32) for g, s in zip(GROUPS, shapes)
    ]
    scratch += [pltpu.VMEM((7, *s), bf16) for s in shapes]
    scratch += [pltpu.VMEM((11 if "B" in k else 9, *s), bf16) for k, s in zip(KINDS, shapes)]
    sq = [(s[0], 128) if g.rows else (2, 8, s[1]) for g, s in zip(GROUPS, shapes)]
    scratch += [pltpu.VMEM(s, f32) for s in sq]
    scratch += [pltpu.VMEM((models - 1, *s), f32) for s in sq]
    scratch += [
        pltpu.VMEM((2, vec), f32),
        pltpu.VMEM((2, width), f32),
        pltpu.VMEM((replicas - 1, 2, width), f32),
        pltpu.VMEM((2, width), f32),
        pltpu.VMEM((replicas - 1, 2, width), f32),
        pltpu.VMEM((replicas, width), f32),
        pltpu.VMEM((replicas, width), f32),
    ]
    dma = pltpu.SemaphoreType.DMA
    scratch += [dma((n,)), dma((chunks, 11)), dma((chunks, 3)), dma((chunks, 8))]
    scratch += [dma((chunks, models - 1))] * 2 + [dma((replicas - 1,))] * 4
    scratch += [dma((chunks,))] + [dma((n,))] * 2 + [dma(())]
    out = pl.pallas_call(
        functools.partial(kernel, replicas, models, 4.0, shapes),
        out_shape=[pltpu.VMEM(*h) for h in held],
        in_specs=part * 3,
        out_specs=[VM] * len(held),
        scratch_shapes=scratch,
        compiler_params=pltpu.CompilerParams(
            collective_id=0, has_side_effects=True, vmem_limit_bytes=54 * 1024 * 1024
        ),
    )(*args)
    outs = [
        S((replicas, a.shape[1] // replicas, a.shape[2]) if rows else a.shape[1:], bf16)
        for a, rows in zip(slopes, by_rows)
    ]
    outs += [S((replicas, width), bf16)] * 2
    for _ in range(2):
        outs += [S(a.shape, f32) for a in params] + [S((1, width), f32)] * 2
    out = pl.pallas_call(
        functools.partial(finish, shapes),
        out_shape=outs,
        in_specs=[VM] * len(held),
        out_specs=[ANY] * len(outs),
        scratch_shapes=[dma((3, n)), dma((6,))],
        compiler_params=pltpu.CompilerParams(vmem_limit_bytes=1024 * 1024),
    )(*out)
    flat = lambda a: a.reshape(-1)
    return (
        *(a.reshape(-1, a.shape[-1]) for a in out[0:6]), flat(out[6]), flat(out[7]),
        *out[8:14], flat(out[14]), flat(out[15]),
        *out[16:22], flat(out[22]), flat(out[23]),
    )


def plain(
    slope_up,
    slope_down,
    slope_query,
    slope_key,
    slope_value,
    slope_mixed,
    slope_norm,
    slope_bias,
    param_up,
    param_down,
    param_query,
    param_key,
    param_value,
    param_mixed,
    param_norm,
    param_bias,
    state_up,
    state_down,
    state_query,
    state_key,
    state_value,
    state_mixed,
    state_norm,
    state_bias,
):
    mean_up, mean_down, mean_query, mean_key, mean_value, mean_mixed = (
        lax.psum_scatter(slope_up[0], "replica", scatter_dimension=0, tiled=True),
        lax.psum_scatter(slope_down[0], "replica", scatter_dimension=1, tiled=True),
        lax.psum_scatter(slope_query[0], "replica", scatter_dimension=0, tiled=True),
        lax.psum_scatter(slope_key[0], "replica", scatter_dimension=0, tiled=True),
        lax.psum_scatter(slope_value[0], "replica", scatter_dimension=0, tiled=True),
        lax.psum_scatter(slope_mixed[0], "replica", scatter_dimension=1, tiled=True),
    )
    whole_norm, whole_bias = lax.psum((slope_norm[0], slope_bias[0]), "replica")
    place = lax.axis_index("replica")
    mean_norm = lax.dynamic_slice_in_dim(
        whole_norm, place * param_norm.shape[0], param_norm.shape[0]
    )
    mean_bias = lax.dynamic_slice_in_dim(
        whole_bias, place * param_bias.shape[0], param_bias.shape[0]
    )
    mean_rate = lax.axis_size("replica") ** (-0.5)
    mean_up = mean_up * mean_rate
    mean_down = mean_down * mean_rate
    mean_query = mean_query * mean_rate
    mean_key = mean_key * mean_rate
    mean_value = mean_value * mean_rate
    mean_mixed = mean_mixed * mean_rate
    mean_norm = mean_norm * mean_rate
    mean_bias = mean_bias * mean_rate
    (
        own_up,
        own_down,
        own_query,
        own_key,
        own_value,
        own_mixed,
        slope_up_norm,
        slope_down_norm,
        slope_query_norm,
        slope_key_norm,
        slope_value_norm,
        slope_mixed_norm,
    ) = lax.psum(
        (
            jnp.sum(param_up * param_up, axis=1, keepdims=True),
            jnp.sum(param_down * param_down, axis=0, keepdims=True),
            jnp.sum(param_query * param_query, axis=1, keepdims=True),
            jnp.sum(param_key * param_key, axis=1, keepdims=True),
            jnp.sum(param_value * param_value, axis=1, keepdims=True),
            jnp.sum(param_mixed * param_mixed, axis=0, keepdims=True),
            jnp.sum(mean_up * mean_up, axis=1, keepdims=True),
            jnp.sum(mean_down * mean_down, axis=0, keepdims=True),
            jnp.sum(mean_query * mean_query, axis=1, keepdims=True),
            jnp.sum(mean_key * mean_key, axis=1, keepdims=True),
            jnp.sum(mean_value * mean_value, axis=1, keepdims=True),
            jnp.sum(mean_mixed * mean_mixed, axis=0, keepdims=True),
        ),
        "model",
    )
    mean_up = mean_up * (jnp.sqrt(own_up) * lax.rsqrt(slope_up_norm + 1e-06))
    mean_down = mean_down * (jnp.sqrt(own_down) * lax.rsqrt(slope_down_norm + 1e-06))
    mean_query = mean_query * (jnp.sqrt(own_query) * lax.rsqrt(slope_query_norm + 1e-06))
    mean_key = mean_key * (jnp.sqrt(own_key) * lax.rsqrt(slope_key_norm + 1e-06))
    mean_value = mean_value * (jnp.sqrt(own_value) * lax.rsqrt(slope_value_norm + 1e-06))
    mean_mixed = mean_mixed * (jnp.sqrt(own_mixed) * lax.rsqrt(slope_mixed_norm + 1e-06))
    state_new_up = hold_rate * state_up + (1.0 - hold_rate) * mean_up * mean_up
    next_up = param_up - learn_rate * mean_up * lax.rsqrt(state_new_up + 1e-06)
    state_new_down = hold_rate * state_down + (1.0 - hold_rate) * mean_down * mean_down
    next_down = param_down - learn_rate * mean_down * lax.rsqrt(state_new_down + 1e-06)
    state_new_query = hold_rate * state_query + (1.0 - hold_rate) * mean_query * mean_query
    next_query = param_query - learn_rate * mean_query * lax.rsqrt(state_new_query + 1e-06)
    state_new_key = hold_rate * state_key + (1.0 - hold_rate) * mean_key * mean_key
    next_key = param_key - learn_rate * mean_key * lax.rsqrt(state_new_key + 1e-06)
    state_new_value = hold_rate * state_value + (1.0 - hold_rate) * mean_value * mean_value
    next_value = param_value - learn_rate * mean_value * lax.rsqrt(state_new_value + 1e-06)
    state_new_mixed = hold_rate * state_mixed + (1.0 - hold_rate) * mean_mixed * mean_mixed
    next_mixed = param_mixed - learn_rate * mean_mixed * lax.rsqrt(state_new_mixed + 1e-06)
    state_new_norm = hold_rate * state_norm + (1.0 - hold_rate) * mean_norm * mean_norm
    next_norm = param_norm - learn_rate * mean_norm * lax.rsqrt(state_new_norm + 1e-06)
    state_new_bias = hold_rate * state_bias + (1.0 - hold_rate) * mean_bias * mean_bias
    next_bias = param_bias - learn_rate * mean_bias * lax.rsqrt(state_new_bias + 1e-06)
    half_up, half_down, half_query, half_key, half_value, half_mixed, half_norm, half_bias = (
        lax.all_gather(next_up.astype(jnp.bfloat16), "replica", axis=0, tiled=True),
        lax.all_gather(next_down.astype(jnp.bfloat16), "replica", axis=1, tiled=True),
        lax.all_gather(next_query.astype(jnp.bfloat16), "replica", axis=0, tiled=True),
        lax.all_gather(next_key.astype(jnp.bfloat16), "replica", axis=0, tiled=True),
        lax.all_gather(next_value.astype(jnp.bfloat16), "replica", axis=0, tiled=True),
        lax.all_gather(next_mixed.astype(jnp.bfloat16), "replica", axis=1, tiled=True),
        lax.all_gather(next_norm.astype(jnp.bfloat16), "replica", axis=0, tiled=True),
        lax.all_gather(next_bias.astype(jnp.bfloat16), "replica", axis=0, tiled=True),
    )
    return (
        half_up,
        half_down,
        half_query,
        half_key,
        half_value,
        half_mixed,
        half_norm,
        half_bias,
        next_up,
        next_down,
        next_query,
        next_key,
        next_value,
        next_mixed,
        next_norm,
        next_bias,
        state_new_up,
        state_new_down,
        state_new_query,
        state_new_key,
        state_new_value,
        state_new_mixed,
        state_new_norm,
        state_new_bias,
    )


def solution(mesh):
    replicas, models = mesh.shape["replica"], mesh.shape["model"]

    def local(*args):
        if replicas != 2**3 or any(a.shape[k] % 128 for a in args[8:14] for k in (0, 1)):
            return plain(*args)
        shapes = []
        for g, kinds in zip(GROUPS, KINDS):
            h, w = args[8 + g.members[0]].shape
            shapes.append((h, w * len(g.members)))
            if h % (16 * len(kinds)) or (w != 128 and not g.rows):
                return plain(*args)
        if args[14].shape[0] % 128:
            return plain(*args)
        return fused(replicas, models, shapes, *args)

    placed = (
        P("replica", None, "model"),
        P("replica", "model", None),
        P("replica", None, "model"),
        P("replica", None, "model"),
        P("replica", None, "model"),
        P("replica", "model", None),
        P("replica", None),
        P("replica", None),
        P("replica", "model"),
        P("model", "replica"),
        P("replica", "model"),
        P("replica", "model"),
        P("replica", "model"),
        P("model", "replica"),
        P("replica"),
        P("replica"),
        P("replica", "model"),
        P("model", "replica"),
        P("replica", "model"),
        P("replica", "model"),
        P("replica", "model"),
        P("model", "replica"),
        P("replica"),
        P("replica"),
    )
    return jax.shard_map(
        local,
        mesh=mesh,
        in_specs=placed,
        out_specs=(
            P(None, "model"),
            P("model", None),
            P(None, "model"),
            P(None, "model"),
            P(None, "model"),
            P("model", None),
            P(),
            P(),
            P("replica", "model"),
            P("model", "replica"),
            P("replica", "model"),
            P("replica", "model"),
            P("replica", "model"),
            P("model", "replica"),
            P("replica"),
            P("replica"),
            P("replica", "model"),
            P("model", "replica"),
            P("replica", "model"),
            P("replica", "model"),
            P("replica", "model"),
            P("model", "replica"),
            P("replica"),
            P("replica"),
        ),
        check_vma=False,
    )
```

time: 138 us -> 124 us (0.90)
  Pallas kernels: 138 us -> 123 us
    pallas_call x1, Pallas kernels: 134 us -> 120 us  [fused(): pl.pallas_call(functools.partial(kernel, replicas, models, 4.0, shapes),...]
where the time goes in v1:
time: 124 us
  Pallas kernels  123 us (99%)
    pallas_call x1, Pallas kernels, fused(): pl.pallas_call(functools.partial(kernel, replicas, models, 4.0, shapes),...  120 us
    pallas_call x1, Pallas kernels, fused(): pl.pallas_call(functools.partial(finish, shapes), out_shape=outs, in_spec...  3.78 us

profile of v1, /device:TPU:0, one launch (start us, length us, event | category | flops | bytes accessed | tf_op | source)
XLA Modules:
  0.0 124.3 jit_solution(8821058761232095841)
XLA Ops:
  0.7 119.7 %shard_map.415 = (bf16[8,128,1024]{2,1,0:T(8,128)(2,1)S(1)}, bf16[8,1024,128]{2,1,0:T(8,128)(2,1)S(1)}, bf16[8,256,128]{2,1,0:T(8,128)(2,1)S(1)}, bf16[8,128,768...) custom-call(f32[8,128,1024]{2,1,0:T(8,128)} %bitcast.20, ...), custom_call_target="tpu_custom_call" | custom-call | tf_op jit(solution)/shard_map/pallas_call | solution.py:599
  120.4 3.8 %shard_map.416 = (bf16[8,128,1024]{2,1,0:T(8,128)(2,1)}, bf16[1024,1024]{1,0:T(8,128)(2,1)}, bf16[8,128,256]{2,1,0:T(8,128)(2,1)}, bf16[8,128,256]{2,1,0:T(8,128...) custom-call(bf16[8,128,1024]{2,1,0:T(8,128)(2,1)S(1)} %get-tuple-ele, ...), custom_call_target="tpu_custom_call" | custom-call | tf_op jit(solution)/shard_map/pallas_call | solution.py:616

commit v2 on v1

--- a/solution.py
+++ b/solution.py
@@ -20,119 +20,116 @@
 
 
 GROUPS = (Group((0,), True), Group((1,), False), Group((5,), False), Group((2, 3, 4), True))
-KINDS = (("A", "A", "B", "B"), ("A", "A", "A", "A"), ("A",), ("A", "B", "A", "B"))
-CHUNKS = ((0, 0), (0, 2), (0, 3), (3, 1), (1, 2), (3, 0), (1, 0), (1, 3), (1, 1), (3, 2), (0, 1), (3, 3), (2, 0))
-OWN = (0, 3, 1, 2)
-SENT = ({"A": (4, 1, 0), "B": (1, 2, 0)}, {"A": (4, 2, 3), "B": (1, 4, 6)})
+A, B = 0, 1
+E, G, N, X, U, V, SY, SI, SO, AY, AI, AO = range(12)
+SIZES = ((2, 2, 2, 2), (4, 4), (8,), (1, 2, 2, 2, 1))
+SUMS = ((B, A, B, A), (A, A), (A,), (A, A, A, B, B))
+BACK = ((A, B, A, B), (A, A), (B,), (B, B, A, A, B))
+CHUNKS = ((3, 0), (3, 4), (0, 3), (0, 1), (2, 0), (3, 3), (1, 0), (1, 1), (3, 2), (0, 0), (0, 2), (3, 1))
+OWN = (3, 0, 2, 1)
+SENT = (((4, 1, 0), (1, 2, 0)), ((4, 2, 3), (1, 4, 6)))
 STEP = 16384
 END = (
-    ("E", 0, 0, 7), ("sY", 0, 0, 6), ("E", 0, 0, 5), ("sY", 0, 0, 4), ("E", 0, 0, 3), ("E", 0, 2, 6),
-    ("sI", 0, 2, 6), ("E", 0, 2, 7), ("sI", 0, 2, 7), ("E", 0, 2, 4), ("E", 0, 2, 5), ("E", 0, 2, 2),
-    ("E", 0, 2, 3), ("E", 0, 0, 1), ("E", 0, 3, 6), ("E", 0, 3, 7), ("E", 0, 3, 4), ("sY", 0, 0, 2),
-    ("E", 0, 3, 5), ("E", 0, 3, 2), ("E", 0, 3, 3), ("sI", 0, 2, 4), ("E", 3, 1, 6), ("E", 3, 1, 7),
-    ("E", 3, 1, 4), ("E", 3, 1, 5), ("E", 3, 1, 2), ("E", 3, 1, 3), ("E", 1, 2, 7), ("E", 1, 2, 5),
-    ("E", 1, 2, 3), ("sY", 0, 0, 0), ("E", 1, 2, 1), ("V", 0, 0, 0), ("E", 3, 0, 7), ("E", 3, 0, 5),
-    ("sI", 0, 2, 5), ("E", 3, 0, 3), ("E", 3, 0, 1), ("G", 0, 0, 6), ("E", 1, 0, 7), ("E", 1, 0, 5),
-    ("E", 1, 0, 3), ("E", 1, 0, 1), ("E", 1, 3, 7), ("sY", 1, 2, 6), ("E", 1, 3, 5), ("E", 1, 3, 3),
-    ("E", 1, 3, 1), ("sI", 0, 0, 6), ("E", 1, 1, 7), ("E", 1, 1, 5), ("G", 0, 0, 4), ("E", 1, 1, 3),
-    ("E", 1, 1, 1), ("E", 3, 2, 7), ("E", 3, 2, 5), ("E", 3, 2, 3), ("sY", 1, 2, 4), ("E", 3, 2, 1),
-    ("E", 0, 1, 7), ("E", 0, 1, 5), ("E", 0, 1, 3), ("sI", 0, 0, 4), ("E", 0, 1, 1), ("G", 0, 0, 2),
-    ("E", 3, 3, 6), ("E", 3, 3, 7), ("E", 3, 3, 4), ("E", 3, 3, 5), ("E", 3, 3, 2), ("E", 3, 3, 3),
-    ("sY", 1, 2, 2), ("E", 2, 0, 7), ("E", 2, 0, 5), ("E", 2, 0, 3), ("sI", 0, 0, 2), ("E", 2, 0, 1),
-    ("sY", 1, 2, 0), ("sI", 0, 2, 2), ("G", 1, 2, 6), ("sY", 3, 0, 6), ("sI", 0, 2, 3), ("G", 1, 2, 4),
-    ("sY", 3, 0, 4), ("sI", 0, 3, 6), ("G", 1, 2, 2), ("sY", 3, 0, 2), ("G", 0, 2, 1), ("sI", 0, 3, 7),
-    ("sY", 0, 2, 0), ("G", 3, 0, 6), ("sY", 3, 0, 0), ("sI", 0, 3, 4), ("G", 3, 0, 4), ("sY", 1, 0, 6),
-    ("sI", 0, 3, 5), ("G", 3, 0, 2), ("N", 0, 0, 0), ("n", 0, 0, 0), ("sY", 1, 0, 4), ("sI", 0, 3, 2),
-    ("N", 0, 2, 0), ("n", 0, 2, 0), ("sY", 1, 0, 2), ("sI", 0, 3, 3), ("sY", 1, 0, 0), ("sI", 3, 1, 6),
-    ("G", 1, 0, 6), ("U", 0, 0, 0), ("aY", 0, 0, 0), ("U", 0, 2, 0), ("sI", 3, 1, 7), ("G", 1, 0, 4),
-    ("aY", 0, 0, 2), ("sI", 3, 1, 4), ("G", 1, 0, 2), ("sI", 3, 1, 5), ("aY", 0, 2, 0), ("sI", 3, 1, 2),
-    ("G", 0, 3, 1), ("sY", 0, 3, 0), ("sI", 3, 1, 3), ("aY", 0, 0, 4), ("aI", 0, 0, 0), ("V", 0, 0, 1),
-    ("aI", 0, 2, 0), ("sY", 1, 3, 6), ("aI", 0, 2, 1), ("sY", 1, 3, 4), ("N", 0, 3, 0), ("n", 0, 3, 0),
-    ("sI", 1, 2, 6), ("sY", 1, 3, 2), ("sI", 1, 2, 4), ("sY", 1, 3, 0), ("G", 1, 3, 6), ("G", 3, 1, 1),
-    ("sI", 1, 2, 2), ("U", 0, 3, 0), ("sY", 3, 1, 0), ("G", 1, 3, 4), ("aI", 0, 3, 0), ("aY", 0, 3, 0),
-    ("G", 1, 3, 2), ("sY", 1, 1, 6), ("sI", 3, 0, 6), ("sY", 1, 1, 4), ("sI", 3, 0, 4), ("N", 3, 1, 0),
-    ("n", 3, 1, 0), ("sI", 3, 0, 2), ("aY", 0, 0, 6), ("aI", 0, 3, 1), ("sY", 1, 1, 2), ("sI", 1, 0, 6),
-    ("G", 1, 1, 6), ("U", 3, 1, 0), ("sY", 1, 1, 0), ("sI", 1, 0, 4), ("G", 1, 1, 4), ("sY", 3, 2, 6),
-    ("sI", 1, 0, 2), ("sY", 3, 2, 4), ("sI", 1, 3, 6), ("G", 1, 1, 2), ("N", 1, 2, 0), ("sY", 3, 2, 2),
-    ("sI", 1, 3, 4), ("sY", 3, 2, 0), ("G", 3, 2, 6), ("sY", 0, 1, 6), ("sI", 1, 3, 2), ("G", 3, 2, 4),
-    ("sY", 0, 1, 4), ("sI", 1, 1, 6), ("G", 3, 2, 2), ("sY", 0, 1, 2), ("N", 3, 0, 0), ("n", 3, 0, 0),
-    ("sI", 1, 1, 4), ("sY", 0, 1, 0), ("sI", 1, 1, 2), ("G", 0, 1, 6), ("aY", 3, 1, 0), ("aI", 3, 1, 0),
-    ("G", 0, 1, 4), ("U", 3, 0, 0), ("aY", 3, 0, 0), ("sI", 3, 2, 6), ("G", 0, 1, 2), ("sY", 2, 0, 6),
-    ("N", 1, 0, 0), ("sI", 3, 2, 4), ("sY", 2, 0, 4), ("sI", 3, 2, 2), ("aY", 3, 0, 2), ("aI", 3, 1, 1),
-    ("N", 1, 3, 0), ("sI", 0, 1, 6), ("aY", 3, 0, 4), ("G", 2, 0, 6), ("sI", 0, 1, 4), ("sY", 2, 0, 2),
-    ("G", 2, 0, 4), ("sY", 2, 0, 0), ("sI", 0, 1, 2), ("N", 1, 1, 0), ("V", 0, 0, 2), ("n", 1, 0, 0),
-    ("aI", 3, 0, 0), ("sI", 3, 3, 6), ("U", 1, 2, 0), ("aY", 1, 2, 0), ("U", 1, 0, 0), ("aY", 1, 0, 0),
-    ("U", 1, 3, 0), ("U", 1, 1, 0), ("aI", 1, 2, 0), ("G", 2, 0, 2), ("aY", 1, 2, 2), ("sI", 3, 3, 7),
-    ("aY", 1, 0, 2), ("sI", 3, 3, 4), ("N", 3, 2, 0), ("n", 3, 2, 0), ("sI", 3, 3, 5), ("aY", 1, 3, 0),
-    ("sI", 3, 3, 2), ("aY", 1, 1, 0), ("sI", 3, 3, 3), ("aY", 1, 3, 2), ("U", 3, 2, 0), ("aI", 1, 0, 0),
-    ("sI", 2, 0, 6), ("aY", 1, 2, 4), ("sI", 2, 0, 4), ("aY", 1, 0, 4), ("N", 0, 1, 0), ("n", 0, 1, 0),
-    ("sI", 2, 0, 2), ("aY", 3, 2, 0), ("aI", 1, 3, 0), ("aY", 1, 1, 2), ("U", 0, 1, 0), ("aY", 0, 1, 0),
-    ("aI", 1, 1, 0), ("aY", 1, 2, 6), ("aI", 3, 2, 0), ("G", 3, 3, 1), ("sY", 3, 3, 0), ("aI", 0, 1, 0),
-    ("aY", 3, 0, 6), ("aY", 1, 3, 4), ("aY", 3, 2, 2), ("N", 3, 3, 0), ("n", 3, 3, 0), ("aY", 1, 1, 4),
-    ("aY", 0, 1, 2), ("aY", 1, 0, 6), ("N", 2, 0, 0), ("n", 2, 0, 0), ("U", 3, 3, 0), ("aI", 3, 3, 0),
-    ("aY", 3, 3, 0), ("aY", 3, 2, 4), ("U", 2, 0, 0), ("aI", 2, 0, 0), ("aY", 1, 3, 6), ("aY", 2, 0, 0),
-    ("aI", 3, 3, 1), ("aY", 1, 1, 6), ("aY", 3, 2, 6), ("aY", 0, 1, 4), ("aY", 0, 1, 6), ("aY", 2, 0, 4),
-    ("aY", 2, 0, 2), ("aY", 2, 0, 6),
+    (E, 3, 0, 5), (SY, 3, 0, 4), (E, 3, 4, 7), (SI, 3, 4, 7), (E, 3, 4, 4), (SI, 3, 4, 4),
+    (E, 3, 0, 3), (SY, 3, 0, 2), (E, 3, 4, 2), (E, 3, 4, 3), (E, 3, 4, 5), (SI, 3, 4, 5),
+    (E, 3, 0, 7), (SY, 3, 0, 6), (E, 3, 4, 6), (E, 3, 0, 1), (SY, 3, 0, 0), (E, 0, 3, 3),
+    (SI, 3, 4, 6), (E, 0, 3, 5), (E, 0, 3, 1), (E, 0, 3, 7), (SY, 0, 3, 6), (E, 2, 0, 5),
+    (SI, 3, 4, 2), (V, 0, 0, 0), (E, 0, 1, 3), (E, 0, 1, 7), (SY, 0, 1, 6), (E, 2, 0, 3),
+    (SI, 3, 4, 3), (E, 0, 1, 5), (E, 3, 3, 4), (E, 3, 3, 5), (E, 3, 3, 7), (SI, 3, 3, 7),
+    (G, 3, 0, 4), (E, 1, 0, 3), (E, 3, 3, 6), (E, 1, 0, 5), (SI, 3, 0, 4), (G, 3, 0, 2),
+    (SY, 0, 3, 4), (E, 0, 1, 1), (E, 3, 3, 2), (E, 2, 0, 7), (G, 3, 0, 6), (E, 3, 3, 3),
+    (E, 1, 1, 5), (SI, 3, 0, 6), (E, 2, 0, 1), (E, 1, 0, 7), (E, 1, 1, 3), (SI, 3, 3, 6),
+    (SY, 2, 0, 6), (E, 0, 0, 5), (E, 0, 0, 4), (E, 1, 1, 7), (SI, 3, 0, 2), (E, 3, 2, 5),
+    (E, 0, 0, 2), (E, 0, 0, 6), (G, 0, 3, 6), (E, 1, 0, 1), (E, 0, 0, 3), (E, 1, 1, 1),
+    (SI, 0, 3, 6), (SY, 1, 0, 6), (E, 0, 2, 4), (E, 3, 2, 3), (E, 0, 2, 5), (E, 3, 2, 7),
+    (SI, 0, 0, 6), (E, 3, 2, 1), (E, 0, 2, 7), (G, 0, 1, 6), (E, 0, 0, 7), (E, 0, 2, 3),
+    (SY, 0, 3, 2), (E, 0, 2, 6), (E, 0, 2, 2), (E, 3, 1, 5), (E, 3, 1, 7), (E, 3, 1, 3),
+    (SI, 0, 1, 6), (E, 3, 1, 1), (G, 0, 3, 4), (G, 3, 4, 1), (SI, 0, 3, 4), (G, 2, 0, 6),
+    (SY, 3, 4, 0), (SI, 2, 0, 6), (SY, 0, 3, 0), (SY, 0, 1, 4), (SI, 0, 0, 7), (G, 1, 0, 6),
+    (G, 3, 3, 1), (SY, 3, 2, 6), (SI, 1, 0, 6), (G, 0, 3, 2), (N, 3, 0, 0), (X, 3, 0, 0),
+    (N, 3, 4, 0), (X, 3, 4, 0), (SY, 1, 1, 6), (SI, 0, 3, 2), (SY, 0, 1, 0), (G, 0, 1, 4),
+    (U, 3, 0, 0), (U, 3, 4, 0), (AI, 3, 0, 0), (G, 3, 2, 6), (N, 0, 3, 0), (X, 0, 3, 0),
+    (SY, 3, 3, 0), (AI, 3, 4, 0), (SI, 0, 1, 4), (SY, 0, 1, 2), (SI, 0, 2, 6), (G, 1, 1, 6),
+    (SY, 2, 0, 0), (SI, 1, 1, 6), (U, 0, 3, 0), (N, 0, 1, 0), (X, 0, 1, 0), (SY, 2, 0, 4),
+    (SI, 0, 2, 7), (V, 0, 0, 1), (N, 3, 3, 0), (X, 3, 3, 0), (SY, 2, 0, 2), (G, 0, 1, 2),
+    (SY, 1, 0, 4), (SI, 0, 1, 2), (U, 0, 1, 0), (N, 2, 0, 0), (X, 2, 0, 0), (SY, 1, 1, 4),
+    (U, 3, 3, 0), (SI, 3, 2, 6), (G, 0, 0, 1), (G, 2, 0, 4), (AI, 0, 3, 0), (G, 2, 0, 2),
+    (SY, 1, 0, 2), (SI, 3, 3, 5), (U, 2, 0, 0), (SI, 3, 3, 4), (G, 1, 0, 4), (SI, 2, 0, 4),
+    (SY, 1, 0, 0), (SI, 2, 0, 2), (SI, 3, 3, 2), (G, 1, 1, 4), (SY, 1, 1, 2), (SI, 1, 0, 4),
+    (AI, 0, 1, 0), (G, 1, 0, 2), (SY, 3, 2, 4), (SI, 3, 3, 3), (N, 1, 0, 0), (SY, 1, 1, 0),
+    (AI, 3, 3, 0), (SY, 3, 1, 6), (SI, 1, 1, 4), (G, 1, 1, 2), (SI, 1, 0, 2), (G, 0, 2, 1),
+    (G, 3, 2, 4), (SY, 3, 2, 2), (SY, 3, 2, 0), (SI, 1, 1, 2), (SY, 0, 0, 0), (N, 1, 1, 0),
+    (X, 1, 0, 0), (SY, 0, 2, 0), (G, 3, 1, 6), (SI, 3, 1, 6), (G, 3, 2, 2), (SY, 3, 1, 4),
+    (N, 3, 2, 0), (X, 3, 2, 0), (SY, 3, 1, 0), (U, 1, 0, 0), (U, 1, 1, 0), (N, 0, 0, 0),
+    (X, 0, 0, 0), (AI, 2, 0, 0), (SY, 3, 1, 2), (AY, 3, 4, 0), (SI, 3, 2, 4), (N, 0, 2, 0),
+    (X, 0, 2, 0), (U, 3, 2, 0), (AY, 3, 0, 0), (G, 3, 1, 4), (SI, 0, 0, 5), (AY, 0, 3, 0),
+    (AY, 0, 1, 0), (U, 0, 0, 0), (SI, 0, 0, 4), (G, 3, 1, 2), (V, 0, 0, 2), (AY, 2, 0, 0),
+    (U, 0, 2, 0), (AI, 3, 4, 1), (AY, 3, 3, 0), (AI, 3, 0, 1), (AI, 0, 3, 1), (AY, 1, 0, 0),
+    (SI, 3, 2, 2), (AY, 1, 1, 0), (AI, 0, 1, 1), (AI, 2, 0, 1), (AY, 3, 2, 0), (AI, 1, 0, 0),
+    (N, 3, 1, 0), (X, 3, 1, 0), (SI, 0, 2, 5), (AY, 3, 3, 6), (U, 3, 1, 0), (AY, 3, 3, 2),
+    (SI, 0, 0, 3), (AY, 1, 0, 2), (AI, 1, 1, 0), (AY, 0, 0, 0), (SI, 0, 0, 2), (AY, 0, 2, 0),
+    (SI, 0, 2, 3), (AY, 1, 1, 2), (SI, 0, 2, 2), (AY, 3, 3, 4), (SI, 0, 2, 4), (SI, 3, 1, 4),
+    (AY, 3, 2, 2), (AY, 3, 1, 0), (AI, 0, 0, 0), (AY, 1, 0, 4), (AI, 3, 2, 0), (AY, 1, 1, 4),
+    (AI, 0, 2, 0), (SI, 3, 1, 2), (AY, 3, 2, 4), (AI, 3, 1, 1), (AI, 3, 1, 0), (AY, 0, 0, 2),
+    (AY, 1, 0, 6), (AY, 1, 1, 6), (AY, 0, 0, 4), (AY, 3, 2, 6), (AY, 0, 0, 6), (AY, 0, 2, 2),
+    (AY, 0, 2, 6), (AY, 0, 2, 4),
 )
 MID = (
-    ("E", 0, 0, 7), ("sY", 0, 0, 6), ("E", 0, 0, 5), ("sY", 0, 0, 4), ("E", 0, 0, 3), ("E", 0, 0, 1),
-    ("E", 1, 2, 7), ("E", 1, 2, 5), ("E", 1, 2, 3), ("sY", 0, 0, 2), ("E", 1, 2, 1), ("E", 3, 0, 7),
-    ("E", 3, 0, 5), ("E", 3, 0, 3), ("E", 3, 0, 1), ("E", 1, 0, 7), ("E", 1, 0, 5), ("E", 1, 0, 3),
-    ("E", 1, 0, 1), ("E", 1, 3, 7), ("E", 1, 3, 5), ("E", 1, 3, 3), ("sY", 0, 0, 0), ("E", 1, 3, 1),
-    ("E", 1, 1, 7), ("E", 1, 1, 5), ("E", 1, 1, 3), ("E", 1, 1, 1), ("E", 3, 2, 7), ("E", 3, 2, 5),
-    ("E", 3, 2, 3), ("E", 3, 2, 1), ("G", 0, 2, 6), ("sI", 0, 2, 6), ("E", 0, 1, 7), ("E", 0, 1, 5),
-    ("sY", 1, 2, 6), ("E", 0, 1, 3), ("E", 0, 1, 1), ("E", 2, 0, 7), ("E", 2, 0, 5), ("V", 0, 0, 0),
-    ("E", 2, 0, 3), ("E", 2, 0, 1), ("G", 0, 2, 7), ("sI", 0, 2, 7), ("sY", 1, 2, 4), ("G", 0, 2, 4),
-    ("sI", 0, 2, 4), ("sY", 1, 2, 2), ("G", 0, 2, 0), ("sO", 0, 2, 0), ("G", 0, 2, 5), ("sI", 0, 2, 5),
-    ("sY", 1, 2, 0), ("G", 0, 2, 1), ("sO", 0, 2, 1), ("G", 0, 0, 6), ("sI", 0, 0, 6), ("sY", 3, 0, 6),
-    ("G", 0, 0, 4), ("sI", 0, 0, 4), ("sY", 3, 0, 4), ("sY", 3, 0, 2), ("G", 0, 0, 0), ("sO", 0, 0, 0),
-    ("sY", 3, 0, 0), ("sY", 1, 0, 6), ("N", 0, 0, 0), ("n", 0, 0, 0), ("G", 0, 2, 3), ("sY", 0, 2, 2),
-    ("G", 0, 3, 6), ("sI", 0, 3, 6), ("sY", 1, 0, 4), ("G", 0, 3, 7), ("sI", 0, 3, 7), ("U", 0, 0, 0),
-    ("aY", 0, 0, 2), ("aO", 0, 0, 2), ("aI", 0, 0, 2), ("G", 0, 3, 4), ("sI", 0, 3, 4), ("sY", 1, 0, 2),
-    ("G", 0, 3, 0), ("sO", 0, 3, 0), ("N", 0, 2, 0), ("n", 0, 2, 0), ("G", 0, 3, 5), ("sI", 0, 3, 5),
-    ("sY", 1, 0, 0), ("G", 0, 3, 1), ("sO", 0, 3, 1), ("sY", 1, 3, 6), ("aO", 0, 0, 4), ("aY", 0, 0, 4),
-    ("U", 0, 2, 0), ("aO", 0, 2, 2), ("aI", 0, 2, 2), ("G", 3, 1, 6), ("sI", 3, 1, 6), ("aY", 0, 2, 2),
-    ("G", 3, 1, 7), ("sI", 3, 1, 7), ("G", 0, 3, 3), ("G", 3, 1, 4), ("sY", 0, 3, 2), ("sI", 3, 1, 4),
-    ("aO", 0, 2, 4), ("G", 3, 1, 5), ("sI", 3, 1, 5), ("sY", 1, 3, 4), ("G", 3, 1, 0), ("sO", 3, 1, 0),
-    ("sY", 1, 3, 2), ("G", 3, 1, 1), ("sO", 3, 1, 1), ("aO", 0, 2, 3), ("aI", 0, 2, 3), ("sY", 1, 3, 0),
-    ("aI", 0, 0, 0), ("N", 0, 3, 0), ("n", 0, 3, 0), ("G", 3, 1, 3), ("sY", 3, 1, 2), ("aI", 0, 2, 0),
-    ("aO", 0, 2, 5), ("aY", 0, 0, 0), ("aI", 0, 2, 1), ("sY", 1, 1, 6), ("aO", 0, 0, 6), ("U", 0, 3, 0),
-    ("aO", 0, 3, 2), ("aI", 0, 3, 2), ("G", 1, 2, 6), ("sI", 1, 2, 6), ("aY", 0, 0, 6), ("aO", 0, 2, 6),
-    ("N", 3, 1, 0), ("n", 3, 1, 0), ("G", 1, 2, 4), ("sI", 1, 2, 4), ("aY", 0, 3, 2), ("aO", 0, 2, 7),
-    ("sY", 1, 1, 4), ("aO", 0, 3, 4), ("aI", 0, 3, 0), ("U", 3, 1, 0), ("sY", 1, 1, 2), ("aI", 3, 1, 2),
-    ("G", 1, 2, 0), ("sO", 1, 2, 0), ("G", 3, 0, 6), ("sI", 3, 0, 6), ("G", 3, 0, 4), ("V", 0, 0, 1),
-    ("sY", 1, 1, 0), ("N", 1, 2, 0), ("aO", 3, 1, 2), ("aI", 0, 3, 3), ("sY", 3, 2, 6), ("aO", 0, 3, 6),
-    ("sI", 3, 0, 4), ("aO", 0, 3, 3), ("sY", 3, 2, 4), ("aI", 0, 3, 1), ("G", 3, 0, 0), ("sY", 3, 2, 2),
-    ("G", 1, 0, 6), ("sO", 3, 0, 0), ("sI", 1, 0, 6), ("sY", 3, 2, 0), ("G", 1, 0, 4), ("aO", 0, 3, 5),
-    ("sI", 1, 0, 4), ("sY", 0, 1, 6), ("N", 3, 0, 0), ("n", 3, 0, 0), ("aO", 3, 1, 4), ("sY", 0, 1, 4),
-    ("aO", 0, 3, 7), ("G", 1, 3, 6), ("sI", 1, 3, 6), ("sY", 0, 1, 2), ("G", 1, 0, 0), ("sO", 1, 0, 0),
-    ("G", 1, 3, 4), ("sI", 1, 3, 4), ("U", 3, 0, 0), ("aY", 3, 1, 2), ("aI", 3, 0, 2), ("N", 1, 0, 0),
-    ("aO", 3, 0, 2), ("sY", 0, 1, 0), ("G", 1, 3, 0), ("sO", 1, 3, 0), ("G", 1, 1, 6), ("aY", 3, 0, 2),
-    ("sI", 1, 1, 6), ("N", 1, 3, 0), ("G", 1, 1, 4), ("sY", 2, 0, 6), ("sI", 1, 1, 4), ("aO", 3, 0, 4),
-    ("aO", 3, 1, 3), ("aI", 3, 1, 3), ("aY", 3, 0, 4), ("G", 1, 1, 0), ("sO", 1, 1, 0), ("sY", 2, 0, 4),
-    ("aI", 3, 1, 0), ("G", 3, 2, 6), ("sY", 2, 0, 2), ("sI", 3, 2, 6), ("N", 1, 1, 0), ("n", 1, 0, 0),
-    ("G", 3, 2, 4), ("aO", 3, 1, 5), ("sI", 3, 2, 4), ("sY", 2, 0, 0), ("aO", 3, 1, 6), ("aI", 3, 1, 1),
-    ("U", 1, 2, 0), ("aY", 1, 2, 2), ("aO", 1, 2, 2), ("aI", 1, 2, 2), ("U", 1, 0, 0), ("aO", 1, 0, 2),
-    ("U", 1, 3, 0), ("U", 1, 1, 0), ("G", 3, 2, 0), ("aY", 1, 0, 2), ("aI", 1, 0, 2), ("N", 3, 2, 0),
-    ("n", 3, 2, 0), ("G", 0, 1, 6), ("sO", 3, 2, 0), ("sI", 0, 1, 6), ("aY", 1, 3, 2), ("G", 0, 1, 4),
-    ("aO", 3, 1, 7), ("sI", 0, 1, 4), ("aY", 1, 1, 2), ("aO", 1, 3, 2), ("U", 3, 2, 0), ("aO", 1, 2, 4),
-    ("aY", 1, 2, 4), ("aI", 3, 0, 0), ("G", 3, 3, 6), ("aO", 1, 0, 4), ("aY", 3, 0, 0), ("sI", 3, 3, 6),
-    ("G", 0, 1, 0), ("aI", 1, 2, 0), ("sO", 0, 1, 0), ("aY", 1, 2, 0), ("N", 0, 1, 0), ("n", 0, 1, 0),
-    ("aI", 1, 3, 2), ("V", 0, 0, 2), ("G", 3, 3, 7), ("aY", 1, 0, 4), ("aO", 1, 1, 2), ("G", 3, 3, 4),
-    ("sI", 3, 3, 7), ("aY", 3, 0, 6), ("G", 3, 3, 0), ("sO", 3, 3, 0), ("G", 3, 3, 5), ("sI", 3, 3, 4),
-    ("aY", 3, 2, 2), ("aO", 1, 2, 6), ("U", 0, 1, 0), ("sI", 3, 3, 5), ("aY", 1, 2, 6), ("aO", 3, 0, 6),
-    ("aI", 1, 1, 2), ("aY", 1, 3, 4), ("G", 3, 3, 1), ("sO", 3, 3, 1), ("aI", 1, 0, 0), ("aY", 1, 0, 0),
-    ("G", 2, 0, 6), ("aO", 1, 3, 4), ("sI", 2, 0, 6), ("G", 3, 3, 3), ("sY", 3, 3, 2), ("aO", 3, 2, 2),
-    ("G", 2, 0, 4), ("sI", 2, 0, 4), ("aO", 1, 1, 4), ("aY", 1, 1, 4), ("aI", 3, 2, 2), ("aO", 0, 1, 2),
-    ("aY", 0, 1, 2), ("aI", 1, 3, 0), ("aO", 1, 0, 6), ("aY", 1, 0, 6), ("G", 2, 0, 0), ("N", 3, 3, 0),
-    ("n", 3, 3, 0), ("aI", 1, 1, 0), ("sO", 2, 0, 0), ("aY", 1, 3, 0), ("N", 2, 0, 0), ("n", 2, 0, 0),
-    ("aI", 3, 2, 0), ("aO", 3, 2, 4), ("aY", 1, 1, 0), ("aI", 0, 1, 2), ("U", 3, 3, 0), ("aY", 1, 3, 6),
-    ("aO", 1, 3, 6), ("aI", 0, 1, 0), ("U", 2, 0, 0), ("aO", 3, 3, 2), ("aY", 1, 1, 6), ("aI", 3, 3, 2),
-    ("aO", 1, 1, 6), ("aY", 3, 2, 6), ("aI", 2, 0, 2), ("aO", 3, 2, 6), ("aY", 3, 2, 4), ("aO", 0, 1, 4),
-    ("aY", 3, 2, 0), ("aI", 3, 3, 0), ("aO", 0, 1, 6), ("aY", 0, 1, 6), ("aO", 3, 3, 4), ("aY", 0, 1, 4),
-    ("aI", 2, 0, 0), ("aO", 3, 3, 6), ("aY", 0, 1, 0), ("aO", 2, 0, 4), ("aY", 3, 3, 2), ("aI", 3, 3, 1),
-    ("aO", 2, 0, 2), ("aY", 2, 0, 4), ("aO", 2, 0, 6), ("aY", 2, 0, 6), ("aO", 3, 3, 7), ("aY", 2, 0, 2),
-    ("aI", 3, 3, 3), ("aO", 3, 3, 3), ("aY", 2, 0, 0), ("aO", 3, 3, 5),
+    (E, 3, 0, 1), (SY, 3, 0, 0), (E, 3, 0, 3), (SY, 3, 0, 2), (E, 3, 0, 5), (E, 3, 0, 7),
+    (E, 0, 3, 5), (E, 0, 3, 1), (SY, 3, 0, 6), (E, 0, 3, 3), (E, 0, 1, 3), (E, 0, 1, 1),
+    (E, 2, 0, 3), (SY, 3, 0, 4), (E, 2, 0, 1), (E, 0, 1, 5), (E, 2, 0, 5), (E, 0, 3, 7),
+    (SY, 0, 3, 6), (E, 0, 1, 7), (E, 2, 0, 7), (E, 1, 0, 1), (SY, 0, 3, 0), (E, 1, 0, 3),
+    (E, 1, 0, 5), (E, 1, 0, 7), (E, 1, 1, 3), (E, 1, 1, 5), (G, 3, 4, 7), (SI, 3, 4, 7),
+    (E, 1, 1, 1), (E, 3, 2, 3), (V, 0, 0, 0), (G, 3, 4, 4), (SI, 3, 4, 4), (SY, 0, 1, 0),
+    (E, 3, 2, 1), (E, 3, 2, 5), (E, 1, 1, 7), (G, 3, 4, 5), (SI, 3, 4, 5), (E, 3, 1, 3),
+    (E, 3, 2, 7), (E, 3, 1, 1), (G, 3, 4, 6), (SI, 3, 4, 6), (E, 3, 1, 5), (E, 3, 1, 7),
+    (SY, 0, 1, 6), (G, 3, 4, 1), (SO, 3, 4, 1), (SY, 2, 0, 6), (G, 3, 3, 7), (SI, 3, 3, 7),
+    (G, 3, 4, 3), (G, 3, 0, 4), (SI, 3, 0, 4), (G, 3, 4, 0), (SO, 3, 4, 0), (SY, 3, 4, 2),
+    (G, 3, 0, 6), (SI, 3, 0, 6), (G, 3, 3, 6), (SI, 3, 3, 6), (SY, 0, 3, 4), (SY, 0, 3, 2),
+    (G, 3, 3, 1), (SO, 3, 3, 1), (G, 0, 3, 6), (SI, 0, 3, 6), (N, 3, 0, 0), (X, 3, 0, 0),
+    (SY, 2, 0, 0), (G, 3, 0, 0), (SO, 3, 0, 0), (N, 3, 4, 0), (X, 3, 4, 0), (G, 0, 0, 6),
+    (SI, 0, 0, 6), (G, 3, 3, 0), (SO, 3, 3, 0), (SY, 1, 0, 6), (G, 0, 1, 6), (SI, 0, 1, 6),
+    (SY, 1, 0, 0), (U, 3, 0, 0), (AO, 3, 0, 2), (AI, 3, 0, 2), (G, 0, 3, 0), (SO, 0, 3, 0),
+    (G, 0, 3, 4), (SI, 0, 3, 4), (U, 3, 4, 0), (AO, 3, 4, 2), (AI, 3, 4, 2), (G, 0, 0, 0),
+    (G, 2, 0, 6), (SO, 0, 0, 0), (AY, 3, 4, 2), (SI, 2, 0, 6), (G, 0, 1, 0), (SO, 0, 1, 0),
+    (G, 0, 0, 7), (SI, 0, 0, 7), (AO, 3, 0, 4), (AY, 3, 0, 2), (AO, 3, 4, 4), (SY, 0, 1, 4),
+    (G, 1, 0, 6), (SI, 1, 0, 6), (SY, 0, 1, 2), (G, 2, 0, 0), (SO, 2, 0, 0), (N, 0, 3, 0),
+    (X, 0, 3, 0), (SY, 1, 1, 6), (AO, 3, 4, 3), (AI, 3, 4, 3), (G, 0, 0, 1), (AO, 3, 0, 3),
+    (SY, 1, 1, 0), (SO, 0, 0, 1), (AI, 3, 0, 3), (AI, 3, 4, 0), (G, 0, 1, 4), (SI, 0, 1, 4),
+    (AI, 3, 0, 0), (U, 0, 3, 0), (AO, 0, 3, 2), (G, 0, 2, 6), (G, 1, 0, 0), (AY, 0, 3, 2),
+    (SO, 1, 0, 0), (SI, 0, 2, 6), (AO, 3, 4, 5), (AI, 0, 3, 2), (G, 1, 1, 6), (SI, 1, 1, 6),
+    (SY, 2, 0, 2), (AO, 3, 0, 5), (G, 0, 2, 7), (SI, 0, 2, 7), (SY, 2, 0, 4), (AO, 3, 4, 6),
+    (G, 0, 2, 0), (AO, 3, 0, 6), (N, 0, 1, 0), (X, 0, 1, 0), (SO, 0, 2, 0), (SY, 3, 2, 6),
+    (AO, 0, 3, 4), (AI, 0, 3, 3), (SY, 3, 2, 0), (AO, 0, 3, 3), (SY, 1, 0, 4), (AI, 0, 3, 0),
+    (G, 3, 3, 5), (U, 0, 1, 0), (AO, 0, 1, 2), (AY, 0, 1, 2), (G, 1, 1, 0), (SI, 3, 3, 5),
+    (G, 3, 3, 4), (V, 0, 0, 1), (SO, 1, 1, 0), (G, 3, 2, 6), (G, 0, 2, 1), (SI, 3, 3, 4),
+    (G, 2, 0, 4), (SO, 0, 2, 1), (SY, 1, 0, 2), (SI, 2, 0, 4), (SI, 3, 2, 6), (SY, 1, 1, 4),
+    (AO, 0, 3, 5), (AI, 0, 1, 2), (AI, 0, 1, 3), (AO, 0, 1, 3), (SY, 1, 1, 2), (G, 1, 0, 4),
+    (N, 2, 0, 0), (AO, 0, 3, 6), (X, 2, 0, 0), (SI, 1, 0, 4), (G, 3, 2, 0), (AI, 0, 1, 0),
+    (SO, 3, 2, 0), (G, 3, 3, 3), (SY, 3, 3, 2), (AO, 0, 1, 4), (U, 2, 0, 0), (AO, 0, 1, 5),
+    (AI, 2, 0, 2), (AY, 2, 0, 2), (AO, 2, 0, 2), (AI, 3, 3, 0), (G, 1, 1, 4), (AY, 3, 3, 0),
+    (SI, 1, 1, 4), (SY, 3, 2, 4), (AO, 0, 1, 6), (N, 3, 3, 0), (X, 3, 3, 0), (SY, 3, 1, 6),
+    (N, 1, 0, 0), (AO, 2, 0, 4), (SY, 3, 1, 0), (AI, 2, 0, 3), (AO, 2, 0, 3), (AY, 3, 3, 6),
+    (AO, 3, 3, 6), (SY, 3, 2, 2), (U, 3, 3, 0), (AI, 3, 3, 2), (AO, 3, 3, 2), (AY, 3, 3, 2),
+    (G, 3, 1, 6), (SI, 3, 1, 6), (N, 1, 1, 0), (X, 1, 0, 0), (SY, 3, 1, 2), (AI, 2, 0, 0),
+    (AO, 2, 0, 5), (SY, 3, 1, 4), (G, 3, 2, 4), (SI, 3, 2, 4), (AO, 3, 3, 4), (AY, 3, 3, 4),
+    (G, 0, 0, 5), (SI, 0, 0, 5), (G, 3, 1, 0), (SO, 3, 1, 0), (U, 1, 0, 0), (AO, 1, 0, 2),
+    (AY, 1, 0, 2), (AI, 1, 0, 2), (U, 1, 1, 0), (AY, 1, 1, 2), (G, 0, 0, 4), (AO, 1, 1, 2),
+    (SI, 0, 0, 4), (AO, 2, 0, 6), (AI, 3, 0, 1), (N, 3, 2, 0), (X, 3, 2, 0), (AI, 3, 4, 1),
+    (AI, 0, 3, 1), (AY, 1, 0, 4), (AI, 0, 1, 1), (AO, 1, 0, 4), (U, 3, 2, 0), (AY, 3, 2, 2),
+    (AI, 1, 1, 2), (AO, 3, 2, 2), (AI, 2, 0, 1), (AY, 1, 0, 0), (AO, 3, 4, 7), (G, 0, 2, 5),
+    (AO, 3, 0, 7), (SI, 0, 2, 5), (V, 0, 0, 2), (AO, 0, 3, 7), (G, 0, 0, 3), (SY, 0, 0, 2),
+    (AO, 0, 1, 7), (AI, 3, 2, 2), (AY, 1, 1, 4), (AO, 1, 1, 4), (AI, 1, 0, 0), (AY, 1, 1, 0),
+    (AO, 2, 0, 7), (AI, 1, 1, 0), (N, 0, 0, 0), (X, 0, 0, 0), (AY, 3, 2, 4), (G, 0, 2, 3),
+    (AO, 3, 2, 4), (SY, 0, 2, 2), (U, 0, 0, 0), (AO, 0, 0, 2), (AI, 0, 0, 2), (AO, 1, 0, 6),
+    (G, 0, 2, 4), (AY, 1, 0, 6), (SI, 0, 2, 4), (G, 3, 1, 4), (AY, 0, 0, 2), (SI, 3, 1, 4),
+    (AO, 1, 1, 6), (AI, 0, 0, 0), (AO, 0, 0, 4), (AY, 0, 0, 4), (AI, 3, 2, 0), (N, 0, 2, 0),
+    (AY, 1, 1, 6), (X, 0, 2, 0), (AI, 0, 2, 0), (N, 3, 1, 0), (X, 3, 1, 0), (AI, 3, 1, 1),
+    (AY, 3, 2, 0), (AO, 0, 0, 6), (AI, 3, 1, 0), (AO, 3, 2, 6), (U, 0, 2, 0), (AI, 0, 2, 2),
+    (AO, 0, 2, 2), (AY, 0, 2, 2), (U, 3, 1, 0), (AI, 3, 1, 2), (AO, 3, 1, 2), (AY, 3, 1, 2),
+    (AO, 0, 2, 6), (AY, 3, 2, 6), (AO, 3, 1, 7), (AY, 0, 0, 6), (AY, 0, 2, 4), (AO, 0, 2, 4),
+    (AI, 3, 1, 3), (AO, 3, 1, 3), (AY, 0, 2, 6), (AO, 3, 1, 4), (AY, 0, 0, 0), (AO, 3, 1, 6),
+    (AY, 0, 2, 0), (AO, 3, 1, 5),
 )
 
 
@@ -207,8 +204,9 @@
 
     lanes = functools.partial(lanes_of, shapes)
     at = {k: i for i, k in enumerate(CHUNKS)}
-    height = lambda g: shapes[g][0] // len(KINDS[g])
-    rows = lambda g, c: pl.ds(c * height(g), height(g))
+    unit = lambda g: shapes[g][0] // sum(SIZES[g])
+    height = lambda g, c: unit(g) * SIZES[g][c]
+    rows = lambda g, c: pl.ds(unit(g) * sum(SIZES[g][:c]), height(g, c))
 
     def source(g, c, s):
         w = shapes[g][1]
@@ -216,8 +214,8 @@
             return xin[g].at[slab[s], rows(g, c)]
         return xin[g].at[rows(g, c), pl.ds(pl.multiple_of(slab[s] * w, w), w)]
 
-    def loop(g, body):
-        h, w = height(g), shapes[g][1]
+    def loop(g, c, body):
+        h, w = height(g, c), shapes[g][1]
         step = min(h, max(16, STEP // w // 16 * 16))
         while h % step:
             step -= 16
@@ -313,40 +311,40 @@
 
     def run(mid, order):
         mine = 1 if mid else 0
-        peers = {"Y": z * 2 + (1 - y), "n": None}
+        peers = {}
         if mid:
-            peers["sO"] = peers["aO"] = side * 6 + y
-            peers["sI"] = peers["aI"] = (3 - z) * 2 + y
+            peers[SO] = peers[AO] = side * 6 + y
+            peers[SI] = peers[AI] = (3 - z) * 2 + y
         else:
-            peers["sI"] = peers["aI"] = (1 + side) * 2 + y
-        peers["sY"] = peers["aY"] = z * 2 + (1 - y)
+            peers[SI] = peers[AI] = (1 + side) * 2 + y
+        peers[SY] = peers[AY] = z * 2 + (1 - y)
         done = set()
 
         def kind(g, c):
-            return KINDS[g][c]
+            return SUMS[g][c]
 
         def landing(g, c, by, s):
-            if kind(g, c) == "A":
-                return {"Y": 0, "O": 3, "I": 7}[by] + s // 2
-            return {"Y": 10, "O": s - 2, "I": 6 + s}[by]
+            if kind(g, c) == A:
+                return (0, 7, 3)[by] + s // 2
+            return (10, 6 + s, s - 2)[by]
 
         def outgoing(g, c, op, s):
             p = s // 2
-            if kind(g, c) == "A":
-                if op == "sY":
+            if kind(g, c) == A:
+                if op == SY:
                     return p
                 return 3 + p if p else 4
-            if op == "sY":
+            if op == SY:
                 return 6
             if not mid:
                 return s - 2
             return s - 4 if p >= 2 else 4 + s
 
         def across(op, s):
-            return (3 - s // 2) * 2 + s % 2 if mid and op[1] == "I" else s
+            return (3 - s // 2) * 2 + s % 2 if mid and op in (SI, AI) else s
 
         def send(op, g, c, s):
-            by = {"sY": "Y", "sO": "I", "sI": "I" if mid else "O"}[op]
+            by = {SY: 0, SO: 1, SI: 1 if mid else 2}[op]
             slot = landing(g, c, by, across(op, s))
             return remote(
                 enc[g].at[outgoing(g, c, op, s), rows(g, c)],
@@ -357,9 +355,9 @@
             )
 
         def gather(op, g, c, s):
-            to = s + 1 if op == "aY" else across(op, s)
+            to = s + 1 if op == AY else across(op, s)
             ref = full[g].at[slab[s], rows(g, c)]
-            link = {"aY": 0, "aI": 1, "aO": 2}[op]
+            link = {AY: 0, AI: 1, AO: 2}[op]
             return remote(ref, ref, ag_s.at[at[g, c], link], ag_r.at[at[g, c], to], peers[op])
 
         def got(g, c, s):
@@ -380,18 +378,18 @@
                 whole(ref, sem)
 
         def loaded(g, c):
-            once(("load", g, c), chunk_of(g, c), load_sem.at[at[g, c]])
+            once((-1, g, c), chunk_of(g, c), load_sem.at[at[g, c]])
 
         def parts(g, c, s):
             loaded(g, c)
             by = []
-            a, p = kind(g, c) == "A", s // 2
+            a, p = kind(g, c) == A, s // 2
             if a or s == mine * 2:
-                by.append("Y")
+                by.append(0)
             if mid and p >= 1:
-                by.append("O")
+                by.append(2)
             if p == mine or (mid and p == 0):
-                by.append("I")
+                by.append(1)
             return [arrived(g, c, b, s) for b in by]
 
         def encode_op(g, c, s, op):
@@ -401,11 +399,11 @@
             def body(d):
                 dst[d, :] = encode(src[d, :])
 
-            loop(g, body)
+            loop(g, c, body)
 
         def add_op(g, c, s):
             src = source(g, c, s)
-            op = "sY" if s // 2 == mine else "sO" if mid and s < 2 else "sI"
+            op = SY if s // 2 == mine else SO if mid and s < 2 else SI
             dst = enc[g].at[outgoing(g, c, op, s), rows(g, c)]
             got = parts(g, c, s)
 
@@ -415,12 +413,12 @@
                     total = total + decode(ref[d, :])
                 dst[d, :] = encode(total)
 
-            loop(g, body)
+            loop(g, c, body)
 
         def mean_op(g, c):
             acc = source(g, c, mine * 2)
             got = parts(g, c, mine * 2)
-            once(("own", g), own[g], own_sem.at[g])
+            once((-2, g), own[g], own_sem.at[g])
             held = own[g].at[rows(g, c)]
             k = len(GROUPS[g].members)
             w = shapes[g][1] // k
@@ -454,7 +452,7 @@
                     sq[g][0] += jnp.sum((p * p).reshape(-1, 8, w), axis=0)
                     sq[g][1] += jnp.sum((v * v).reshape(-1, 8, w), axis=0)
 
-            loop(g, body)
+            loop(g, c, body)
 
         def norms(g, c, j):
             if GROUPS[g].rows:
@@ -466,10 +464,10 @@
         def update_op(g, c):
             first = c if GROUPS[g].rows else 0
             for j in range(1, models):
-                if ("norm", g, first, j) not in done:
-                    done.add(("norm", g, first, j))
+                if (-4, g, first, j) not in done:
+                    done.add((-4, g, first, j))
                     norms(g, first, j).wait_recv()
-            once(("st", g), st[g], st_sem.at[g])
+            once((-3, g), st[g], st_sem.at[g])
             acc, half = source(g, c, mine * 2), full[g].at[slab[mine * 2], rows(g, c)]
             held, hold = own[g].at[rows(g, c)], st[g].at[rows(g, c)]
             k = len(GROUPS[g].members)
@@ -504,27 +502,27 @@
                 def body(d):
                     put(d, slice(None), t)
 
-            loop(g, body)
+            loop(g, c, body)
 
         met = False
         for op, g, c, s in order:
-            if op not in ("E", "G") and not met:
+            if op not in (E, G) and not met:
                 met = True
                 pl.semaphore_wait(barrier, replicas + models - 2)
-            if op == "E":
-                encode_op(g, c, s, "sY" if kind(g, c) == "A" else "sI")
-            elif op == "G":
+            if op == E:
+                encode_op(g, c, s, SY if kind(g, c) == A else SI)
+            elif op == G:
                 add_op(g, c, s)
-            elif op in ("sY", "sI", "sO"):
+            elif op in (SY, SI, SO):
                 send(op, g, c, s).start()
-            elif op == "N":
+            elif op == N:
                 mean_op(g, c)
-            elif op == "n":
+            elif op == X:
                 for j in range(1, models):
                     norms(g, c, j).start()
-            elif op == "U":
+            elif op == U:
                 update_op(g, c)
-            elif op == "V":
+            elif op == V:
                 (vec_start, vec_update, vec_finish)[s]()
             else:
                 got(g, c, s)
@@ -536,7 +534,7 @@
         for g in groups:
             whole(enc[g], rs_s.at[g])
         for g, c in CHUNKS:
-            for link, count in enumerate(SENT[mid][kind(g, c)]):
+            for link, count in enumerate(SENT[mid][BACK[g][c]]):
                 if count:
                     whole(full[g].at[pl.ds(0, count), rows(g, c)], ag_s.at[at[g, c], link])
             if GROUPS[g].rows or c == 0:
@@ -579,7 +577,7 @@
         pltpu.VMEM((replicas, *s) if g.rows else (s[0], s[1] * replicas), f32) for g, s in zip(GROUPS, shapes)
     ]
     scratch += [pltpu.VMEM((7, *s), bf16) for s in shapes]
-    scratch += [pltpu.VMEM((11 if "B" in k else 9, *s), bf16) for k, s in zip(KINDS, shapes)]
+    scratch += [pltpu.VMEM((11 if B in k else 9, *s), bf16) for k, s in zip(SUMS, shapes)]
     sq = [(s[0], 128) if g.rows else (2, 8, s[1]) for g, s in zip(GROUPS, shapes)]
     scratch += [pltpu.VMEM(s, f32) for s in sq]
     scratch += [pltpu.VMEM((models - 1, *s), f32) for s in sq]
@@ -777,10 +775,10 @@
         if replicas != 2**3 or any(a.shape[k] % 128 for a in args[8:14] for k in (0, 1)):
             return plain(*args)
         shapes = []
-        for g, kinds in zip(GROUPS, KINDS):
+        for g, sizes in zip(GROUPS, SIZES):
             h, w = args[8 + g.members[0]].shape
             shapes.append((h, w * len(g.members)))
-            if h % (16 * len(kinds)) or (w != 128 and not g.rows):
+            if h % (16 * sum(sizes)) or (w != 128 and not g.rows):
                 return plain(*args)
         if args[14].shape[0] % 128:
             return plain(*args)

time: 124 us -> 120 us (0.968)
  Pallas kernels: 123 us -> 119 us
    pallas_call x1, Pallas kernels: 120 us -> 116 us  [fused(): pl.pallas_call(functools.partial(kernel, replicas, models, 4.0, shapes),...]
where the time goes in v2:
time: 120 us
  Pallas kernels  119 us (99%)
    pallas_call x1, Pallas kernels, fused(): pl.pallas_call(functools.partial(kernel, replicas, models, 4.0, shapes),...  116 us
    pallas_call x1, Pallas kernels, fused(): pl.pallas_call(functools.partial(finish, shapes), out_shape=outs, in_spec...  3.78 us

profile of v2, /device:TPU:0, one launch (start us, length us, event | category | flops | bytes accessed | tf_op | source)
XLA Modules:
  0.0 120.0 jit_solution(6002927168576757308)
XLA Ops:
  0.7 115.6 %shard_map.415 = (bf16[8,128,1024]{2,1,0:T(8,128)(2,1)S(1)}, bf16[8,1024,128]{2,1,0:T(8,128)(2,1)S(1)}, bf16[8,256,128]{2,1,0:T(8,128)(2,1)S(1)}, bf16[8,128,768...) custom-call(f32[8,128,1024]{2,1,0:T(8,128)} %bitcast.20, ...), custom_call_target="tpu_custom_call" | custom-call | tf_op jit(solution)/shard_map/pallas_call | solution.py:597
  116.2 3.8 %shard_map.416 = (bf16[8,128,1024]{2,1,0:T(8,128)(2,1)}, bf16[1024,1024]{1,0:T(8,128)(2,1)}, bf16[8,128,256]{2,1,0:T(8,128)(2,1)}, bf16[8,128,256]{2,1,0:T(8,128...) custom-call(bf16[8,128,1024]{2,1,0:T(8,128)(2,1)S(1)} %get-tuple-ele, ...), custom_call_target="tpu_custom_call" | custom-call | tf_op jit(solution)/shard_map/pallas_call | solution.py:614

commit v3 on v2

--- a/solution.py
+++ b/solution.py
@@ -22,114 +22,121 @@
 GROUPS = (Group((0,), True), Group((1,), False), Group((5,), False), Group((2, 3, 4), True))
 A, B = 0, 1
 E, G, N, X, U, V, SY, SI, SO, AY, AI, AO = range(12)
-SIZES = ((2, 2, 2, 2), (4, 4), (8,), (1, 2, 2, 2, 1))
-SUMS = ((B, A, B, A), (A, A), (A,), (A, A, A, B, B))
-BACK = ((A, B, A, B), (A, A), (B,), (B, B, A, A, B))
-CHUNKS = ((3, 0), (3, 4), (0, 3), (0, 1), (2, 0), (3, 3), (1, 0), (1, 1), (3, 2), (0, 0), (0, 2), (3, 1))
-OWN = (3, 0, 2, 1)
+SIZES = ((2, 2, 2, 2), (2, 2, 2, 2), (8,), (2, 2, 2, 2))
+SUMS = ((B, A, A, A), (A, A, A, A), (A,), (B, B, B, B))
+BACK = ((A, B, B, B), (A, A, A, A), (B,), (A, A, A, A))
+CHUNKS = ((0, 3), (3, 2), (0, 0), (3, 0), (0, 2), (1, 2), (1, 1), (3, 3), (0, 1), (3, 1), (1, 3), (2, 0), (1, 0))
+OWN = (0, 3, 1, 2)
 SENT = (((4, 1, 0), (1, 2, 0)), ((4, 2, 3), (1, 4, 6)))
 STEP = 16384
 END = (
-    (E, 3, 0, 5), (SY, 3, 0, 4), (E, 3, 4, 7), (SI, 3, 4, 7), (E, 3, 4, 4), (SI, 3, 4, 4),
-    (E, 3, 0, 3), (SY, 3, 0, 2), (E, 3, 4, 2), (E, 3, 4, 3), (E, 3, 4, 5), (SI, 3, 4, 5),
-    (E, 3, 0, 7), (SY, 3, 0, 6), (E, 3, 4, 6), (E, 3, 0, 1), (SY, 3, 0, 0), (E, 0, 3, 3),
-    (SI, 3, 4, 6), (E, 0, 3, 5), (E, 0, 3, 1), (E, 0, 3, 7), (SY, 0, 3, 6), (E, 2, 0, 5),
-    (SI, 3, 4, 2), (V, 0, 0, 0), (E, 0, 1, 3), (E, 0, 1, 7), (SY, 0, 1, 6), (E, 2, 0, 3),
-    (SI, 3, 4, 3), (E, 0, 1, 5), (E, 3, 3, 4), (E, 3, 3, 5), (E, 3, 3, 7), (SI, 3, 3, 7),
-    (G, 3, 0, 4), (E, 1, 0, 3), (E, 3, 3, 6), (E, 1, 0, 5), (SI, 3, 0, 4), (G, 3, 0, 2),
-    (SY, 0, 3, 4), (E, 0, 1, 1), (E, 3, 3, 2), (E, 2, 0, 7), (G, 3, 0, 6), (E, 3, 3, 3),
-    (E, 1, 1, 5), (SI, 3, 0, 6), (E, 2, 0, 1), (E, 1, 0, 7), (E, 1, 1, 3), (SI, 3, 3, 6),
-    (SY, 2, 0, 6), (E, 0, 0, 5), (E, 0, 0, 4), (E, 1, 1, 7), (SI, 3, 0, 2), (E, 3, 2, 5),
-    (E, 0, 0, 2), (E, 0, 0, 6), (G, 0, 3, 6), (E, 1, 0, 1), (E, 0, 0, 3), (E, 1, 1, 1),
-    (SI, 0, 3, 6), (SY, 1, 0, 6), (E, 0, 2, 4), (E, 3, 2, 3), (E, 0, 2, 5), (E, 3, 2, 7),
-    (SI, 0, 0, 6), (E, 3, 2, 1), (E, 0, 2, 7), (G, 0, 1, 6), (E, 0, 0, 7), (E, 0, 2, 3),
-    (SY, 0, 3, 2), (E, 0, 2, 6), (E, 0, 2, 2), (E, 3, 1, 5), (E, 3, 1, 7), (E, 3, 1, 3),
-    (SI, 0, 1, 6), (E, 3, 1, 1), (G, 0, 3, 4), (G, 3, 4, 1), (SI, 0, 3, 4), (G, 2, 0, 6),
-    (SY, 3, 4, 0), (SI, 2, 0, 6), (SY, 0, 3, 0), (SY, 0, 1, 4), (SI, 0, 0, 7), (G, 1, 0, 6),
-    (G, 3, 3, 1), (SY, 3, 2, 6), (SI, 1, 0, 6), (G, 0, 3, 2), (N, 3, 0, 0), (X, 3, 0, 0),
-    (N, 3, 4, 0), (X, 3, 4, 0), (SY, 1, 1, 6), (SI, 0, 3, 2), (SY, 0, 1, 0), (G, 0, 1, 4),
-    (U, 3, 0, 0), (U, 3, 4, 0), (AI, 3, 0, 0), (G, 3, 2, 6), (N, 0, 3, 0), (X, 0, 3, 0),
-    (SY, 3, 3, 0), (AI, 3, 4, 0), (SI, 0, 1, 4), (SY, 0, 1, 2), (SI, 0, 2, 6), (G, 1, 1, 6),
-    (SY, 2, 0, 0), (SI, 1, 1, 6), (U, 0, 3, 0), (N, 0, 1, 0), (X, 0, 1, 0), (SY, 2, 0, 4),
-    (SI, 0, 2, 7), (V, 0, 0, 1), (N, 3, 3, 0), (X, 3, 3, 0), (SY, 2, 0, 2), (G, 0, 1, 2),
-    (SY, 1, 0, 4), (SI, 0, 1, 2), (U, 0, 1, 0), (N, 2, 0, 0), (X, 2, 0, 0), (SY, 1, 1, 4),
-    (U, 3, 3, 0), (SI, 3, 2, 6), (G, 0, 0, 1), (G, 2, 0, 4), (AI, 0, 3, 0), (G, 2, 0, 2),
-    (SY, 1, 0, 2), (SI, 3, 3, 5), (U, 2, 0, 0), (SI, 3, 3, 4), (G, 1, 0, 4), (SI, 2, 0, 4),
-    (SY, 1, 0, 0), (SI, 2, 0, 2), (SI, 3, 3, 2), (G, 1, 1, 4), (SY, 1, 1, 2), (SI, 1, 0, 4),
-    (AI, 0, 1, 0), (G, 1, 0, 2), (SY, 3, 2, 4), (SI, 3, 3, 3), (N, 1, 0, 0), (SY, 1, 1, 0),
-    (AI, 3, 3, 0), (SY, 3, 1, 6), (SI, 1, 1, 4), (G, 1, 1, 2), (SI, 1, 0, 2), (G, 0, 2, 1),
-    (G, 3, 2, 4), (SY, 3, 2, 2), (SY, 3, 2, 0), (SI, 1, 1, 2), (SY, 0, 0, 0), (N, 1, 1, 0),
-    (X, 1, 0, 0), (SY, 0, 2, 0), (G, 3, 1, 6), (SI, 3, 1, 6), (G, 3, 2, 2), (SY, 3, 1, 4),
-    (N, 3, 2, 0), (X, 3, 2, 0), (SY, 3, 1, 0), (U, 1, 0, 0), (U, 1, 1, 0), (N, 0, 0, 0),
-    (X, 0, 0, 0), (AI, 2, 0, 0), (SY, 3, 1, 2), (AY, 3, 4, 0), (SI, 3, 2, 4), (N, 0, 2, 0),
-    (X, 0, 2, 0), (U, 3, 2, 0), (AY, 3, 0, 0), (G, 3, 1, 4), (SI, 0, 0, 5), (AY, 0, 3, 0),
-    (AY, 0, 1, 0), (U, 0, 0, 0), (SI, 0, 0, 4), (G, 3, 1, 2), (V, 0, 0, 2), (AY, 2, 0, 0),
-    (U, 0, 2, 0), (AI, 3, 4, 1), (AY, 3, 3, 0), (AI, 3, 0, 1), (AI, 0, 3, 1), (AY, 1, 0, 0),
-    (SI, 3, 2, 2), (AY, 1, 1, 0), (AI, 0, 1, 1), (AI, 2, 0, 1), (AY, 3, 2, 0), (AI, 1, 0, 0),
-    (N, 3, 1, 0), (X, 3, 1, 0), (SI, 0, 2, 5), (AY, 3, 3, 6), (U, 3, 1, 0), (AY, 3, 3, 2),
-    (SI, 0, 0, 3), (AY, 1, 0, 2), (AI, 1, 1, 0), (AY, 0, 0, 0), (SI, 0, 0, 2), (AY, 0, 2, 0),
-    (SI, 0, 2, 3), (AY, 1, 1, 2), (SI, 0, 2, 2), (AY, 3, 3, 4), (SI, 0, 2, 4), (SI, 3, 1, 4),
-    (AY, 3, 2, 2), (AY, 3, 1, 0), (AI, 0, 0, 0), (AY, 1, 0, 4), (AI, 3, 2, 0), (AY, 1, 1, 4),
-    (AI, 0, 2, 0), (SI, 3, 1, 2), (AY, 3, 2, 4), (AI, 3, 1, 1), (AI, 3, 1, 0), (AY, 0, 0, 2),
-    (AY, 1, 0, 6), (AY, 1, 1, 6), (AY, 0, 0, 4), (AY, 3, 2, 6), (AY, 0, 0, 6), (AY, 0, 2, 2),
-    (AY, 0, 2, 6), (AY, 0, 2, 4),
+    (E, 0, 3, 1), (SY, 0, 3, 0), (E, 0, 3, 3), (SY, 0, 3, 2), (E, 3, 2, 6), (SI, 3, 2, 6),
+    (E, 3, 2, 7), (SI, 3, 2, 7), (E, 0, 3, 5), (E, 0, 0, 7), (E, 0, 3, 7), (E, 3, 0, 7),
+    (E, 0, 0, 6), (E, 0, 2, 1), (E, 0, 2, 7), (E, 0, 2, 5), (SY, 0, 3, 4), (SI, 0, 0, 7),
+    (E, 0, 2, 3), (E, 1, 2, 5), (E, 1, 2, 3), (E, 3, 0, 6), (E, 3, 3, 6), (E, 3, 3, 7),
+    (E, 1, 2, 7), (SI, 3, 0, 7), (E, 0, 1, 3), (E, 0, 1, 5), (E, 3, 1, 7), (SY, 0, 3, 6),
+    (E, 3, 1, 6), (E, 1, 3, 7), (E, 1, 3, 3), (E, 1, 3, 5), (E, 2, 0, 7), (E, 2, 0, 5),
+    (E, 1, 1, 5), (E, 1, 0, 7), (SI, 3, 1, 7), (E, 1, 0, 5), (E, 2, 0, 3), (E, 1, 1, 7),
+    (SY, 1, 0, 6), (E, 1, 0, 3), (E, 1, 1, 3), (E, 1, 2, 1), (E, 1, 3, 1), (SI, 0, 0, 6),
+    (E, 1, 1, 1), (E, 0, 0, 5), (G, 0, 3, 2), (E, 0, 1, 7), (E, 0, 0, 4), (SY, 0, 2, 0),
+    (E, 1, 0, 1), (E, 3, 2, 5), (E, 3, 2, 4), (SI, 3, 3, 6), (E, 0, 0, 3), (E, 3, 2, 3),
+    (E, 2, 0, 1), (E, 0, 0, 2), (G, 0, 3, 4), (E, 0, 1, 1), (E, 3, 1, 5), (E, 3, 2, 2),
+    (SY, 0, 2, 6), (E, 3, 3, 5), (E, 3, 0, 5), (SI, 0, 3, 4), (E, 3, 0, 4), (E, 3, 0, 3),
+    (E, 3, 1, 3), (E, 3, 3, 3), (E, 3, 1, 4), (G, 0, 3, 6), (E, 3, 0, 2), (E, 3, 3, 4),
+    (SY, 0, 2, 4), (SI, 0, 3, 6), (E, 3, 1, 2), (E, 3, 3, 2), (G, 1, 0, 6), (SI, 3, 1, 6),
+    (SY, 0, 2, 2), (SI, 1, 0, 6), (SY, 1, 2, 4), (G, 3, 2, 1), (G, 0, 2, 6), (SI, 0, 3, 2),
+    (SY, 1, 2, 2), (G, 0, 2, 4), (SI, 3, 0, 6), (G, 0, 0, 1), (SY, 0, 0, 0), (G, 0, 2, 2),
+    (SI, 0, 2, 4), (G, 3, 0, 1), (SY, 3, 0, 0), (G, 3, 1, 1), (SI, 3, 3, 7), (G, 1, 2, 4),
+    (SY, 0, 1, 2), (SI, 0, 2, 6), (G, 1, 2, 2), (SY, 1, 3, 6), (SI, 0, 2, 2), (N, 0, 0, 0),
+    (V, 0, 0, 0), (SY, 1, 2, 6), (X, 0, 0, 0), (SI, 1, 2, 4), (SY, 1, 3, 2), (SI, 1, 2, 2),
+    (G, 0, 1, 2), (N, 0, 3, 0), (X, 0, 3, 0), (SY, 0, 1, 4), (U, 0, 0, 0), (SI, 0, 1, 2),
+    (G, 1, 3, 6), (SY, 2, 0, 6), (AI, 0, 0, 0), (G, 1, 2, 6), (SY, 1, 0, 4), (U, 0, 3, 0),
+    (AI, 0, 3, 0), (G, 1, 3, 2), (AY, 0, 3, 0), (N, 3, 0, 0), (X, 3, 0, 0), (SI, 1, 2, 6),
+    (G, 0, 1, 4), (SY, 2, 0, 4), (G, 3, 3, 1), (SI, 0, 1, 4), (G, 2, 0, 6), (AY, 0, 0, 0),
+    (SI, 2, 0, 6), (G, 1, 0, 4), (U, 3, 0, 0), (SY, 3, 2, 0), (SI, 1, 3, 6), (SY, 1, 3, 4),
+    (AI, 0, 3, 1), (G, 2, 0, 4), (SY, 1, 1, 4), (AI, 3, 0, 0), (N, 0, 2, 0), (X, 0, 2, 0),
+    (SY, 2, 0, 2), (N, 3, 2, 0), (SI, 1, 0, 4), (X, 3, 2, 0), (SY, 3, 3, 0), (SI, 2, 0, 4),
+    (G, 1, 3, 4), (SY, 1, 1, 6), (U, 0, 2, 0), (SI, 1, 3, 4), (G, 1, 1, 4), (SY, 1, 0, 2),
+    (U, 3, 2, 0), (AI, 0, 2, 0), (G, 2, 0, 2), (AY, 0, 2, 0), (N, 3, 3, 0), (AI, 3, 2, 0),
+    (X, 3, 3, 0), (SY, 3, 1, 0), (G, 1, 1, 6), (SI, 1, 1, 6), (SY, 1, 1, 2), (SI, 2, 0, 2),
+    (G, 1, 0, 2), (SY, 1, 2, 0), (U, 3, 3, 0), (SI, 1, 1, 4), (AY, 3, 0, 0), (N, 3, 1, 0),
+    (V, 0, 0, 1), (AI, 3, 3, 0), (X, 3, 1, 0), (AY, 0, 0, 6), (G, 1, 1, 2), (AY, 3, 3, 0),
+    (SI, 1, 3, 2), (SI, 1, 0, 2), (N, 1, 2, 0), (AY, 3, 2, 0), (U, 3, 1, 0), (SI, 1, 1, 2),
+    (SY, 1, 3, 0), (SY, 1, 1, 0), (SI, 0, 0, 5), (SY, 0, 1, 6), (SI, 0, 0, 4), (SY, 1, 0, 0),
+    (SI, 3, 2, 5), (N, 1, 3, 0), (AY, 3, 1, 0), (SI, 3, 2, 4), (SI, 0, 0, 3), (AY, 3, 0, 6),
+    (G, 0, 1, 6), (AY, 3, 2, 6), (SI, 3, 2, 3), (SY, 2, 0, 0), (N, 1, 0, 0), (SI, 0, 0, 2),
+    (N, 1, 1, 0), (X, 1, 0, 0), (SY, 0, 1, 0), (SI, 3, 1, 5), (AY, 3, 3, 6), (SI, 3, 2, 2),
+    (SI, 3, 3, 5), (U, 1, 3, 0), (AY, 1, 3, 0), (U, 1, 1, 0), (U, 1, 0, 0), (SI, 3, 0, 5),
+    (AY, 1, 1, 0), (U, 1, 2, 0), (N, 2, 0, 0), (X, 2, 0, 0), (SI, 3, 0, 4), (AY, 1, 0, 0),
+    (SI, 3, 0, 3), (AY, 1, 2, 0), (SI, 0, 1, 6), (U, 2, 0, 0), (SI, 3, 1, 3), (AY, 1, 1, 2),
+    (SI, 3, 3, 3), (AY, 1, 3, 2), (AI, 1, 1, 0), (AY, 1, 0, 2), (SI, 3, 1, 4), (AY, 2, 0, 0),
+    (SI, 3, 0, 2), (AY, 1, 2, 2), (AI, 1, 2, 0), (AI, 1, 3, 0), (V, 0, 0, 2), (AY, 1, 3, 4),
+    (SI, 3, 3, 4), (AY, 1, 0, 4), (AI, 3, 1, 0), (AY, 1, 1, 4), (SI, 3, 1, 2), (AY, 0, 0, 2),
+    (AI, 2, 0, 0), (AY, 3, 2, 2), (N, 0, 1, 0), (SI, 3, 3, 2), (X, 0, 1, 0), (AY, 1, 2, 4),
+    (AI, 1, 0, 0), (AY, 0, 0, 4), (AI, 0, 2, 1), (U, 0, 1, 0), (AY, 3, 2, 4), (AI, 2, 0, 1),
+    (AY, 1, 1, 6), (AI, 0, 1, 0), (AY, 0, 1, 0), (AY, 3, 0, 2), (AY, 1, 3, 6), (AY, 1, 2, 6),
+    (AI, 0, 1, 1), (AY, 3, 1, 6), (AY, 3, 1, 2), (AY, 3, 0, 4), (AY, 3, 3, 2), (AY, 3, 1, 4),
+    (AY, 1, 0, 6), (AY, 3, 3, 4),
 )
 MID = (
-    (E, 3, 0, 1), (SY, 3, 0, 0), (E, 3, 0, 3), (SY, 3, 0, 2), (E, 3, 0, 5), (E, 3, 0, 7),
-    (E, 0, 3, 5), (E, 0, 3, 1), (SY, 3, 0, 6), (E, 0, 3, 3), (E, 0, 1, 3), (E, 0, 1, 1),
-    (E, 2, 0, 3), (SY, 3, 0, 4), (E, 2, 0, 1), (E, 0, 1, 5), (E, 2, 0, 5), (E, 0, 3, 7),
-    (SY, 0, 3, 6), (E, 0, 1, 7), (E, 2, 0, 7), (E, 1, 0, 1), (SY, 0, 3, 0), (E, 1, 0, 3),
-    (E, 1, 0, 5), (E, 1, 0, 7), (E, 1, 1, 3), (E, 1, 1, 5), (G, 3, 4, 7), (SI, 3, 4, 7),
-    (E, 1, 1, 1), (E, 3, 2, 3), (V, 0, 0, 0), (G, 3, 4, 4), (SI, 3, 4, 4), (SY, 0, 1, 0),
-    (E, 3, 2, 1), (E, 3, 2, 5), (E, 1, 1, 7), (G, 3, 4, 5), (SI, 3, 4, 5), (E, 3, 1, 3),
-    (E, 3, 2, 7), (E, 3, 1, 1), (G, 3, 4, 6), (SI, 3, 4, 6), (E, 3, 1, 5), (E, 3, 1, 7),
-    (SY, 0, 1, 6), (G, 3, 4, 1), (SO, 3, 4, 1), (SY, 2, 0, 6), (G, 3, 3, 7), (SI, 3, 3, 7),
-    (G, 3, 4, 3), (G, 3, 0, 4), (SI, 3, 0, 4), (G, 3, 4, 0), (SO, 3, 4, 0), (SY, 3, 4, 2),
-    (G, 3, 0, 6), (SI, 3, 0, 6), (G, 3, 3, 6), (SI, 3, 3, 6), (SY, 0, 3, 4), (SY, 0, 3, 2),
-    (G, 3, 3, 1), (SO, 3, 3, 1), (G, 0, 3, 6), (SI, 0, 3, 6), (N, 3, 0, 0), (X, 3, 0, 0),
-    (SY, 2, 0, 0), (G, 3, 0, 0), (SO, 3, 0, 0), (N, 3, 4, 0), (X, 3, 4, 0), (G, 0, 0, 6),
-    (SI, 0, 0, 6), (G, 3, 3, 0), (SO, 3, 3, 0), (SY, 1, 0, 6), (G, 0, 1, 6), (SI, 0, 1, 6),
-    (SY, 1, 0, 0), (U, 3, 0, 0), (AO, 3, 0, 2), (AI, 3, 0, 2), (G, 0, 3, 0), (SO, 0, 3, 0),
-    (G, 0, 3, 4), (SI, 0, 3, 4), (U, 3, 4, 0), (AO, 3, 4, 2), (AI, 3, 4, 2), (G, 0, 0, 0),
-    (G, 2, 0, 6), (SO, 0, 0, 0), (AY, 3, 4, 2), (SI, 2, 0, 6), (G, 0, 1, 0), (SO, 0, 1, 0),
-    (G, 0, 0, 7), (SI, 0, 0, 7), (AO, 3, 0, 4), (AY, 3, 0, 2), (AO, 3, 4, 4), (SY, 0, 1, 4),
-    (G, 1, 0, 6), (SI, 1, 0, 6), (SY, 0, 1, 2), (G, 2, 0, 0), (SO, 2, 0, 0), (N, 0, 3, 0),
-    (X, 0, 3, 0), (SY, 1, 1, 6), (AO, 3, 4, 3), (AI, 3, 4, 3), (G, 0, 0, 1), (AO, 3, 0, 3),
-    (SY, 1, 1, 0), (SO, 0, 0, 1), (AI, 3, 0, 3), (AI, 3, 4, 0), (G, 0, 1, 4), (SI, 0, 1, 4),
-    (AI, 3, 0, 0), (U, 0, 3, 0), (AO, 0, 3, 2), (G, 0, 2, 6), (G, 1, 0, 0), (AY, 0, 3, 2),
-    (SO, 1, 0, 0), (SI, 0, 2, 6), (AO, 3, 4, 5), (AI, 0, 3, 2), (G, 1, 1, 6), (SI, 1, 1, 6),
-    (SY, 2, 0, 2), (AO, 3, 0, 5), (G, 0, 2, 7), (SI, 0, 2, 7), (SY, 2, 0, 4), (AO, 3, 4, 6),
-    (G, 0, 2, 0), (AO, 3, 0, 6), (N, 0, 1, 0), (X, 0, 1, 0), (SO, 0, 2, 0), (SY, 3, 2, 6),
-    (AO, 0, 3, 4), (AI, 0, 3, 3), (SY, 3, 2, 0), (AO, 0, 3, 3), (SY, 1, 0, 4), (AI, 0, 3, 0),
-    (G, 3, 3, 5), (U, 0, 1, 0), (AO, 0, 1, 2), (AY, 0, 1, 2), (G, 1, 1, 0), (SI, 3, 3, 5),
-    (G, 3, 3, 4), (V, 0, 0, 1), (SO, 1, 1, 0), (G, 3, 2, 6), (G, 0, 2, 1), (SI, 3, 3, 4),
-    (G, 2, 0, 4), (SO, 0, 2, 1), (SY, 1, 0, 2), (SI, 2, 0, 4), (SI, 3, 2, 6), (SY, 1, 1, 4),
-    (AO, 0, 3, 5), (AI, 0, 1, 2), (AI, 0, 1, 3), (AO, 0, 1, 3), (SY, 1, 1, 2), (G, 1, 0, 4),
-    (N, 2, 0, 0), (AO, 0, 3, 6), (X, 2, 0, 0), (SI, 1, 0, 4), (G, 3, 2, 0), (AI, 0, 1, 0),
-    (SO, 3, 2, 0), (G, 3, 3, 3), (SY, 3, 3, 2), (AO, 0, 1, 4), (U, 2, 0, 0), (AO, 0, 1, 5),
-    (AI, 2, 0, 2), (AY, 2, 0, 2), (AO, 2, 0, 2), (AI, 3, 3, 0), (G, 1, 1, 4), (AY, 3, 3, 0),
-    (SI, 1, 1, 4), (SY, 3, 2, 4), (AO, 0, 1, 6), (N, 3, 3, 0), (X, 3, 3, 0), (SY, 3, 1, 6),
-    (N, 1, 0, 0), (AO, 2, 0, 4), (SY, 3, 1, 0), (AI, 2, 0, 3), (AO, 2, 0, 3), (AY, 3, 3, 6),
-    (AO, 3, 3, 6), (SY, 3, 2, 2), (U, 3, 3, 0), (AI, 3, 3, 2), (AO, 3, 3, 2), (AY, 3, 3, 2),
-    (G, 3, 1, 6), (SI, 3, 1, 6), (N, 1, 1, 0), (X, 1, 0, 0), (SY, 3, 1, 2), (AI, 2, 0, 0),
-    (AO, 2, 0, 5), (SY, 3, 1, 4), (G, 3, 2, 4), (SI, 3, 2, 4), (AO, 3, 3, 4), (AY, 3, 3, 4),
-    (G, 0, 0, 5), (SI, 0, 0, 5), (G, 3, 1, 0), (SO, 3, 1, 0), (U, 1, 0, 0), (AO, 1, 0, 2),
-    (AY, 1, 0, 2), (AI, 1, 0, 2), (U, 1, 1, 0), (AY, 1, 1, 2), (G, 0, 0, 4), (AO, 1, 1, 2),
-    (SI, 0, 0, 4), (AO, 2, 0, 6), (AI, 3, 0, 1), (N, 3, 2, 0), (X, 3, 2, 0), (AI, 3, 4, 1),
-    (AI, 0, 3, 1), (AY, 1, 0, 4), (AI, 0, 1, 1), (AO, 1, 0, 4), (U, 3, 2, 0), (AY, 3, 2, 2),
-    (AI, 1, 1, 2), (AO, 3, 2, 2), (AI, 2, 0, 1), (AY, 1, 0, 0), (AO, 3, 4, 7), (G, 0, 2, 5),
-    (AO, 3, 0, 7), (SI, 0, 2, 5), (V, 0, 0, 2), (AO, 0, 3, 7), (G, 0, 0, 3), (SY, 0, 0, 2),
-    (AO, 0, 1, 7), (AI, 3, 2, 2), (AY, 1, 1, 4), (AO, 1, 1, 4), (AI, 1, 0, 0), (AY, 1, 1, 0),
-    (AO, 2, 0, 7), (AI, 1, 1, 0), (N, 0, 0, 0), (X, 0, 0, 0), (AY, 3, 2, 4), (G, 0, 2, 3),
-    (AO, 3, 2, 4), (SY, 0, 2, 2), (U, 0, 0, 0), (AO, 0, 0, 2), (AI, 0, 0, 2), (AO, 1, 0, 6),
-    (G, 0, 2, 4), (AY, 1, 0, 6), (SI, 0, 2, 4), (G, 3, 1, 4), (AY, 0, 0, 2), (SI, 3, 1, 4),
-    (AO, 1, 1, 6), (AI, 0, 0, 0), (AO, 0, 0, 4), (AY, 0, 0, 4), (AI, 3, 2, 0), (N, 0, 2, 0),
-    (AY, 1, 1, 6), (X, 0, 2, 0), (AI, 0, 2, 0), (N, 3, 1, 0), (X, 3, 1, 0), (AI, 3, 1, 1),
-    (AY, 3, 2, 0), (AO, 0, 0, 6), (AI, 3, 1, 0), (AO, 3, 2, 6), (U, 0, 2, 0), (AI, 0, 2, 2),
-    (AO, 0, 2, 2), (AY, 0, 2, 2), (U, 3, 1, 0), (AI, 3, 1, 2), (AO, 3, 1, 2), (AY, 3, 1, 2),
-    (AO, 0, 2, 6), (AY, 3, 2, 6), (AO, 3, 1, 7), (AY, 0, 0, 6), (AY, 0, 2, 4), (AO, 0, 2, 4),
-    (AI, 3, 1, 3), (AO, 3, 1, 3), (AY, 0, 2, 6), (AO, 3, 1, 4), (AY, 0, 0, 0), (AO, 3, 1, 6),
-    (AY, 0, 2, 0), (AO, 3, 1, 5),
+    (E, 0, 3, 1), (SY, 0, 3, 0), (E, 0, 3, 3), (SY, 0, 3, 2), (E, 0, 3, 5), (E, 0, 3, 7),
+    (E, 0, 2, 1), (E, 0, 2, 5), (E, 0, 2, 3), (SY, 0, 3, 4), (E, 1, 2, 5), (E, 1, 2, 7),
+    (E, 0, 2, 7), (E, 1, 2, 1), (E, 1, 1, 7), (E, 1, 1, 5), (E, 1, 2, 3), (E, 0, 1, 5),
+    (E, 0, 1, 7), (E, 0, 1, 3), (E, 1, 1, 3), (SY, 0, 3, 6), (E, 1, 1, 1), (E, 1, 3, 7),
+    (E, 1, 3, 3), (E, 2, 0, 7), (E, 2, 0, 1), (E, 2, 0, 5), (G, 3, 2, 6), (SI, 3, 2, 6),
+    (E, 1, 0, 7), (E, 1, 0, 1), (E, 1, 0, 5), (SY, 0, 2, 0), (E, 1, 3, 1), (E, 1, 3, 5),
+    (E, 2, 0, 3), (G, 3, 2, 7), (SI, 3, 2, 7), (E, 1, 0, 3), (E, 0, 1, 1), (SY, 1, 2, 4),
+    (G, 0, 0, 7), (SI, 0, 0, 7), (SY, 1, 0, 6), (G, 3, 0, 7), (SI, 3, 0, 7), (G, 3, 2, 0),
+    (SO, 3, 2, 0), (G, 3, 1, 7), (SI, 3, 1, 7), (G, 3, 2, 1), (SY, 0, 2, 4), (SO, 3, 2, 1),
+    (G, 0, 0, 6), (SI, 0, 0, 6), (SY, 0, 2, 2), (G, 0, 0, 1), (SO, 0, 0, 1), (G, 3, 3, 6),
+    (SI, 3, 3, 6), (G, 3, 0, 1), (SY, 1, 0, 0), (SO, 3, 0, 1), (G, 0, 3, 4), (SI, 0, 3, 4),
+    (G, 3, 1, 1), (SO, 3, 1, 1), (SY, 1, 0, 4), (G, 0, 3, 6), (SI, 0, 3, 6), (G, 0, 0, 0),
+    (SO, 0, 0, 0), (SY, 1, 2, 6), (G, 3, 1, 6), (SI, 3, 1, 6), (G, 3, 3, 0), (SO, 3, 3, 0),
+    (SY, 0, 2, 6), (G, 1, 0, 6), (SI, 1, 0, 6), (SY, 0, 1, 4), (N, 0, 3, 0), (V, 0, 0, 0),
+    (X, 0, 3, 0), (G, 0, 3, 0), (SO, 0, 3, 0), (SY, 1, 2, 0), (G, 3, 0, 6), (SI, 3, 0, 6),
+    (G, 3, 1, 0), (SO, 3, 1, 0), (SY, 1, 1, 6), (G, 0, 2, 4), (SI, 0, 2, 4), (G, 1, 0, 0),
+    (SO, 1, 0, 0), (G, 3, 3, 7), (SI, 3, 3, 7), (U, 0, 3, 0), (AY, 0, 3, 2), (AO, 0, 3, 2),
+    (AI, 0, 3, 2), (G, 3, 0, 0), (SO, 3, 0, 0), (G, 0, 2, 6), (SY, 0, 1, 6), (SI, 0, 2, 6),
+    (N, 0, 2, 0), (SY, 2, 0, 6), (X, 0, 2, 0), (G, 3, 3, 1), (SO, 3, 3, 1), (G, 1, 2, 4),
+    (SI, 1, 2, 4), (SY, 1, 3, 6), (AO, 0, 3, 3), (AI, 0, 3, 3), (AO, 0, 3, 4), (SY, 1, 1, 4),
+    (U, 0, 2, 0), (AI, 0, 2, 2), (AO, 0, 2, 2), (G, 0, 2, 0), (SY, 2, 0, 0), (SO, 0, 2, 0),
+    (AI, 0, 0, 0), (SY, 0, 1, 2), (AO, 0, 3, 5), (AI, 0, 3, 0), (SY, 1, 2, 2), (AO, 0, 2, 4),
+    (G, 1, 2, 6), (SI, 1, 2, 6), (AY, 0, 2, 2), (AO, 0, 0, 6), (G, 0, 1, 4), (SI, 0, 1, 4),
+    (AY, 0, 0, 0), (AO, 0, 3, 6), (G, 2, 0, 6), (SI, 2, 0, 6), (SY, 1, 3, 2), (N, 1, 2, 0),
+    (G, 1, 3, 6), (SI, 1, 3, 6), (SY, 2, 0, 4), (G, 1, 2, 0), (SO, 1, 2, 0), (AI, 0, 2, 3),
+    (AO, 0, 2, 3), (N, 0, 1, 0), (X, 0, 1, 0), (SY, 1, 3, 0), (AI, 0, 3, 1), (G, 2, 0, 0),
+    (SO, 2, 0, 0), (AY, 0, 0, 6), (AI, 3, 0, 0), (G, 1, 0, 4), (SY, 1, 3, 4), (SI, 1, 0, 4),
+    (U, 0, 1, 0), (AO, 0, 1, 2), (G, 2, 0, 4), (AO, 0, 2, 5), (AI, 0, 1, 2), (SY, 1, 1, 2),
+    (G, 1, 3, 0), (SO, 1, 3, 0), (SI, 2, 0, 4), (SY, 2, 0, 2), (AO, 0, 3, 7), (AI, 0, 2, 0),
+    (SY, 1, 0, 2), (G, 1, 3, 4), (AO, 3, 0, 6), (AI, 3, 2, 0), (AY, 0, 1, 2), (G, 1, 1, 6),
+    (AO, 0, 1, 4), (SI, 1, 1, 6), (SY, 1, 1, 0), (SI, 1, 3, 4), (N, 2, 0, 0), (X, 2, 0, 0),
+    (AY, 3, 2, 0), (G, 1, 1, 4), (AO, 0, 2, 6), (SI, 1, 1, 4), (AY, 3, 0, 0), (AO, 3, 2, 6),
+    (AI, 3, 3, 0), (AO, 0, 1, 3), (AY, 3, 0, 6), (U, 2, 0, 0), (AO, 2, 0, 2), (AY, 2, 0, 2),
+    (AI, 2, 0, 2), (G, 1, 1, 0), (N, 1, 0, 0), (AY, 3, 3, 0), (SO, 1, 1, 0), (AI, 0, 1, 3),
+    (N, 1, 3, 0), (N, 1, 1, 0), (SY, 0, 1, 0), (X, 1, 0, 0), (AO, 3, 3, 6), (AY, 3, 2, 6),
+    (G, 0, 0, 5), (SI, 0, 0, 5), (AO, 2, 0, 3), (AI, 2, 0, 3), (AY, 3, 3, 6), (AO, 2, 0, 4),
+    (G, 0, 0, 4), (SI, 0, 0, 4), (U, 1, 3, 0), (AY, 1, 3, 2), (U, 1, 2, 0), (AO, 0, 1, 5),
+    (G, 3, 2, 5), (U, 1, 1, 0), (V, 0, 0, 1), (AY, 1, 2, 2), (SI, 3, 2, 5), (U, 1, 0, 0),
+    (G, 3, 2, 4), (AO, 1, 2, 2), (SI, 3, 2, 4), (AY, 1, 1, 2), (G, 0, 0, 3), (AO, 1, 1, 2),
+    (AI, 1, 3, 2), (AY, 1, 0, 2), (AI, 1, 2, 2), (AO, 1, 3, 2), (SY, 0, 0, 2), (G, 3, 2, 3),
+    (AI, 1, 0, 2), (AO, 1, 0, 2), (G, 3, 1, 5), (SY, 3, 2, 2), (AI, 1, 1, 2), (AO, 2, 0, 5),
+    (AY, 1, 3, 4), (G, 3, 3, 5), (SI, 3, 3, 5), (AO, 1, 3, 4), (G, 3, 0, 5), (AY, 1, 2, 4),
+    (SI, 3, 0, 5), (AO, 1, 2, 4), (G, 3, 0, 4), (N, 0, 0, 0), (X, 0, 0, 0), (AY, 1, 0, 4),
+    (SI, 3, 1, 5), (N, 3, 2, 0), (AO, 1, 0, 4), (X, 3, 2, 0), (SI, 3, 0, 4), (AY, 1, 1, 4),
+    (G, 0, 1, 6), (AO, 1, 1, 4), (SI, 0, 1, 6), (U, 0, 0, 0), (AY, 0, 0, 2), (AI, 0, 0, 2),
+    (G, 3, 0, 3), (AO, 0, 0, 2), (SY, 3, 0, 2), (G, 3, 3, 3), (U, 3, 2, 0), (G, 3, 1, 3),
+    (AI, 3, 2, 2), (AO, 3, 2, 2), (SY, 3, 1, 2), (AI, 1, 1, 0), (AY, 1, 1, 0), (G, 3, 1, 4),
+    (G, 0, 1, 0), (SO, 0, 1, 0), (SI, 3, 1, 4), (AY, 3, 2, 2), (AO, 0, 0, 4), (N, 3, 0, 0),
+    (X, 3, 0, 0), (AY, 1, 2, 0), (AI, 1, 2, 0), (AO, 3, 2, 4), (SY, 3, 3, 2), (AI, 1, 3, 0),
+    (AO, 1, 1, 6), (AY, 1, 3, 0), (G, 3, 3, 4), (SI, 3, 3, 4), (U, 3, 0, 0), (AO, 3, 0, 2),
+    (AY, 0, 0, 4), (AI, 3, 0, 2), (AO, 1, 2, 6), (V, 0, 0, 2), (AI, 3, 1, 0), (N, 3, 1, 0),
+    (X, 3, 1, 0), (AY, 3, 1, 0), (AO, 1, 3, 6), (AI, 2, 0, 0), (AY, 1, 3, 6), (N, 3, 3, 0),
+    (AY, 1, 2, 6), (X, 3, 3, 0), (AO, 3, 0, 4), (U, 3, 1, 0), (AO, 3, 1, 2), (AI, 3, 1, 2),
+    (AI, 1, 0, 0), (AY, 1, 1, 6), (AO, 3, 1, 6), (AI, 0, 2, 1), (AY, 3, 0, 2), (AO, 2, 0, 6),
+    (U, 3, 3, 0), (AI, 3, 3, 2), (AO, 3, 3, 2), (AY, 3, 2, 4), (AI, 2, 0, 1), (AO, 3, 1, 4),
+    (AY, 3, 3, 2), (AI, 0, 1, 0), (AO, 1, 0, 6), (AY, 3, 1, 2), (AO, 0, 2, 7), (AY, 3, 0, 4),
+    (AY, 1, 0, 0), (AO, 3, 3, 4), (AY, 1, 0, 6), (AI, 0, 1, 1), (AO, 2, 0, 7), (AY, 3, 3, 4),
+    (AO, 0, 1, 6), (AY, 3, 1, 4), (AY, 3, 1, 6), (AO, 0, 1, 7),
 )
 
 
@@ -230,23 +237,38 @@
         pltpu.make_async_copy(ref, ref, sem).wait()
 
     barrier = pltpu.get_barrier_semaphore()
-    for j in range(1, replicas):
-        pl.semaphore_signal(barrier, inc=1, device_id={"replica": lax.rem(r + j, replicas)}, device_id_type=MESH)
+
+    def greet(axis, to):
+        pl.semaphore_signal(barrier, inc=1, device_id={axis: to}, device_id_type=MESH)
+
+    @pl.when(z > 0)
+    def _():
+        greet("replica", r - 2)
+
+    @pl.when(z < 3)
+    def _():
+        greet("replica", r + 2)
+
+    greet("replica", z * 2 + (1 - y))
     for j in range(1, models):
-        pl.semaphore_signal(barrier, inc=1, device_id={"model": lax.rem(m + j, models)}, device_id_type=MESH)
+        greet("model", lax.rem(m + j, models))
 
     def chunk_of(g, c):
         return xin[g].at[:, rows(g, c)] if GROUPS[g].rows else xin[g].at[rows(g, c)]
 
-    for g, c in CHUNKS:
+    def load(g, c):
         for i, a in enumerate(GROUPS[g].members):
             src = slopes[a].at[:, rows(g, c)] if GROUPS[g].rows else slopes[a].at[rows(g, c)]
             pltpu.make_async_copy(src, lanes(g, chunk_of(g, c), i), load_sem.at[at[g, c]]).start()
-    for g in OWN:
-        for i, a in enumerate(GROUPS[g].members):
-            pltpu.make_async_copy(params[a], lanes(g, own[g], i), own_sem.at[g]).start()
-            pltpu.make_async_copy(states[a], lanes(g, st[g], i), st_sem.at[g]).start()
-
+
+    def load_own():
+        for g in OWN:
+            for i, a in enumerate(GROUPS[g].members):
+                pltpu.make_async_copy(params[a], lanes(g, own[g], i), own_sem.at[g]).start()
+                pltpu.make_async_copy(states[a], lanes(g, st[g], i), st_sem.at[g]).start()
+
+    for g, c in CHUNKS[:2]:
+        load(g, c)
     vs[0:1, :] = slope_norm[...]
     vs[1:2, :] = slope_bias[...]
     for g in groups:
@@ -319,6 +341,7 @@
             peers[SI] = peers[AI] = (1 + side) * 2 + y
         peers[SY] = peers[AY] = z * 2 + (1 - y)
         done = set()
+        ahead = list(CHUNKS[2:])
 
         def kind(g, c):
             return SUMS[g][c]
@@ -378,6 +401,10 @@
                 whole(ref, sem)
 
         def loaded(g, c):
+            while (g, c) in ahead:
+                load(*ahead.pop(0))
+                if not ahead:
+                    load_own()
             once((-1, g, c), chunk_of(g, c), load_sem.at[at[g, c]])
 
         def parts(g, c, s):
@@ -505,10 +532,14 @@
             loop(g, c, body)
 
         met = False
-        for op, g, c, s in order:
+        for i, (op, g, c, s) in enumerate(order):
+            if ahead and i % 2:
+                load(*ahead.pop(0))
+                if not ahead:
+                    load_own()
             if op not in (E, G) and not met:
                 met = True
-                pl.semaphore_wait(barrier, replicas + models - 2)
+                pl.semaphore_wait(barrier, models + (2 if mid else 1))
             if op == E:
                 encode_op(g, c, s, SY if kind(g, c) == A else SI)
             elif op == G:

time: 120 us -> 118 us (0.983)
  Pallas kernels: 119 us -> 117 us
    pallas_call x1, Pallas kernels: 116 us -> 113 us  [fused(): pl.pallas_call(functools.partial(kernel, replicas, models, 4.0, shapes),...]
where the time goes in v3:
time: 118 us
  Pallas kernels  117 us (99%)
    pallas_call x1, Pallas kernels, fused(): pl.pallas_call(functools.partial(kernel, replicas, models, 4.0, shapes),...  113 us
    pallas_call x1, Pallas kernels, fused(): pl.pallas_call(functools.partial(finish, shapes), out_shape=outs, in_spec...  3.78 us

profile of v3, /device:TPU:0, one launch (start us, length us, event | category | flops | bytes accessed | tf_op | source)
XLA Modules:
  0.0 118.0 jit_solution(6268015325565937808)
XLA Ops:
  0.7 113.4 %shard_map.415 = (bf16[8,128,1024]{2,1,0:T(8,128)(2,1)S(1)}, bf16[8,1024,128]{2,1,0:T(8,128)(2,1)S(1)}, bf16[8,256,128]{2,1,0:T(8,128)(2,1)S(1)}, bf16[8,128,768...) custom-call(f32[8,128,1024]{2,1,0:T(8,128)} %bitcast.20, ...), custom_call_target="tpu_custom_call" | custom-call | tf_op jit(solution)/shard_map/pallas_call | solution.py:628
  114.1 3.8 %shard_map.416 = (bf16[8,128,1024]{2,1,0:T(8,128)(2,1)}, bf16[1024,1024]{1,0:T(8,128)(2,1)}, bf16[8,128,256]{2,1,0:T(8,128)(2,1)}, bf16[8,128,256]{2,1,0:T(8,128...) custom-call(bf16[8,128,1024]{2,1,0:T(8,128)(2,1)S(1)} %get-tuple-ele, ...), custom_call_target="tpu_custom_call" | custom-call | tf_op jit(solution)/shard_map/pallas_call | solution.py:645

commit v4 on v3

--- a/solution.py
+++ b/solution.py
@@ -23,120 +23,120 @@
 A, B = 0, 1
 E, G, N, X, U, V, SY, SI, SO, AY, AI, AO = range(12)
 SIZES = ((2, 2, 2, 2), (2, 2, 2, 2), (8,), (2, 2, 2, 2))
-SUMS = ((B, A, A, A), (A, A, A, A), (A,), (B, B, B, B))
-BACK = ((A, B, B, B), (A, A, A, A), (B,), (A, A, A, A))
-CHUNKS = ((0, 3), (3, 2), (0, 0), (3, 0), (0, 2), (1, 2), (1, 1), (3, 3), (0, 1), (3, 1), (1, 3), (2, 0), (1, 0))
-OWN = (0, 3, 1, 2)
+SUMS = ((B, B, B, A), (A, A, A, A), (A,), (A, B, B, A))
+BACK = ((A, A, A, A), (A, B, A, A), (B,), (B, A, A, B))
+CHUNKS = ((3, 2), (3, 0), (3, 1), (2, 0), (3, 3), (1, 3), (0, 0), (1, 0), (0, 3), (1, 2), (0, 1), (1, 1), (0, 2))
+OWN = (3, 2, 0, 1)
 SENT = (((4, 1, 0), (1, 2, 0)), ((4, 2, 3), (1, 4, 6)))
 STEP = 16384
 END = (
-    (E, 0, 3, 1), (SY, 0, 3, 0), (E, 0, 3, 3), (SY, 0, 3, 2), (E, 3, 2, 6), (SI, 3, 2, 6),
-    (E, 3, 2, 7), (SI, 3, 2, 7), (E, 0, 3, 5), (E, 0, 0, 7), (E, 0, 3, 7), (E, 3, 0, 7),
-    (E, 0, 0, 6), (E, 0, 2, 1), (E, 0, 2, 7), (E, 0, 2, 5), (SY, 0, 3, 4), (SI, 0, 0, 7),
-    (E, 0, 2, 3), (E, 1, 2, 5), (E, 1, 2, 3), (E, 3, 0, 6), (E, 3, 3, 6), (E, 3, 3, 7),
-    (E, 1, 2, 7), (SI, 3, 0, 7), (E, 0, 1, 3), (E, 0, 1, 5), (E, 3, 1, 7), (SY, 0, 3, 6),
-    (E, 3, 1, 6), (E, 1, 3, 7), (E, 1, 3, 3), (E, 1, 3, 5), (E, 2, 0, 7), (E, 2, 0, 5),
-    (E, 1, 1, 5), (E, 1, 0, 7), (SI, 3, 1, 7), (E, 1, 0, 5), (E, 2, 0, 3), (E, 1, 1, 7),
-    (SY, 1, 0, 6), (E, 1, 0, 3), (E, 1, 1, 3), (E, 1, 2, 1), (E, 1, 3, 1), (SI, 0, 0, 6),
-    (E, 1, 1, 1), (E, 0, 0, 5), (G, 0, 3, 2), (E, 0, 1, 7), (E, 0, 0, 4), (SY, 0, 2, 0),
-    (E, 1, 0, 1), (E, 3, 2, 5), (E, 3, 2, 4), (SI, 3, 3, 6), (E, 0, 0, 3), (E, 3, 2, 3),
-    (E, 2, 0, 1), (E, 0, 0, 2), (G, 0, 3, 4), (E, 0, 1, 1), (E, 3, 1, 5), (E, 3, 2, 2),
-    (SY, 0, 2, 6), (E, 3, 3, 5), (E, 3, 0, 5), (SI, 0, 3, 4), (E, 3, 0, 4), (E, 3, 0, 3),
-    (E, 3, 1, 3), (E, 3, 3, 3), (E, 3, 1, 4), (G, 0, 3, 6), (E, 3, 0, 2), (E, 3, 3, 4),
-    (SY, 0, 2, 4), (SI, 0, 3, 6), (E, 3, 1, 2), (E, 3, 3, 2), (G, 1, 0, 6), (SI, 3, 1, 6),
-    (SY, 0, 2, 2), (SI, 1, 0, 6), (SY, 1, 2, 4), (G, 3, 2, 1), (G, 0, 2, 6), (SI, 0, 3, 2),
-    (SY, 1, 2, 2), (G, 0, 2, 4), (SI, 3, 0, 6), (G, 0, 0, 1), (SY, 0, 0, 0), (G, 0, 2, 2),
-    (SI, 0, 2, 4), (G, 3, 0, 1), (SY, 3, 0, 0), (G, 3, 1, 1), (SI, 3, 3, 7), (G, 1, 2, 4),
-    (SY, 0, 1, 2), (SI, 0, 2, 6), (G, 1, 2, 2), (SY, 1, 3, 6), (SI, 0, 2, 2), (N, 0, 0, 0),
-    (V, 0, 0, 0), (SY, 1, 2, 6), (X, 0, 0, 0), (SI, 1, 2, 4), (SY, 1, 3, 2), (SI, 1, 2, 2),
-    (G, 0, 1, 2), (N, 0, 3, 0), (X, 0, 3, 0), (SY, 0, 1, 4), (U, 0, 0, 0), (SI, 0, 1, 2),
-    (G, 1, 3, 6), (SY, 2, 0, 6), (AI, 0, 0, 0), (G, 1, 2, 6), (SY, 1, 0, 4), (U, 0, 3, 0),
-    (AI, 0, 3, 0), (G, 1, 3, 2), (AY, 0, 3, 0), (N, 3, 0, 0), (X, 3, 0, 0), (SI, 1, 2, 6),
-    (G, 0, 1, 4), (SY, 2, 0, 4), (G, 3, 3, 1), (SI, 0, 1, 4), (G, 2, 0, 6), (AY, 0, 0, 0),
-    (SI, 2, 0, 6), (G, 1, 0, 4), (U, 3, 0, 0), (SY, 3, 2, 0), (SI, 1, 3, 6), (SY, 1, 3, 4),
-    (AI, 0, 3, 1), (G, 2, 0, 4), (SY, 1, 1, 4), (AI, 3, 0, 0), (N, 0, 2, 0), (X, 0, 2, 0),
-    (SY, 2, 0, 2), (N, 3, 2, 0), (SI, 1, 0, 4), (X, 3, 2, 0), (SY, 3, 3, 0), (SI, 2, 0, 4),
-    (G, 1, 3, 4), (SY, 1, 1, 6), (U, 0, 2, 0), (SI, 1, 3, 4), (G, 1, 1, 4), (SY, 1, 0, 2),
-    (U, 3, 2, 0), (AI, 0, 2, 0), (G, 2, 0, 2), (AY, 0, 2, 0), (N, 3, 3, 0), (AI, 3, 2, 0),
-    (X, 3, 3, 0), (SY, 3, 1, 0), (G, 1, 1, 6), (SI, 1, 1, 6), (SY, 1, 1, 2), (SI, 2, 0, 2),
-    (G, 1, 0, 2), (SY, 1, 2, 0), (U, 3, 3, 0), (SI, 1, 1, 4), (AY, 3, 0, 0), (N, 3, 1, 0),
-    (V, 0, 0, 1), (AI, 3, 3, 0), (X, 3, 1, 0), (AY, 0, 0, 6), (G, 1, 1, 2), (AY, 3, 3, 0),
-    (SI, 1, 3, 2), (SI, 1, 0, 2), (N, 1, 2, 0), (AY, 3, 2, 0), (U, 3, 1, 0), (SI, 1, 1, 2),
-    (SY, 1, 3, 0), (SY, 1, 1, 0), (SI, 0, 0, 5), (SY, 0, 1, 6), (SI, 0, 0, 4), (SY, 1, 0, 0),
-    (SI, 3, 2, 5), (N, 1, 3, 0), (AY, 3, 1, 0), (SI, 3, 2, 4), (SI, 0, 0, 3), (AY, 3, 0, 6),
-    (G, 0, 1, 6), (AY, 3, 2, 6), (SI, 3, 2, 3), (SY, 2, 0, 0), (N, 1, 0, 0), (SI, 0, 0, 2),
-    (N, 1, 1, 0), (X, 1, 0, 0), (SY, 0, 1, 0), (SI, 3, 1, 5), (AY, 3, 3, 6), (SI, 3, 2, 2),
-    (SI, 3, 3, 5), (U, 1, 3, 0), (AY, 1, 3, 0), (U, 1, 1, 0), (U, 1, 0, 0), (SI, 3, 0, 5),
-    (AY, 1, 1, 0), (U, 1, 2, 0), (N, 2, 0, 0), (X, 2, 0, 0), (SI, 3, 0, 4), (AY, 1, 0, 0),
-    (SI, 3, 0, 3), (AY, 1, 2, 0), (SI, 0, 1, 6), (U, 2, 0, 0), (SI, 3, 1, 3), (AY, 1, 1, 2),
-    (SI, 3, 3, 3), (AY, 1, 3, 2), (AI, 1, 1, 0), (AY, 1, 0, 2), (SI, 3, 1, 4), (AY, 2, 0, 0),
-    (SI, 3, 0, 2), (AY, 1, 2, 2), (AI, 1, 2, 0), (AI, 1, 3, 0), (V, 0, 0, 2), (AY, 1, 3, 4),
-    (SI, 3, 3, 4), (AY, 1, 0, 4), (AI, 3, 1, 0), (AY, 1, 1, 4), (SI, 3, 1, 2), (AY, 0, 0, 2),
-    (AI, 2, 0, 0), (AY, 3, 2, 2), (N, 0, 1, 0), (SI, 3, 3, 2), (X, 0, 1, 0), (AY, 1, 2, 4),
-    (AI, 1, 0, 0), (AY, 0, 0, 4), (AI, 0, 2, 1), (U, 0, 1, 0), (AY, 3, 2, 4), (AI, 2, 0, 1),
-    (AY, 1, 1, 6), (AI, 0, 1, 0), (AY, 0, 1, 0), (AY, 3, 0, 2), (AY, 1, 3, 6), (AY, 1, 2, 6),
-    (AI, 0, 1, 1), (AY, 3, 1, 6), (AY, 3, 1, 2), (AY, 3, 0, 4), (AY, 3, 3, 2), (AY, 3, 1, 4),
-    (AY, 1, 0, 6), (AY, 3, 3, 4),
+    (E, 3, 2, 6), (SI, 3, 2, 6), (E, 3, 2, 7), (SI, 3, 2, 7), (E, 3, 0, 3), (SY, 3, 0, 2),
+    (E, 3, 0, 5), (SY, 3, 0, 4), (E, 3, 1, 7), (E, 3, 1, 6), (E, 2, 0, 5), (E, 2, 0, 3),
+    (SI, 3, 1, 7), (E, 3, 3, 3), (E, 3, 3, 7), (SY, 2, 0, 4), (E, 2, 0, 7), (E, 3, 3, 1),
+    (E, 0, 0, 7), (E, 2, 0, 1), (E, 3, 3, 5), (SI, 0, 0, 7), (E, 1, 0, 5), (E, 0, 0, 6),
+    (SY, 3, 3, 2), (E, 1, 3, 7), (E, 0, 3, 7), (E, 1, 2, 7), (E, 1, 3, 5), (E, 0, 1, 7),
+    (SI, 0, 1, 7), (E, 0, 1, 6), (E, 1, 1, 7), (E, 1, 1, 5), (E, 0, 2, 7), (SY, 2, 0, 2),
+    (E, 1, 2, 5), (E, 3, 0, 7), (G, 3, 0, 2), (E, 1, 3, 3), (E, 1, 0, 3), (SI, 3, 1, 6),
+    (E, 1, 1, 3), (E, 1, 2, 3), (SY, 3, 3, 6), (E, 0, 2, 5), (E, 1, 0, 7), (G, 3, 0, 4),
+    (E, 0, 3, 1), (E, 0, 3, 3), (E, 3, 1, 4), (SI, 3, 0, 4), (E, 1, 3, 1), (E, 3, 1, 5),
+    (SY, 2, 0, 6), (E, 0, 3, 5), (E, 0, 2, 4), (G, 2, 0, 4), (E, 3, 0, 1), (E, 0, 1, 5),
+    (SI, 0, 2, 7), (E, 1, 1, 1), (E, 0, 2, 3), (SY, 3, 3, 0), (E, 0, 2, 2), (E, 3, 1, 2),
+    (G, 3, 3, 2), (E, 1, 2, 1), (SI, 0, 1, 6), (E, 3, 1, 3), (E, 1, 0, 1), (E, 0, 1, 3),
+    (E, 0, 1, 4), (E, 0, 0, 5), (SY, 2, 0, 0), (E, 0, 1, 2), (E, 0, 2, 6), (G, 2, 0, 2),
+    (E, 0, 0, 4), (SI, 2, 0, 4), (E, 0, 0, 3), (E, 0, 0, 2), (SY, 3, 3, 4), (E, 3, 2, 5),
+    (E, 3, 2, 4), (G, 3, 3, 6), (E, 3, 2, 3), (E, 3, 2, 2), (SI, 3, 0, 2), (SY, 1, 0, 4),
+    (G, 2, 0, 6), (SY, 1, 2, 6), (SI, 0, 0, 6), (G, 3, 2, 1), (SI, 2, 0, 6), (SY, 1, 1, 6),
+    (G, 3, 1, 1), (SI, 3, 3, 6), (G, 3, 3, 4), (SY, 3, 1, 0), (SI, 2, 0, 2), (G, 0, 0, 1),
+    (G, 1, 0, 4), (SY, 1, 3, 6), (SI, 3, 3, 4), (SY, 1, 1, 4), (G, 0, 1, 1), (G, 1, 2, 6),
+    (SI, 1, 0, 4), (SY, 0, 3, 6), (G, 1, 1, 6), (SI, 3, 3, 2), (N, 3, 1, 0), (V, 0, 0, 0),
+    (SY, 1, 3, 4), (X, 3, 1, 0), (SI, 1, 2, 6), (G, 0, 2, 1), (G, 1, 3, 6), (SY, 3, 2, 0),
+    (SI, 1, 1, 6), (G, 1, 1, 4), (SY, 1, 2, 4), (SI, 1, 3, 6), (SY, 3, 0, 6), (U, 3, 1, 0),
+    (G, 0, 3, 6), (AI, 3, 1, 0), (SY, 1, 3, 2), (G, 1, 3, 4), (SI, 1, 3, 4), (SY, 1, 0, 2),
+    (N, 3, 2, 0), (X, 3, 2, 0), (SI, 1, 1, 4), (N, 2, 0, 0), (SY, 1, 1, 2), (X, 2, 0, 0),
+    (G, 1, 2, 4), (SI, 1, 2, 4), (N, 3, 3, 0), (X, 3, 3, 0), (G, 3, 0, 6), (SY, 1, 2, 2),
+    (SI, 0, 2, 5), (U, 3, 2, 0), (SY, 0, 1, 0), (G, 1, 3, 2), (SI, 1, 3, 2), (U, 2, 0, 0),
+    (G, 1, 0, 2), (AY, 3, 2, 0), (U, 3, 3, 0), (SI, 3, 0, 6), (G, 1, 1, 2), (SY, 1, 0, 6),
+    (SI, 1, 1, 2), (SY, 0, 3, 0), (G, 1, 2, 2), (SI, 1, 0, 2), (SY, 0, 2, 0), (N, 0, 1, 0),
+    (X, 0, 1, 0), (SI, 1, 2, 2), (SY, 0, 3, 2), (SI, 3, 1, 4), (G, 1, 0, 6), (SY, 1, 3, 0),
+    (SI, 3, 1, 5), (SY, 0, 3, 4), (U, 0, 1, 0), (AI, 3, 2, 0), (SY, 3, 0, 0), (SI, 0, 2, 4),
+    (SI, 0, 1, 5), (G, 0, 3, 2), (AY, 3, 3, 0), (SY, 1, 1, 0), (SI, 0, 2, 3), (N, 1, 3, 0),
+    (V, 0, 0, 1), (AY, 2, 0, 0), (SI, 0, 2, 2), (G, 0, 3, 4), (SY, 0, 0, 0), (AI, 0, 1, 0),
+    (AY, 3, 1, 0), (SI, 1, 0, 6), (N, 1, 1, 0), (AY, 0, 1, 0), (N, 3, 0, 0), (SI, 3, 1, 2),
+    (X, 3, 0, 0), (SY, 1, 2, 0), (SI, 3, 1, 3), (SY, 1, 0, 0), (N, 0, 0, 0), (SI, 0, 1, 3),
+    (X, 0, 0, 0), (AY, 3, 1, 6), (SI, 0, 1, 4), (U, 3, 0, 0), (AY, 1, 0, 2), (SI, 0, 0, 5),
+    (AY, 1, 2, 2), (N, 1, 2, 0), (AI, 3, 3, 1), (U, 0, 0, 0), (AY, 0, 0, 0), (SI, 0, 1, 2),
+    (AY, 3, 2, 6), (SI, 0, 3, 4), (AY, 1, 3, 2), (SI, 0, 2, 6), (AY, 1, 0, 4), (SI, 0, 3, 6),
+    (AY, 3, 0, 0), (SI, 0, 0, 4), (AY, 1, 3, 4), (SI, 0, 3, 2), (AY, 1, 2, 4), (AI, 0, 0, 0),
+    (AY, 0, 1, 6), (SI, 0, 0, 3), (N, 1, 0, 0), (X, 1, 0, 0), (AY, 0, 2, 2), (AI, 3, 3, 0),
+    (AI, 2, 0, 1), (AY, 0, 2, 4), (SI, 0, 0, 2), (AY, 3, 1, 2), (U, 1, 0, 0), (U, 1, 2, 0),
+    (AY, 1, 0, 0), (U, 1, 1, 0), (U, 1, 3, 0), (SI, 3, 2, 5), (AY, 1, 2, 0), (AI, 3, 0, 0),
+    (AY, 0, 1, 2), (AI, 1, 0, 0), (N, 0, 2, 0), (X, 0, 2, 0), (V, 0, 0, 2), (AY, 1, 1, 0),
+    (SI, 3, 2, 4), (AY, 1, 3, 0), (SI, 3, 2, 3), (N, 0, 3, 0), (X, 0, 3, 0), (AI, 1, 3, 0),
+    (AY, 3, 1, 4), (U, 0, 2, 0), (AI, 0, 2, 0), (AY, 0, 2, 0), (SI, 3, 2, 2), (AY, 0, 3, 2),
+    (U, 0, 3, 0), (AI, 1, 2, 0), (AY, 0, 1, 4), (AI, 0, 3, 0), (AY, 0, 3, 0), (AI, 3, 0, 1),
+    (AY, 0, 0, 6), (AI, 2, 0, 0), (AY, 0, 3, 4), (AI, 1, 1, 0), (AY, 0, 0, 2), (AI, 1, 1, 1),
+    (AY, 1, 0, 6), (AY, 0, 0, 4), (AY, 1, 3, 6), (AY, 0, 2, 6), (AY, 3, 2, 2), (AY, 1, 2, 6),
+    (AY, 0, 3, 6), (AY, 3, 2, 4),
 )
 MID = (
-    (E, 0, 3, 1), (SY, 0, 3, 0), (E, 0, 3, 3), (SY, 0, 3, 2), (E, 0, 3, 5), (E, 0, 3, 7),
-    (E, 0, 2, 1), (E, 0, 2, 5), (E, 0, 2, 3), (SY, 0, 3, 4), (E, 1, 2, 5), (E, 1, 2, 7),
-    (E, 0, 2, 7), (E, 1, 2, 1), (E, 1, 1, 7), (E, 1, 1, 5), (E, 1, 2, 3), (E, 0, 1, 5),
-    (E, 0, 1, 7), (E, 0, 1, 3), (E, 1, 1, 3), (SY, 0, 3, 6), (E, 1, 1, 1), (E, 1, 3, 7),
-    (E, 1, 3, 3), (E, 2, 0, 7), (E, 2, 0, 1), (E, 2, 0, 5), (G, 3, 2, 6), (SI, 3, 2, 6),
-    (E, 1, 0, 7), (E, 1, 0, 1), (E, 1, 0, 5), (SY, 0, 2, 0), (E, 1, 3, 1), (E, 1, 3, 5),
-    (E, 2, 0, 3), (G, 3, 2, 7), (SI, 3, 2, 7), (E, 1, 0, 3), (E, 0, 1, 1), (SY, 1, 2, 4),
-    (G, 0, 0, 7), (SI, 0, 0, 7), (SY, 1, 0, 6), (G, 3, 0, 7), (SI, 3, 0, 7), (G, 3, 2, 0),
-    (SO, 3, 2, 0), (G, 3, 1, 7), (SI, 3, 1, 7), (G, 3, 2, 1), (SY, 0, 2, 4), (SO, 3, 2, 1),
-    (G, 0, 0, 6), (SI, 0, 0, 6), (SY, 0, 2, 2), (G, 0, 0, 1), (SO, 0, 0, 1), (G, 3, 3, 6),
-    (SI, 3, 3, 6), (G, 3, 0, 1), (SY, 1, 0, 0), (SO, 3, 0, 1), (G, 0, 3, 4), (SI, 0, 3, 4),
-    (G, 3, 1, 1), (SO, 3, 1, 1), (SY, 1, 0, 4), (G, 0, 3, 6), (SI, 0, 3, 6), (G, 0, 0, 0),
-    (SO, 0, 0, 0), (SY, 1, 2, 6), (G, 3, 1, 6), (SI, 3, 1, 6), (G, 3, 3, 0), (SO, 3, 3, 0),
-    (SY, 0, 2, 6), (G, 1, 0, 6), (SI, 1, 0, 6), (SY, 0, 1, 4), (N, 0, 3, 0), (V, 0, 0, 0),
-    (X, 0, 3, 0), (G, 0, 3, 0), (SO, 0, 3, 0), (SY, 1, 2, 0), (G, 3, 0, 6), (SI, 3, 0, 6),
-    (G, 3, 1, 0), (SO, 3, 1, 0), (SY, 1, 1, 6), (G, 0, 2, 4), (SI, 0, 2, 4), (G, 1, 0, 0),
-    (SO, 1, 0, 0), (G, 3, 3, 7), (SI, 3, 3, 7), (U, 0, 3, 0), (AY, 0, 3, 2), (AO, 0, 3, 2),
-    (AI, 0, 3, 2), (G, 3, 0, 0), (SO, 3, 0, 0), (G, 0, 2, 6), (SY, 0, 1, 6), (SI, 0, 2, 6),
-    (N, 0, 2, 0), (SY, 2, 0, 6), (X, 0, 2, 0), (G, 3, 3, 1), (SO, 3, 3, 1), (G, 1, 2, 4),
-    (SI, 1, 2, 4), (SY, 1, 3, 6), (AO, 0, 3, 3), (AI, 0, 3, 3), (AO, 0, 3, 4), (SY, 1, 1, 4),
-    (U, 0, 2, 0), (AI, 0, 2, 2), (AO, 0, 2, 2), (G, 0, 2, 0), (SY, 2, 0, 0), (SO, 0, 2, 0),
-    (AI, 0, 0, 0), (SY, 0, 1, 2), (AO, 0, 3, 5), (AI, 0, 3, 0), (SY, 1, 2, 2), (AO, 0, 2, 4),
-    (G, 1, 2, 6), (SI, 1, 2, 6), (AY, 0, 2, 2), (AO, 0, 0, 6), (G, 0, 1, 4), (SI, 0, 1, 4),
-    (AY, 0, 0, 0), (AO, 0, 3, 6), (G, 2, 0, 6), (SI, 2, 0, 6), (SY, 1, 3, 2), (N, 1, 2, 0),
-    (G, 1, 3, 6), (SI, 1, 3, 6), (SY, 2, 0, 4), (G, 1, 2, 0), (SO, 1, 2, 0), (AI, 0, 2, 3),
-    (AO, 0, 2, 3), (N, 0, 1, 0), (X, 0, 1, 0), (SY, 1, 3, 0), (AI, 0, 3, 1), (G, 2, 0, 0),
-    (SO, 2, 0, 0), (AY, 0, 0, 6), (AI, 3, 0, 0), (G, 1, 0, 4), (SY, 1, 3, 4), (SI, 1, 0, 4),
-    (U, 0, 1, 0), (AO, 0, 1, 2), (G, 2, 0, 4), (AO, 0, 2, 5), (AI, 0, 1, 2), (SY, 1, 1, 2),
-    (G, 1, 3, 0), (SO, 1, 3, 0), (SI, 2, 0, 4), (SY, 2, 0, 2), (AO, 0, 3, 7), (AI, 0, 2, 0),
-    (SY, 1, 0, 2), (G, 1, 3, 4), (AO, 3, 0, 6), (AI, 3, 2, 0), (AY, 0, 1, 2), (G, 1, 1, 6),
-    (AO, 0, 1, 4), (SI, 1, 1, 6), (SY, 1, 1, 0), (SI, 1, 3, 4), (N, 2, 0, 0), (X, 2, 0, 0),
-    (AY, 3, 2, 0), (G, 1, 1, 4), (AO, 0, 2, 6), (SI, 1, 1, 4), (AY, 3, 0, 0), (AO, 3, 2, 6),
-    (AI, 3, 3, 0), (AO, 0, 1, 3), (AY, 3, 0, 6), (U, 2, 0, 0), (AO, 2, 0, 2), (AY, 2, 0, 2),
-    (AI, 2, 0, 2), (G, 1, 1, 0), (N, 1, 0, 0), (AY, 3, 3, 0), (SO, 1, 1, 0), (AI, 0, 1, 3),
-    (N, 1, 3, 0), (N, 1, 1, 0), (SY, 0, 1, 0), (X, 1, 0, 0), (AO, 3, 3, 6), (AY, 3, 2, 6),
-    (G, 0, 0, 5), (SI, 0, 0, 5), (AO, 2, 0, 3), (AI, 2, 0, 3), (AY, 3, 3, 6), (AO, 2, 0, 4),
-    (G, 0, 0, 4), (SI, 0, 0, 4), (U, 1, 3, 0), (AY, 1, 3, 2), (U, 1, 2, 0), (AO, 0, 1, 5),
-    (G, 3, 2, 5), (U, 1, 1, 0), (V, 0, 0, 1), (AY, 1, 2, 2), (SI, 3, 2, 5), (U, 1, 0, 0),
-    (G, 3, 2, 4), (AO, 1, 2, 2), (SI, 3, 2, 4), (AY, 1, 1, 2), (G, 0, 0, 3), (AO, 1, 1, 2),
-    (AI, 1, 3, 2), (AY, 1, 0, 2), (AI, 1, 2, 2), (AO, 1, 3, 2), (SY, 0, 0, 2), (G, 3, 2, 3),
-    (AI, 1, 0, 2), (AO, 1, 0, 2), (G, 3, 1, 5), (SY, 3, 2, 2), (AI, 1, 1, 2), (AO, 2, 0, 5),
-    (AY, 1, 3, 4), (G, 3, 3, 5), (SI, 3, 3, 5), (AO, 1, 3, 4), (G, 3, 0, 5), (AY, 1, 2, 4),
-    (SI, 3, 0, 5), (AO, 1, 2, 4), (G, 3, 0, 4), (N, 0, 0, 0), (X, 0, 0, 0), (AY, 1, 0, 4),
-    (SI, 3, 1, 5), (N, 3, 2, 0), (AO, 1, 0, 4), (X, 3, 2, 0), (SI, 3, 0, 4), (AY, 1, 1, 4),
-    (G, 0, 1, 6), (AO, 1, 1, 4), (SI, 0, 1, 6), (U, 0, 0, 0), (AY, 0, 0, 2), (AI, 0, 0, 2),
-    (G, 3, 0, 3), (AO, 0, 0, 2), (SY, 3, 0, 2), (G, 3, 3, 3), (U, 3, 2, 0), (G, 3, 1, 3),
-    (AI, 3, 2, 2), (AO, 3, 2, 2), (SY, 3, 1, 2), (AI, 1, 1, 0), (AY, 1, 1, 0), (G, 3, 1, 4),
-    (G, 0, 1, 0), (SO, 0, 1, 0), (SI, 3, 1, 4), (AY, 3, 2, 2), (AO, 0, 0, 4), (N, 3, 0, 0),
-    (X, 3, 0, 0), (AY, 1, 2, 0), (AI, 1, 2, 0), (AO, 3, 2, 4), (SY, 3, 3, 2), (AI, 1, 3, 0),
-    (AO, 1, 1, 6), (AY, 1, 3, 0), (G, 3, 3, 4), (SI, 3, 3, 4), (U, 3, 0, 0), (AO, 3, 0, 2),
-    (AY, 0, 0, 4), (AI, 3, 0, 2), (AO, 1, 2, 6), (V, 0, 0, 2), (AI, 3, 1, 0), (N, 3, 1, 0),
-    (X, 3, 1, 0), (AY, 3, 1, 0), (AO, 1, 3, 6), (AI, 2, 0, 0), (AY, 1, 3, 6), (N, 3, 3, 0),
-    (AY, 1, 2, 6), (X, 3, 3, 0), (AO, 3, 0, 4), (U, 3, 1, 0), (AO, 3, 1, 2), (AI, 3, 1, 2),
-    (AI, 1, 0, 0), (AY, 1, 1, 6), (AO, 3, 1, 6), (AI, 0, 2, 1), (AY, 3, 0, 2), (AO, 2, 0, 6),
-    (U, 3, 3, 0), (AI, 3, 3, 2), (AO, 3, 3, 2), (AY, 3, 2, 4), (AI, 2, 0, 1), (AO, 3, 1, 4),
-    (AY, 3, 3, 2), (AI, 0, 1, 0), (AO, 1, 0, 6), (AY, 3, 1, 2), (AO, 0, 2, 7), (AY, 3, 0, 4),
-    (AY, 1, 0, 0), (AO, 3, 3, 4), (AY, 1, 0, 6), (AI, 0, 1, 1), (AO, 2, 0, 7), (AY, 3, 3, 4),
-    (AO, 0, 1, 6), (AY, 3, 1, 4), (AY, 3, 1, 6), (AO, 0, 1, 7),
+    (E, 3, 0, 5), (SY, 3, 0, 4), (E, 3, 0, 7), (SY, 3, 0, 6), (E, 3, 0, 3), (E, 3, 0, 1),
+    (E, 2, 0, 5), (E, 2, 0, 3), (E, 3, 3, 7), (E, 2, 0, 1), (E, 2, 0, 7), (SY, 2, 0, 4),
+    (E, 3, 3, 5), (E, 3, 3, 3), (E, 3, 3, 1), (E, 1, 3, 7), (E, 1, 0, 5), (E, 1, 3, 5),
+    (E, 1, 3, 1), (SY, 3, 3, 6), (E, 1, 3, 3), (E, 0, 3, 1), (E, 1, 2, 3), (E, 1, 2, 7),
+    (E, 1, 2, 5), (E, 1, 2, 1), (E, 1, 1, 7), (E, 1, 1, 1), (E, 1, 1, 5), (SY, 2, 0, 2),
+    (G, 3, 2, 6), (SI, 3, 2, 6), (E, 1, 1, 3), (E, 1, 0, 3), (E, 0, 3, 5), (E, 1, 0, 1),
+    (E, 0, 3, 7), (SY, 2, 0, 0), (G, 3, 2, 7), (SI, 3, 2, 7), (E, 0, 3, 3), (E, 1, 0, 7),
+    (G, 3, 1, 7), (SI, 3, 1, 7), (SY, 2, 0, 6), (G, 0, 0, 7), (SI, 0, 0, 7), (SY, 3, 0, 2),
+    (G, 3, 2, 0), (SO, 3, 2, 0), (G, 0, 1, 7), (SI, 0, 1, 7), (G, 3, 2, 1), (SY, 3, 3, 4),
+    (SO, 3, 2, 1), (G, 3, 1, 6), (SI, 3, 1, 6), (G, 3, 1, 1), (SY, 3, 3, 2), (SO, 3, 1, 1),
+    (G, 3, 0, 4), (SI, 3, 0, 4), (SY, 3, 3, 0), (G, 0, 0, 1), (SO, 0, 0, 1), (SY, 1, 2, 2),
+    (G, 0, 2, 7), (SI, 0, 2, 7), (G, 0, 1, 1), (SY, 1, 0, 4), (SO, 0, 1, 1), (G, 0, 1, 6),
+    (SI, 0, 1, 6), (G, 3, 1, 0), (SO, 3, 1, 0), (SY, 1, 1, 6), (G, 2, 0, 4), (SI, 2, 0, 4),
+    (SY, 1, 3, 6), (N, 3, 0, 0), (V, 0, 0, 0), (X, 3, 0, 0), (G, 0, 2, 1), (SO, 0, 2, 1),
+    (SY, 1, 3, 4), (G, 0, 0, 6), (SI, 0, 0, 6), (G, 0, 1, 0), (SO, 0, 1, 0), (SY, 1, 2, 6),
+    (G, 2, 0, 6), (SI, 2, 0, 6), (G, 3, 3, 6), (SI, 3, 3, 6), (U, 3, 0, 0), (SY, 1, 1, 0),
+    (AO, 3, 0, 2), (AI, 3, 0, 2), (N, 2, 0, 0), (X, 2, 0, 0), (SY, 1, 2, 4), (G, 0, 0, 0),
+    (SO, 0, 0, 0), (G, 3, 3, 4), (SI, 3, 3, 4), (SY, 1, 1, 4), (G, 2, 0, 0), (SO, 2, 0, 0),
+    (G, 1, 0, 4), (SI, 1, 0, 4), (G, 3, 3, 0), (SY, 1, 2, 0), (SO, 3, 3, 0), (U, 2, 0, 0),
+    (AI, 2, 0, 2), (AO, 3, 0, 4), (AY, 2, 0, 2), (AO, 2, 0, 2), (G, 1, 2, 6), (SI, 1, 2, 6),
+    (N, 3, 3, 0), (X, 3, 3, 0), (SY, 1, 1, 2), (G, 1, 1, 6), (SI, 1, 1, 6), (AY, 3, 0, 2),
+    (G, 1, 3, 6), (SI, 1, 3, 6), (AO, 2, 0, 4), (SY, 1, 3, 0), (AI, 3, 1, 0), (U, 3, 3, 0),
+    (AO, 3, 3, 2), (SY, 1, 3, 2), (G, 1, 2, 0), (AO, 2, 0, 3), (AI, 3, 3, 2), (G, 1, 3, 4),
+    (AI, 2, 0, 3), (SO, 1, 2, 0), (AY, 3, 3, 2), (G, 1, 1, 0), (G, 1, 1, 4), (SI, 1, 3, 4),
+    (SO, 1, 1, 0), (SY, 0, 3, 0), (G, 1, 2, 4), (SI, 1, 2, 4), (SY, 1, 0, 2), (AO, 3, 0, 3),
+    (G, 1, 3, 0), (G, 0, 2, 5), (SI, 1, 1, 4), (SY, 3, 0, 0), (SO, 1, 3, 0), (AI, 3, 0, 3),
+    (AO, 3, 3, 4), (AY, 3, 1, 0), (G, 3, 0, 6), (AY, 3, 1, 6), (N, 1, 3, 0), (AO, 2, 0, 5),
+    (AI, 3, 3, 3), (SY, 0, 3, 4), (SI, 3, 0, 6), (AO, 3, 1, 6), (SY, 1, 0, 0), (N, 1, 0, 0),
+    (SI, 0, 2, 5), (AO, 3, 3, 3), (N, 1, 1, 0), (SY, 0, 3, 6), (N, 1, 2, 0), (X, 1, 0, 0),
+    (AO, 3, 0, 5), (G, 3, 1, 4), (SI, 3, 1, 4), (SY, 0, 3, 2), (AO, 3, 3, 5), (G, 3, 1, 5),
+    (SI, 3, 1, 5), (G, 3, 0, 0), (SO, 3, 0, 0), (SY, 1, 0, 6), (AI, 3, 2, 0), (U, 1, 0, 0),
+    (AO, 1, 0, 2), (AI, 1, 0, 2), (AY, 3, 2, 0), (U, 1, 3, 0), (AO, 1, 3, 2), (AI, 1, 3, 2),
+    (U, 1, 2, 0), (G, 0, 2, 4), (U, 1, 1, 0), (AY, 1, 0, 2), (AO, 1, 2, 2), (SI, 0, 2, 4),
+    (G, 0, 1, 5), (AY, 1, 3, 2), (AO, 1, 1, 2), (AI, 1, 1, 2), (G, 0, 2, 3), (SY, 0, 2, 2),
+    (AO, 3, 2, 6), (AI, 1, 2, 2), (AY, 1, 1, 2), (AO, 1, 0, 4), (SI, 0, 1, 5), (AY, 3, 2, 6),
+    (AO, 1, 3, 4), (AI, 0, 1, 0), (G, 1, 0, 6), (AY, 0, 1, 0), (AO, 1, 1, 4), (SI, 1, 0, 6),
+    (AY, 1, 0, 4), (N, 0, 2, 0), (X, 0, 2, 0), (G, 3, 1, 3), (AO, 1, 2, 4), (SY, 3, 1, 2),
+    (AI, 1, 1, 3), (AO, 1, 1, 3), (V, 0, 0, 1), (G, 0, 1, 3), (AY, 1, 2, 2), (G, 0, 1, 4),
+    (SI, 0, 1, 4), (AO, 0, 1, 6), (SY, 0, 1, 2), (U, 0, 2, 0), (AI, 0, 2, 2), (G, 0, 0, 5),
+    (AO, 0, 2, 2), (G, 1, 0, 0), (AY, 1, 3, 4), (SI, 0, 0, 5), (SO, 1, 0, 0), (AI, 3, 3, 1),
+    (N, 3, 1, 0), (AY, 0, 1, 6), (X, 3, 1, 0), (AO, 1, 1, 5), (AY, 0, 2, 2), (G, 0, 3, 4),
+    (SI, 0, 3, 4), (AO, 0, 2, 4), (N, 0, 1, 0), (X, 0, 1, 0), (AY, 1, 2, 4), (G, 0, 2, 6),
+    (SI, 0, 2, 6), (U, 3, 1, 0), (AO, 3, 1, 2), (AI, 3, 1, 2), (AY, 0, 2, 4), (G, 0, 3, 6),
+    (AO, 3, 3, 7), (SI, 0, 3, 6), (AY, 3, 1, 2), (G, 0, 0, 4), (SI, 0, 0, 4), (U, 0, 1, 0),
+    (AO, 0, 1, 2), (AY, 0, 1, 2), (N, 0, 3, 0), (X, 0, 3, 0), (AI, 0, 1, 2), (G, 0, 2, 0),
+    (SO, 0, 2, 0), (AY, 0, 0, 0), (AO, 3, 1, 4), (AI, 0, 0, 0), (AY, 3, 1, 4), (G, 0, 0, 3),
+    (G, 0, 3, 0), (SO, 0, 3, 0), (SY, 0, 0, 2), (AI, 3, 3, 0), (U, 0, 3, 0), (AO, 0, 3, 2),
+    (AI, 0, 3, 2), (AY, 0, 3, 2), (AI, 2, 0, 1), (AO, 0, 1, 4), (AY, 0, 1, 4), (AO, 0, 0, 6),
+    (AY, 0, 0, 6), (G, 3, 2, 5), (SI, 3, 2, 5), (AO, 3, 3, 6), (N, 0, 0, 0), (X, 0, 0, 0),
+    (AI, 3, 0, 0), (AY, 0, 3, 4), (AO, 0, 3, 4), (AI, 1, 0, 0), (AY, 1, 0, 0), (AO, 2, 0, 7),
+    (G, 3, 2, 4), (SI, 3, 2, 4), (G, 3, 2, 3), (V, 0, 0, 2), (SY, 3, 2, 2), (U, 0, 0, 0),
+    (AI, 0, 0, 2), (AO, 0, 0, 2), (AY, 0, 0, 2), (AO, 3, 0, 6), (AI, 1, 3, 0), (AY, 1, 3, 0),
+    (AO, 1, 0, 6), (AI, 0, 2, 0), (AY, 1, 0, 6), (N, 3, 2, 0), (X, 3, 2, 0), (AY, 0, 2, 0),
+    (AO, 0, 0, 4), (AI, 1, 2, 0), (AY, 0, 0, 4), (AO, 1, 3, 6), (AI, 0, 3, 0), (AY, 0, 3, 0),
+    (AO, 0, 2, 6), (AI, 3, 0, 1), (U, 3, 2, 0), (AO, 3, 2, 2), (AI, 3, 2, 2), (AY, 1, 2, 0),
+    (AI, 2, 0, 0), (AO, 1, 2, 6), (AY, 1, 3, 6), (AI, 1, 1, 0), (AO, 0, 3, 6), (AY, 3, 2, 2),
+    (AI, 1, 1, 1), (AO, 3, 0, 7), (AY, 0, 3, 6), (AO, 3, 2, 4), (AY, 0, 2, 6), (AO, 2, 0, 6),
+    (AY, 3, 2, 4), (AO, 1, 1, 6), (AY, 1, 2, 6), (AO, 1, 1, 7),
 )
 
 

time: 118 us -> 117 us (level)
  no operation moved by 1% of the time
where the time goes in v4:
time: 117 us
  Pallas kernels  116 us (99%)
    pallas_call x1, Pallas kernels, fused(): pl.pallas_call(functools.partial(kernel, replicas, models, 4.0, shapes),...  112 us
    pallas_call x1, Pallas kernels, fused(): pl.pallas_call(functools.partial(finish, shapes), out_shape=outs, in_spec...  3.78 us

profile of v4, /device:TPU:0, one launch (start us, length us, event | category | flops | bytes accessed | tf_op | source)
XLA Modules:
  0.0 116.9 jit_solution(9081486449061363634)
XLA Ops:
  0.7 112.3 %shard_map.415 = (bf16[8,128,1024]{2,1,0:T(8,128)(2,1)S(1)}, bf16[8,1024,128]{2,1,0:T(8,128)(2,1)S(1)}, bf16[8,256,128]{2,1,0:T(8,128)(2,1)S(1)}, bf16[8,128,768...) custom-call(f32[8,128,1024]{2,1,0:T(8,128)} %bitcast.20, ...), custom_call_target="tpu_custom_call" | custom-call | tf_op jit(solution)/shard_map/pallas_call | solution.py:628
  113.0 3.8 %shard_map.416 = (bf16[8,128,1024]{2,1,0:T(8,128)(2,1)}, bf16[1024,1024]{1,0:T(8,128)(2,1)}, bf16[8,128,256]{2,1,0:T(8,128)(2,1)}, bf16[8,128,256]{2,1,0:T(8,128...) custom-call(bf16[8,128,1024]{2,1,0:T(8,128)(2,1)S(1)} %get-tuple-ele, ...), custom_call_target="tpu_custom_call" | custom-call | tf_op jit(solution)/shard_map/pallas_call | solution.py:645

commit v5 on v4

--- a/solution.py
+++ b/solution.py
@@ -175,9 +175,8 @@
 
 
 def kernel(replicas, models, limit, shapes, *refs):
-    slopes, slope_norm, slope_bias = refs[0:6], refs[6], refs[7]
-    params, param_norm, param_bias = refs[8:14], refs[14], refs[15]
-    states, state_norm, state_bias = refs[16:22], refs[22], refs[23]
+    slopes, params, states = refs[0:6], refs[8:14], refs[16:22]
+    vectors = [refs[i] for i in (6, 7, 14, 15, 22, 23)]
     groups = range(len(GROUPS))
     n = len(GROUPS)
     full, own, st = refs[24 : 24 + n], refs[24 + n : 24 + 2 * n], refs[24 + 2 * n : 24 + 3 * n]
@@ -187,7 +186,8 @@
     xin, enc, rec, sq, sqr = (take() for _ in range(5))
     vs, vown, vrec, vnext, vag, vh_norm, vh_bias = (scratch.pop(0) for _ in range(7))
     rs_s, rs_r, ag_s, ag_r, n_s, n_r, v_s, v_r, w_s, w_r = (scratch.pop(0) for _ in range(10))
-    load_sem, own_sem, st_sem, vown_sem = scratch
+    load_sem, own_sem, st_sem, vown_sem, vec_sem = scratch[0:5]
+    slope_norm, slope_bias, param_norm, param_bias, state_norm, state_bias = small = scratch[5:]
 
     r = lax.axis_index("replica")
     m = lax.axis_index("model")
@@ -266,11 +266,11 @@
             for i, a in enumerate(GROUPS[g].members):
                 pltpu.make_async_copy(params[a], lanes(g, own[g], i), own_sem.at[g]).start()
                 pltpu.make_async_copy(states[a], lanes(g, st[g], i), st_sem.at[g]).start()
+        for i, ref in enumerate(vectors):
+            pltpu.make_async_copy(ref, small[i], vec_sem.at[i]).start()
 
     for g, c in CHUNKS[:2]:
         load(g, c)
-    vs[0:1, :] = slope_norm[...]
-    vs[1:2, :] = slope_bias[...]
     for g in groups:
         if not GROUPS[g].rows:
             sq[g][...] = jnp.zeros_like(sq[g])
@@ -298,6 +298,10 @@
         return remote(vnext, vag.at[j - 1], w_s.at[j - 1], w_r.at[j - 1], lax.rem(r + j, replicas))
 
     def vec_start():
+        for i, ref in enumerate(vectors):
+            pltpu.make_async_copy(ref, small[i], vec_sem.at[i]).wait()
+        vs[0:1, :] = slope_norm[...]
+        vs[1:2, :] = slope_bias[...]
         pltpu.make_async_copy(vs.at[:, pl.ds(pl.multiple_of(r * width, width), width)], vown, vown_sem).start()
         for j in range(1, replicas):
             vec_out(j).start()
@@ -603,7 +607,7 @@
     held = [((replicas, *s), bf16) for s in shapes] + [(s, f32) for s in shapes] * 2
     held += [((replicas, width), bf16)] * 2 + [((1, width), f32)] * 4
     ANY, VM = pl.BlockSpec(memory_space=pl.ANY), pl.BlockSpec(memory_space=pltpu.VMEM)
-    part = [ANY] * 6 + [VM] * 2
+    part = [ANY] * 8
     scratch = [
         pltpu.VMEM((replicas, *s) if g.rows else (s[0], s[1] * replicas), f32) for g, s in zip(GROUPS, shapes)
     ]
@@ -624,7 +628,8 @@
     dma = pltpu.SemaphoreType.DMA
     scratch += [dma((n,)), dma((chunks, 11)), dma((chunks, 3)), dma((chunks, 8))]
     scratch += [dma((chunks, models - 1))] * 2 + [dma((replicas - 1,))] * 4
-    scratch += [dma((chunks,))] + [dma((n,))] * 2 + [dma(())]
+    scratch += [dma((chunks,))] + [dma((n,))] * 2 + [dma(()), dma((6,))]
+    scratch += [pltpu.VMEM((1, vec), f32)] * 2 + [pltpu.VMEM((1, width), f32)] * 4
     out = pl.pallas_call(
         functools.partial(kernel, replicas, models, 4.0, shapes),
         out_shape=[pltpu.VMEM(*h) for h in held],

time: 117 us -> 116 us (level)
  no operation moved by 1% of the time
where the time goes in v5:
time: 116 us
  Pallas kernels  115 us (99%)
    pallas_call x1, Pallas kernels, fused(): pl.pallas_call(functools.partial(kernel, replicas, models, 4.0, shapes),...  112 us
    pallas_call x1, Pallas kernels, fused(): pl.pallas_call(functools.partial(finish, shapes), out_shape=outs, in_spec...  3.78 us

profile of v5, /device:TPU:0, one launch (start us, length us, event | category | flops | bytes accessed | tf_op | source)
XLA Modules:
  0.0 116.3 jit_solution(18166808057130982206)
XLA Ops:
  0.7 111.7 %shard_map.415 = (bf16[8,128,1024]{2,1,0:T(8,128)(2,1)S(1)}, bf16[8,1024,128]{2,1,0:T(8,128)(2,1)S(1)}, bf16[8,256,128]{2,1,0:T(8,128)(2,1)S(1)}, bf16[8,128,768...) custom-call(f32[8,128,1024]{2,1,0:T(8,128)} %bitcast.20, ...), custom_call_target="tpu_custom_call" | custom-call | tf_op jit(solution)/shard_map/pallas_call | solution.py:633
  112.3 3.8 %shard_map.416 = (bf16[8,128,1024]{2,1,0:T(8,128)(2,1)}, bf16[1024,1024]{1,0:T(8,128)(2,1)}, bf16[8,128,256]{2,1,0:T(8,128)(2,1)}, bf16[8,128,256]{2,1,0:T(8,128...) custom-call(bf16[8,128,1024]{2,1,0:T(8,128)(2,1)S(1)} %get-tuple-ele, ...), custom_call_target="tpu_custom_call" | custom-call | tf_op jit(solution)/shard_map/pallas_call | solution.py:650
